TPU v7x, 128 devices: a whole 4x4x4 slice. The times are simulated.
128 devices in a mesh: row: 8 (over x, core), col: 16 (over z, y).
Axes of the slice: x: 4, y: 4, z: 4, core: 2. Of those that a mesh axis runs over, the one named last changes fastest.
Arguments:
- tokens: bfloat16 [1024, 7168], P(('row', 'col')), may hold values from -6 to 6
- router_logits: float32 [1024, 16], P(('row', 'col')), may hold values from -18 to 318
- expert_ids: int32 [1024, 8], P(('row', 'col')), may hold values from 0 to 15, all different within a row; in each aligned block of 8 rows (0 to 7, 8 to 15, ...) at most 8 rows name the same one
- w_gate: bfloat16 [16, 7168, 2048], P('row', None, 'col'), may hold values from -0.3307189 to 0.3307189
- w_up: bfloat16 [16, 7168, 2048], P('row', None, 'col'), may hold values from -0.3307189 to 0.3307189
- w_down: bfloat16 [16, 2048, 7168], P('row', 'col'), may hold values from -0.61871843 to 0.61871843
Outputs:
- merged: bfloat16 [1024, 7168], P(('row', 'col'))
Inputs may be any that keep to these rules, and one draw needn't show every extreme that they name: `expert_ids`: each row names 8 different experts. Among the 8 tokens of one device no expert is named more than 8 times, and in every draw some device names some expert exactly 8 times.
All inputs are finite; a program needn't handle non-finite values.
Results may differ from a plain program's by a relative error of at most 0.015.
Values may be sent and summed in bfloat16 or wider, within the bound.
No kernel may reach another device: no remote copies, remote signals or barrier semaphores. Data moves between devices by JAX's collectives and lax.ppermute only.
A program may use at most 128 MiB of HBM per device.

v0:
```python
import functools

import jax
import jax.numpy as jnp
from jax import lax
from jax.experimental import pallas as pl
from jax.experimental.pallas import tpu as pltpu
from jax.sharding import PartitionSpec as P


AXES = ("row", "col")
ORDER = (("x", "y", "z"), ("y", "z", "x"))
HBM = pl.BlockSpec(memory_space=pltpu.HBM)
VMEM = pl.BlockSpec(memory_space=pltpu.VMEM)


def place(row, col):
    return {"x": row // 2, "core": row % 2, "z": col // 4, "y": col % 4}


def index(at):
    return (at["x"] * 2 + at["core"]) * 16 + at["z"] * 4 + at["y"]


def pairs(phase, shift):
    moves = []
    for row in range(8):
        for col in range(16):
            at = place(row, col)
            to = dict(at)
            axis = ORDER[at["core"]][phase]
            to[axis] = (to[axis] + shift) % 4
            moves.append((index(at), index(to)))
    return moves


def send(value, phase, shift):
    return lax.ppermute(value, AXES, pairs(phase, shift))


def swap(value):
    return lax.ppermute(value, AXES, [(i, i ^ 16) for i in range(128)])


def route_kernel(tokens, routing, block):
    width = tokens.shape[1]
    logits = routing[:, :16]
    names = lax.broadcasted_iota(jnp.int32, logits.shape, 1).astype(jnp.float32)
    chosen = routing[:, 16:17] == names
    for k in range(17, routing.shape[1]):
        chosen = chosen | (routing[:, k : k + 1] == names)
    scores = jnp.where(chosen, logits, -jnp.inf)
    scores = jnp.exp(scores - jnp.max(scores, axis=1, keepdims=True))
    probs = scores / jnp.sum(scores, axis=1, keepdims=True)
    block[:, :width] = tokens[...]
    block[:, width:] = jnp.zeros((block.shape[0], 128), block.dtype)
    block[:, width : width + 16] = probs.astype(block.dtype)


def join_kernel(places, *refs):
    out = refs[-1]
    for (row, col), ref in zip(places, refs[:-1]):
        out[row : row + ref.shape[0], col : col + ref.shape[1]] = ref[...]


def join(rows, cols, *pieces):
    arrays = [piece for piece, _, _ in pieces]
    places = tuple((row, col) for _, row, col in pieces)
    return pl.pallas_call(
        functools.partial(join_kernel, places),
        out_shape=jax.ShapeDtypeStruct((rows, cols), arrays[0].dtype),
        in_specs=[VMEM] * len(arrays),
        out_specs=VMEM,
        compiler_params=pltpu.CompilerParams(vmem_limit_bytes=6 << 20),
        name="join",
    )(*arrays)


def pack_kernel(gate, up, packed, sems):
    per_group, _, units = gate.shape
    copies = []
    for j, weight in enumerate((gate, up)):
        for e in range(per_group):
            k = j * per_group + e
            to = packed.at[:, pl.ds(k * units, units)]
            copies.append(pltpu.make_async_copy(weight.at[e], to, sems.at[k]))
    for copy in copies:
        copy.start()
    for copy in copies:
        copy.wait()


def expert_kernel(piece_a, piece_b, spread, in_own, in_other, down_own, down_other, out_a, out_b, rows):
    half, width = out_a.shape
    rows[:half, :] = piece_a[...]
    rows[half:, :] = piece_b[...]
    weight = jnp.dot(rows[:, width:], spread[...], preferred_element_type=jnp.float32)
    hidden = []
    for k, w_in in enumerate((in_own, in_other)):
        both = jnp.dot(rows[:, :width], w_in[...], preferred_element_type=jnp.float32)
        units = both.shape[1] // 2
        gate = both[:, :units]
        value = gate / (1.0 + jnp.exp(-gate)) * both[:, units:] * weight[:, k * units : (k + 1) * units]
        hidden.append(value.astype(rows.dtype))
    step = width // 7
    for j in range(7):
        cols = slice(j * step, (j + 1) * step)
        part = jnp.dot(hidden[0], down_own[:, cols], preferred_element_type=jnp.float32)
        part = part + jnp.dot(hidden[1], down_other[:, cols], preferred_element_type=jnp.float32)
        part = part.astype(out_a.dtype)
        out_a[:, cols] = part[:half]
        out_b[:, cols] = part[half:]


def experts_of(piece_a, piece_b, weights):
    half, packed = piece_a.shape
    width = packed - 128
    kind = piece_a.dtype
    shape = jax.ShapeDtypeStruct((half, width), kind)
    return pl.pallas_call(
        expert_kernel,
        out_shape=(shape, shape),
        in_specs=[VMEM] * 7,
        out_specs=(VMEM,) * 2,
        scratch_shapes=[pltpu.VMEM((2 * half, packed), kind)],
        compiler_params=pltpu.CompilerParams(vmem_limit_bytes=12 << 20),
        cost_estimate=pl.CostEstimate(
            flops=4 * half * width * 1536, bytes_accessed=half * width * 8, transcendentals=half * 1024
        ),
        name="experts",
    )(piece_a, piece_b, *weights)


def pack(gate, up):
    per_group, width, units = gate.shape
    return pl.pallas_call(
        pack_kernel,
        out_shape=jax.ShapeDtypeStruct((width, 2 * per_group * units), gate.dtype),
        in_specs=[HBM] * 2,
        out_specs=VMEM,
        scratch_shapes=[pltpu.SemaphoreType.DMA((2 * per_group,))],
        compiler_params=pltpu.CompilerParams(vmem_limit_bytes=2 << 20),
        name="pack",
    )(gate, up)


def add_kernel(starts, *refs):
    out = refs[-1]
    total = None
    for start, ref in zip(starts, refs[:-1]):
        piece = ref[start : start + out.shape[0], :].astype(jnp.float32)
        total = piece if total is None else total + piece
    out[...] = total.astype(out.dtype)


def add(rows, *pieces):
    arrays = [piece for piece, _ in pieces]
    starts = tuple(start for _, start in pieces)
    return pl.pallas_call(
        functools.partial(add_kernel, starts),
        out_shape=jax.ShapeDtypeStruct((rows, arrays[0].shape[1]), arrays[0].dtype),
        in_specs=[VMEM] * len(arrays),
        out_specs=VMEM,
        compiler_params=pltpu.CompilerParams(vmem_limit_bytes=6 << 20),
        name="add",
    )(*arrays)


def local(tokens, router_logits, expert_ids, w_gate, w_up, w_down):
    per_group, _, units = w_gate.shape
    count, width = tokens.shape
    packed = width + 128
    near = (1, 3, 2)
    routing = jnp.concatenate([router_logits, expert_ids.astype(jnp.float32)], axis=1)
    block = pl.pallas_call(
        route_kernel,
        out_shape=jax.ShapeDtypeStruct((count, packed), tokens.dtype),
        in_specs=[VMEM] * 2,
        out_specs=VMEM,
        compiler_params=pltpu.CompilerParams(vmem_limit_bytes=2 << 20),
        name="route",
    )(tokens, routing)
    got = [send(block, 0, -k) for k in near]
    gate_other, up_other, down_other = swap(w_gate), swap(w_up), swap(w_down)
    block = join(4 * count, packed, *((piece, k * count, 0) for k, piece in enumerate([block, *got])))
    row = lax.axis_index("row")
    spot = jnp.arange(2 * per_group * units)
    names = jnp.where(spot < per_group * units, row, row ^ 1) * per_group + spot // units % per_group
    spread = (jnp.arange(128)[:, None] == names[None, :]).astype(jnp.bfloat16)

    got = [send(block, 1, -k) for k in near]
    weights = (
        spread, pack(w_gate, w_up), pack(gate_other, up_other), w_down.reshape(-1, width), down_other.reshape(-1, width)
    )
    a0 = join(8 * count, packed, (block, 0, 0), (got[0], 4 * count, 0))
    b0 = join(8 * count, packed, (got[1], 0, 0), (got[2], 4 * count, 0))
    am, bp = send(a0, 2, 1), send(b0, 2, -1)
    oa, ob = send(am, 2, 1), send(bp, 2, -1)
    bm, ap = send(b0, 2, 1), send(a0, 2, -1)

    half = 8 * count
    sa0, sb0 = experts_of(a0, b0, weights)
    sam, sbp = experts_of(am, bp, weights)
    soa, sob = experts_of(oa, ob, weights)
    sap, sbm = experts_of(ap, bm, weights)

    over_a = send(soa, 2, 1)
    over_b = send(sob, 2, -1)
    direct_b = send(sbp, 2, 1)
    direct_a = send(sam, 2, -1)
    relay_a = send(add(half, (sap, 0), (over_a, 0)), 2, 1)
    relay_b = send(add(half, (sbm, 0), (over_b, 0)), 2, -1)

    def group(at, *pieces):
        return add(4 * count, *((piece, at) for piece in pieces))

    got = [send(group(4 * count, sa0, direct_a, relay_a), 1, 1)]
    got.append(send(group(0, sb0, direct_b, relay_b), 1, 3))
    got.append(send(group(4 * count, sb0, direct_b, relay_b), 1, 2))
    pieces = (group(0, sa0, direct_a, relay_a), *got)
    sums = [add(count, *((piece, k * count) for piece in pieces)) for k in range(4)]
    got = [send(sums[j], 0, k) for j, k in ((1, 1), (2, 3), (3, 2))]
    return add(count, *((piece, 0) for piece in (sums[0], *got)))


def solution(mesh):
    in_specs = (
        P(("row", "col"), None),
        P(("row", "col"), None),
        P(("row", "col"), None),
        P("row", None, "col"),
        P("row", None, "col"),
        P("row", "col", None),
    )
    out_specs = P(("row", "col"), None)
    return jax.shard_map(local, mesh=mesh, in_specs=in_specs, out_specs=out_specs, check_vma=False)
```

profile of v0, /device:TPU:24, one launch (start us, length us, event | category | flops | bytes accessed | tf_op | source)
XLA Modules:
  0.0 148.6 jit_solution(7189463327539490727)
XLA Ops:
  0.0 0.5 collective-permute-start.7
  0.5 0.7 convert_element_type.6
  1.2 0.8 pad_maximum_fusion.routing
  2.0 0.9 copy-done.3
  2.9 0.2 route.1.refs_0_
  3.1 2.8 %collective-permute-start = (bf16[8,7296]{1,0:T(8,128)(2,1)S(1)}, bf16[8,7296]{1,0:T(8,128)(2,1)S(1)}, u32[]{:S(2)}, u32[]{:S(2)}) collective-permute-start(bf16[8,7296]{1,0:T(8,128)(2,1)S(1)} %route.1.refs_0_), channel_id=1, source_target_pairs={{0,96},{1,97},{2,98},{3,99},{4,100},{5,101},{6,102},{7,103},{8,104... | collective-permute-start | bytes 350216 | tf_op jit(solution)/shard_map/ppermute | solution.py:38
  5.9 2.4 %collective-permute-done.refs_1_ = bf16[8,7296]{1,0:T(8,128)(2,1)S(1)} collective-permute-done((bf16[8,7296]{1,0:T(8,128)(2,1)S(1)}, bf16[8,7296]{1,0:T(8,128)(2,1)S(1)}, u32[]{:S(2)}, u32[]{:S(2)}) %collective-permute-start) | collective-permute-done | bytes 116768 | tf_op jit(solution)/shard_map/ppermute | solution.py:38
  8.3 2.7 %collective-permute-start.2 = (bf16[8,7296]{1,0:T(8,128)(2,1)S(1)}, bf16[8,7296]{1,0:T(8,128)(2,1)S(1)}, u32[]{:S(2)}, u32[]{:S(2)}) collective-permute-start(bf16[8,7296]{1,0:T(8,128)(2,1)S(1)} %route.1.refs_0_), channel_id=1, source_target_pairs={{0,64},{1,65},{2,66},{3,67},{4,68},{5,69},{6,70},{7,71},{8,72},{9,... | collective-permute-start | bytes 350216 | tf_op jit(solution)/shard_map/ppermute | solution.py:38
  11.0 0.9 collective-permute-done.1.refs_2_
  11.9 2.7 %collective-permute-done.2.refs_3_ = bf16[8,7296]{1,0:T(8,128)(2,1)S(1)} collective-permute-done((bf16[8,7296]{1,0:T(8,128)(2,1)S(1)}, bf16[8,7296]{1,0:T(8,128)(2,1)S(1)}, u32[]{:S(2)}, u32[]{:S(2)}) %collective-permute-start.2) | collective-permute-done | bytes 116768 | tf_op jit(solution)/shard_map/ppermute | solution.py:38
  14.6 0.8 collective-permute-start.3
  15.4 2.5 %collective-permute-start.4 = (bf16[32,7296]{1,0:T(8,128)(2,1)S(1)}, bf16[32,7296]{1,0:T(8,128)(2,1)S(1)}, u32[]{:S(2)}, u32[]{:S(2)}) collective-permute-start(bf16[32,7296]{1,0:T(8,128)(2,1)S(1)} %join.3.refs_0_), channel_id=1, source_target_pairs={{0,1},{1,2},{2,3},{3,0},{4,5},{5,6},{6,7},{7,4},{8,9},{9,10},{10,1... | collective-permute-start | bytes 1400840 | tf_op jit(solution)/shard_map/ppermute | solution.py:38
  17.9 6.5 %collective-permute-done.3.refs_1_ = bf16[32,7296]{1,0:T(8,128)(2,1)S(1)} collective-permute-done((bf16[32,7296]{1,0:T(8,128)(2,1)S(1)}, bf16[32,7296]{1,0:T(8,128)(2,1)S(1)}, u32[]{:S(2)}, u32[]{:S(2)}) %collective-permute-start.3) | collective-permute-done | bytes 466976 | tf_op jit(solution)/shard_map/ppermute | solution.py:38
  24.5 0.0 collective-permute-start.5
  24.5 0.1 join.4.piece_a
  24.6 2.0 %collective-permute-start.9 = (bf16[64,7296]{1,0:T(8,128)(2,1)S(1)}, bf16[64,7296]{1,0:T(8,128)(2,1)S(1)}, u32[]{:S(2)}, u32[]{:S(2)}) collective-permute-start(bf16[64,7296]{1,0:T(8,128)(2,1)S(1)} %join.4.piece_a), channel_id=1, source_target_pairs={{0,4},{1,5},{2,6},{3,7},{4,8},{5,9},{6,10},{7,11},{8,12},{9,13},{1... | collective-permute-start | bytes 2801672 | tf_op jit(solution)/shard_map/ppermute | solution.py:38
  26.5 8.0 %collective-permute-done.5.refs_1_ = bf16[32,7296]{1,0:T(8,128)(2,1)S(1)} collective-permute-done((bf16[32,7296]{1,0:T(8,128)(2,1)S(1)}, bf16[32,7296]{1,0:T(8,128)(2,1)S(1)}, u32[]{:S(2)}, u32[]{:S(2)}) %collective-permute-start.5) | collective-permute-done | bytes 466976 | tf_op jit(solution)/shard_map/ppermute | solution.py:38
  34.5 0.1 join.5.piece_b
  34.6 4.1 %collective-permute-start.10 = (bf16[64,7296]{1,0:T(8,128)(2,1)S(1)}, bf16[64,7296]{1,0:T(8,128)(2,1)}, u32[]{:S(2)}, u32[]{:S(2)}) collective-permute-start(bf16[64,7296]{1,0:T(8,128)(2,1)S(1)} %join.5.piece_b), channel_id=1, source_target_pairs={{0,12},{1,13},{2,14},{3,15},{4,0},{5,1},{6,2},{7,3},{8,4},{9,5},{1... | collective-permute-start | bytes 2801672 | tf_op jit(solution)/shard_map/ppermute | solution.py:38
  38.7 3.7 %collective-permute-done.9.piece_a = bf16[64,7296]{1,0:T(8,128)(2,1)S(1)} collective-permute-done((bf16[64,7296]{1,0:T(8,128)(2,1)S(1)}, bf16[64,7296]{1,0:T(8,128)(2,1)S(1)}, u32[]{:S(2)}, u32[]{:S(2)}) %collective-permute-start.9) | collective-permute-done | bytes 933920 | tf_op jit(solution)/shard_map/ppermute | solution.py:38
  42.4 0.8 collective-permute-start.14
  43.3 6.5 %collective-permute-done.10.piece_b = bf16[64,7296]{1,0:T(8,128)(2,1)} collective-permute-done((bf16[64,7296]{1,0:T(8,128)(2,1)S(1)}, bf16[64,7296]{1,0:T(8,128)(2,1)}, u32[]{:S(2)}, u32[]{:S(2)}) %collective-permute-start.10) | collective-permute-done | bytes 933920 | tf_op jit(solution)/shard_map/ppermute | solution.py:38
  49.8 3.8 %collective-permute-start.15 = (bf16[64,7296]{1,0:T(8,128)(2,1)}, bf16[64,7296]{1,0:T(8,128)(2,1)}, u32[]{:S(2)}, u32[]{:S(2)}) collective-permute-start(bf16[64,7296]{1,0:T(8,128)(2,1)} %collective-permute-done.10.piece_b), channel_id=1, source_target_pairs={{0,12},{1,13},{2,14},{3,15},{4,0},{5,1},{6,2},{7,3},{8,4},{9,5},{1... | collective-permute-start | bytes 2801672 | tf_op jit(solution)/shard_map/ppermute | solution.py:38
  53.6 0.1 collective-permute-start.12
  53.7 2.0 %collective-permute-start.13 = (bf16[64,7296]{1,0:T(8,128)(2,1)S(1)}, bf16[64,7296]{1,0:T(8,128)(2,1)S(1)}, u32[]{:S(2)}, u32[]{:S(2)}) collective-permute-start(bf16[64,7296]{1,0:T(8,128)(2,1)S(1)} %join.5.piece_b), channel_id=1, source_target_pairs={{0,4},{1,5},{2,6},{3,7},{4,8},{5,9},{6,10},{7,11},{8,12},{9,13},{1... | collective-permute-start | bytes 2801672 | tf_op jit(solution)/shard_map/ppermute | solution.py:38
  55.7 2.0 %copy-done.1 = bf16[2,7168,128]{2,1,0:T(8,128)(2,1)S(1)} copy-done((bf16[2,7168,128]{2,1,0:T(8,128)(2,1)S(1)}, bf16[2,7168,128]{2,1,0:T(8,128)(2,1)}, u32[]{:S(2)}) %copy-start.1) | copy-done | bytes 3670040
  57.8 2.0 %copy-done.2 = bf16[2,7168,128]{2,1,0:T(8,128)(2,1)S(1)} copy-done((bf16[2,7168,128]{2,1,0:T(8,128)(2,1)S(1)}, bf16[2,7168,128]{2,1,0:T(8,128)(2,1)}, u32[]{:S(2)}) %copy-start.2) | copy-done | bytes 3670040
  59.8 1.3 pack.2.in_own
  61.1 3.3 %pack.3.in_other = bf16[7168,512]{1,0:T(8,128)(2,1)S(1)} custom-call(bf16[2,7168,128]{2,1,0:T(8,128)(2,1)} %collective-permute-done.6.gate, bf16[2,7168,128]{2,1,0:T(8,128)(2,1)} %collective-permute-done.7.up), custom_call_target="tpu_custom_call" | custom-call | tf_op jit(solution)/shard_map/pack/pallas_call | solution.py:136
  64.5 0.5 collective-permute-done.15.piece_b
  65.0 0.3 copy-done
  65.3 5.8 %experts.7 = (bf16[64,7168]{1,0:T(8,128)(2,1)S(1)}, bf16[64,7168]{1,0:T(8,128)(2,1)S(1)}) custom-call(bf16[64,7296]{1,0:T(8,128)(2,1)} %collective-permute-done.14.piece_a, bf16[64,7296]{1,0:T(8,128)(2,1)} %collective-permute-done.15.piece_b, bf16[128,512]{1,0:T(8,128)(2,1)S(1)} %fusion.spread, bf16[7168,512]{1,0:T(8,128)(2,1)S(1)} %pack.2.in_own, ...), custom_call_target="tpu_custom_call" | custom-call | flops 2818572288 | bytes 3670016 | tf_op jit(solution)/shard_map/experts/pallas_call | solution.py:120
  71.1 0.1 collective-permute-start.16
  71.2 3.6 %collective-permute-start.20 = (bf16[64,7168]{1,0:T(8,128)(2,1)S(1)}, bf16[64,7168]{1,0:T(8,128)(2,1)S(1)}, u32[]{:S(2)}, u32[]{:S(2)}) collective-permute-start(bf16[64,7168]{1,0:T(8,128)(2,1)S(1)} %get-tuple-element.20), channel_id=1, source_target_pairs={{0,12},{1,13},{2,14},{3,15},{4,0},{5,1},{6,2},{7,3},{8,4},{9,5},{1... | collective-permute-start | bytes 2752520 | tf_op jit(solution)/shard_map/ppermute | solution.py:38
  74.8 5.5 %experts.5 = (bf16[64,7168]{1,0:T(8,128)(2,1)S(1)}, bf16[64,7168]{1,0:T(8,128)(2,1)S(1)}) custom-call(bf16[64,7296]{1,0:T(8,128)(2,1)S(1)} %collective-permute-done.9.piece_a, bf16[64,7296]{1,0:T(8,128)(2,1)} %collective-permute-done.10.piece_b, bf16[128,512]{1,0:T(8,128)(2,1)S(1)} %fusion.spread, bf16[7168,512]{1,0:T(8,128)(2,1)S(1)} %pack.2.in_own, ...), custom_call_target="tpu_custom_call" | custom-call | flops 2818572288 | bytes 3670016 | tf_op jit(solution)/shard_map/experts/pallas_call | solution.py:120
  80.4 1.8 %collective-permute-start.11 = (bf16[64,7168]{1,0:T(8,128)(2,1)S(1)}, bf16[64,7168]{1,0:T(8,128)(2,1)S(1)}, u32[]{:S(2)}, u32[]{:S(2)}) collective-permute-start(bf16[64,7168]{1,0:T(8,128)(2,1)S(1)} %get-tuple-element.14), channel_id=1, source_target_pairs={{0,12},{1,13},{2,14},{3,15},{4,0},{5,1},{6,2},{7,3},{8,4},{9,5},{1... | collective-permute-start | bytes 2752520 | tf_op jit(solution)/shard_map/ppermute | solution.py:38
  82.2 5.2 %experts.6 = (bf16[64,7168]{1,0:T(8,128)(2,1)S(1)}, bf16[64,7168]{1,0:T(8,128)(2,1)S(1)}) custom-call(bf16[64,7296]{1,0:T(8,128)(2,1)S(1)} %collective-permute-done.12.piece_a, bf16[64,7296]{1,0:T(8,128)(2,1)S(1)} %collective-permute-done.13.piece_b, bf16[128,512]{1,0:T(8,128)(2,1)S(1)} %fusion.spread, bf16[7168,512]{1,0:T(8,128)(2,1)S(1)} %pack.2.in_own, ...), custom_call_target="tpu_custom_call" | custom-call | flops 2818572288 | bytes 3670016 | tf_op jit(solution)/shard_map/experts/pallas_call | solution.py:120
  87.5 0.2 add.39
  87.7 0.3 collective-permute-start.17
  88.0 0.1 collective-permute-start.19
  88.1 0.2 add.42
  88.3 3.2 %collective-permute-start.21 = (bf16[64,7168]{1,0:T(8,128)(2,1)S(1)}, bf16[64,7168]{1,0:T(8,128)(2,1)S(1)}, u32[]{:S(2)}, u32[]{:S(2)}) collective-permute-start(bf16[64,7168]{1,0:T(8,128)(2,1)S(1)} %add.42), channel_id=1, source_target_pairs={{0,12},{1,13},{2,14},{3,15},{4,0},{5,1},{6,2},{7,3},{8,4},{9,5},{1... | collective-permute-start | bytes 2752520 | tf_op jit(solution)/shard_map/ppermute | solution.py:38
  91.6 5.2 %experts.4 = (bf16[64,7168]{1,0:T(8,128)(2,1)S(1)}, bf16[64,7168]{1,0:T(8,128)(2,1)S(1)}) custom-call(bf16[64,7296]{1,0:T(8,128)(2,1)S(1)} %join.4.piece_a, bf16[64,7296]{1,0:T(8,128)(2,1)S(1)} %join.5.piece_b, bf16[128,512]{1,0:T(8,128)(2,1)S(1)} %fusion.spread, bf16[7168,512]{1,0:T(8,128)(2,1)S(1)} %pack.2.in_own, bf16[7168,512]{1,0:T(8,128)(2,1)S(1)} %pack.3.in_other, ...), custom_call_target="tpu_custom_call" | custom-call | flops 2818572288 | bytes 3670016 | tf_op jit(solution)/shard_map/experts/pallas_call | solution.py:120
  96.8 7.4 %collective-permute-done.17.refs_2_ = bf16[64,7168]{1,0:T(8,128)(2,1)S(1)} collective-permute-done((bf16[64,7168]{1,0:T(8,128)(2,1)S(1)}, bf16[64,7168]{1,0:T(8,128)(2,1)S(1)}, u32[]{:S(2)}, u32[]{:S(2)}) %collective-permute-start.17) | collective-permute-done | bytes 917536 | tf_op jit(solution)/shard_map/ppermute | solution.py:38
  104.2 0.2 add.41
  104.4 0.1 collective-permute-start.18
  104.5 17.5 %collective-permute-done.19.refs_1_ = bf16[64,7168]{1,0:T(8,128)(2,1)S(1)} collective-permute-done((bf16[64,7168]{1,0:T(8,128)(2,1)S(1)}, bf16[64,7168]{1,0:T(8,128)(2,1)S(1)}, u32[]{:S(2)}, u32[]{:S(2)}) %collective-permute-start.19) | collective-permute-done | bytes 917536 | tf_op jit(solution)/shard_map/ppermute | solution.py:38
  122.0 0.2 add.43
  122.2 0.1 collective-permute-start.22
  122.3 0.2 add.44
  122.5 1.1 collective-permute-start.23
  123.5 0.2 add.40.refs_0_
  123.7 14.2 %collective-permute-done.22.refs_2_ = bf16[32,7168]{1,0:T(8,128)(2,1)S(1)} collective-permute-done((bf16[32,7168]{1,0:T(8,128)(2,1)S(1)}, bf16[32,7168]{1,0:T(8,128)(2,1)S(1)}, u32[]{:S(2)}, u32[]{:S(2)}) %collective-permute-start.22) | collective-permute-done | bytes 458784 | tf_op jit(solution)/shard_map/ppermute | solution.py:38
  137.9 0.1 add.46
  138.0 1.2 collective-permute-start.24
  139.2 0.1 add.47
  139.3 2.1 %collective-permute-start.25 = (bf16[8,7168]{1,0:T(8,128)(2,1)S(1)}, bf16[8,7168]{1,0:T(8,128)(2,1)S(1)}, u32[]{:S(2)}, u32[]{:S(2)}) collective-permute-start(bf16[8,7168]{1,0:T(8,128)(2,1)S(1)} %add.47), channel_id=1, source_target_pairs={{0,96},{1,97},{2,98},{3,99},{4,100},{5,101},{6,102},{7,103},{8,104... | collective-permute-start | bytes 344072 | tf_op jit(solution)/shard_map/ppermute | solution.py:38
  141.4 0.1 add.48
  141.5 1.3 collective-permute-start.26
  142.8 0.1 add.45.refs_0_
  142.8 1.2 collective-permute-done.24.refs_1_
  144.0 0.1 collective-permute-done.25.refs_2_
  144.1 3.7 %collective-permute-done.26.refs_3_ = bf16[8,7168]{1,0:T(8,128)(2,1)S(1)} collective-permute-done((bf16[8,7168]{1,0:T(8,128)(2,1)S(1)}, bf16[8,7168]{1,0:T(8,128)(2,1)S(1)}, u32[]{:S(2)}, u32[]{:S(2)}) %collective-permute-start.26) | collective-permute-done | bytes 114720 | tf_op jit(solution)/shard_map/ppermute | solution.py:38
  147.9 0.7 add.49
  (23 shorter events, 0.1 us)
Async XLA Ops:
  0.0 53.6 %collective-permute-start.6 = (bf16[2,7168,128]{2,1,0:T(8,128)(2,1)}, bf16[2,7168,128]{2,1,0:T(8,128)(2,1)}, u32[]{:S(2)}, u32[]{:S(2)}) collective-permute-start(bf16[2,7168,128]{2,1,0:T(8,128)(2,1)} %gate.1), channel_id=1, source_target_pairs={{0,16},{1,17},{2,18},{3,19},{4,20},{5,21},{6,22},{7,23},{8,24},{9,... | collective-permute-start | bytes 11010056 | tf_op jit(solution)/shard_map/ppermute | solution.py:42
  0.0 53.7 %collective-permute-start.7 = (bf16[2,7168,128]{2,1,0:T(8,128)(2,1)}, bf16[2,7168,128]{2,1,0:T(8,128)(2,1)}, u32[]{:S(2)}, u32[]{:S(2)}) collective-permute-start(bf16[2,7168,128]{2,1,0:T(8,128)(2,1)} %up.1), channel_id=1, source_target_pairs={{0,16},{1,17},{2,18},{3,19},{4,20},{5,21},{6,22},{7,23},{8,24},{9,... | collective-permute-start | bytes 11010056 | tf_op jit(solution)/shard_map/ppermute | solution.py:42
  0.5 64.5 %collective-permute-start.8 = (bf16[2,128,7168]{2,1,0:T(8,128)(2,1)}, bf16[2,128,7168]{2,1,0:T(8,128)(2,1)}, u32[]{:S(2)}, u32[]{:S(2)}) collective-permute-start(bf16[2,128,7168]{2,1,0:T(8,128)(2,1)} %param.11), channel_id=1, source_target_pairs={{0,16},{1,17},{2,18},{3,19},{4,20},{5,21},{6,22},{7,23},{8,24},{9,... | collective-permute-start | bytes 11010056 | tf_op jit(solution)/shard_map/ppermute | solution.py:42
  2.0 0.9 copy-start.3
  3.1 5.2 %collective-permute-start = (bf16[8,7296]{1,0:T(8,128)(2,1)S(1)}, bf16[8,7296]{1,0:T(8,128)(2,1)S(1)}, u32[]{:S(2)}, u32[]{:S(2)}) collective-permute-start(bf16[8,7296]{1,0:T(8,128)(2,1)S(1)} %route.1.refs_0_), channel_id=1, source_target_pairs={{0,96},{1,97},{2,98},{3,99},{4,100},{5,101},{6,102},{7,103},{8,104... | collective-permute-start | bytes 350216 | tf_op jit(solution)/shard_map/ppermute | solution.py:38
  5.9 6.0 %collective-permute-start.1 = (bf16[8,7296]{1,0:T(8,128)(2,1)S(1)}, bf16[8,7296]{1,0:T(8,128)(2,1)S(1)}, u32[]{:S(2)}, u32[]{:S(2)}) collective-permute-start(bf16[8,7296]{1,0:T(8,128)(2,1)S(1)} %route.1.refs_0_), channel_id=1, source_target_pairs={{0,32},{1,33},{2,34},{3,35},{4,36},{5,37},{6,38},{7,39},{8,40},{9,... | collective-permute-start | bytes 350216 | tf_op jit(solution)/shard_map/ppermute | solution.py:38
  8.3 6.3 %collective-permute-start.2 = (bf16[8,7296]{1,0:T(8,128)(2,1)S(1)}, bf16[8,7296]{1,0:T(8,128)(2,1)S(1)}, u32[]{:S(2)}, u32[]{:S(2)}) collective-permute-start(bf16[8,7296]{1,0:T(8,128)(2,1)S(1)} %route.1.refs_0_), channel_id=1, source_target_pairs={{0,64},{1,65},{2,66},{3,67},{4,68},{5,69},{6,70},{7,71},{8,72},{9,... | collective-permute-start | bytes 350216 | tf_op jit(solution)/shard_map/ppermute | solution.py:38
  14.6 9.8 %collective-permute-start.3 = (bf16[32,7296]{1,0:T(8,128)(2,1)S(1)}, bf16[32,7296]{1,0:T(8,128)(2,1)S(1)}, u32[]{:S(2)}, u32[]{:S(2)}) collective-permute-start(bf16[32,7296]{1,0:T(8,128)(2,1)S(1)} %join.3.refs_0_), channel_id=1, source_target_pairs={{0,3},{1,0},{2,1},{3,2},{4,7},{5,4},{6,5},{7,6},{8,11},{9,8},{10,9... | collective-permute-start | bytes 1400840 | tf_op jit(solution)/shard_map/ppermute | solution.py:38
  15.4 9.1 %collective-permute-start.4 = (bf16[32,7296]{1,0:T(8,128)(2,1)S(1)}, bf16[32,7296]{1,0:T(8,128)(2,1)S(1)}, u32[]{:S(2)}, u32[]{:S(2)}) collective-permute-start(bf16[32,7296]{1,0:T(8,128)(2,1)S(1)} %join.3.refs_0_), channel_id=1, source_target_pairs={{0,1},{1,2},{2,3},{3,0},{4,5},{5,6},{6,7},{7,4},{8,9},{9,10},{10,1... | collective-permute-start | bytes 1400840 | tf_op jit(solution)/shard_map/ppermute | solution.py:38
  24.5 10.1 %collective-permute-start.5 = (bf16[32,7296]{1,0:T(8,128)(2,1)S(1)}, bf16[32,7296]{1,0:T(8,128)(2,1)S(1)}, u32[]{:S(2)}, u32[]{:S(2)}) collective-permute-start(bf16[32,7296]{1,0:T(8,128)(2,1)S(1)} %join.3.refs_0_), channel_id=1, source_target_pairs={{0,2},{1,3},{2,0},{3,1},{4,6},{5,7},{6,4},{7,5},{8,10},{9,11},{10,... | collective-permute-start | bytes 1400840 | tf_op jit(solution)/shard_map/ppermute | solution.py:38
  24.6 17.9 %collective-permute-start.9 = (bf16[64,7296]{1,0:T(8,128)(2,1)S(1)}, bf16[64,7296]{1,0:T(8,128)(2,1)S(1)}, u32[]{:S(2)}, u32[]{:S(2)}) collective-permute-start(bf16[64,7296]{1,0:T(8,128)(2,1)S(1)} %join.4.piece_a), channel_id=1, source_target_pairs={{0,4},{1,5},{2,6},{3,7},{4,8},{5,9},{6,10},{7,11},{8,12},{9,13},{1... | collective-permute-start | bytes 2801672 | tf_op jit(solution)/shard_map/ppermute | solution.py:38
  34.6 15.2 %collective-permute-start.10 = (bf16[64,7296]{1,0:T(8,128)(2,1)S(1)}, bf16[64,7296]{1,0:T(8,128)(2,1)}, u32[]{:S(2)}, u32[]{:S(2)}) collective-permute-start(bf16[64,7296]{1,0:T(8,128)(2,1)S(1)} %join.5.piece_b), channel_id=1, source_target_pairs={{0,12},{1,13},{2,14},{3,15},{4,0},{5,1},{6,2},{7,3},{8,4},{9,5},{1... | collective-permute-start | bytes 2801672 | tf_op jit(solution)/shard_map/ppermute | solution.py:38
  42.4 22.0 %collective-permute-start.14 = (bf16[64,7296]{1,0:T(8,128)(2,1)S(1)}, bf16[64,7296]{1,0:T(8,128)(2,1)}, u32[]{:S(2)}, u32[]{:S(2)}) collective-permute-start(bf16[64,7296]{1,0:T(8,128)(2,1)S(1)} %collective-permute-done.9.piece_a), channel_id=1, source_target_pairs={{0,4},{1,5},{2,6},{3,7},{4,8},{5,9},{6,10},{7,11},{8,12},{9,13},{1... | collective-permute-start | bytes 2801672 | tf_op jit(solution)/shard_map/ppermute | solution.py:38
  49.8 15.2 %collective-permute-start.15 = (bf16[64,7296]{1,0:T(8,128)(2,1)}, bf16[64,7296]{1,0:T(8,128)(2,1)}, u32[]{:S(2)}, u32[]{:S(2)}) collective-permute-start(bf16[64,7296]{1,0:T(8,128)(2,1)} %collective-permute-done.10.piece_b), channel_id=1, source_target_pairs={{0,12},{1,13},{2,14},{3,15},{4,0},{5,1},{6,2},{7,3},{8,4},{9,5},{1... | collective-permute-start | bytes 2801672 | tf_op jit(solution)/shard_map/ppermute | solution.py:38
  53.6 28.6 %collective-permute-start.12 = (bf16[64,7296]{1,0:T(8,128)(2,1)S(1)}, bf16[64,7296]{1,0:T(8,128)(2,1)S(1)}, u32[]{:S(2)}, u32[]{:S(2)}) collective-permute-start(bf16[64,7296]{1,0:T(8,128)(2,1)S(1)} %join.4.piece_a), channel_id=1, source_target_pairs={{0,12},{1,13},{2,14},{3,15},{4,0},{5,1},{6,2},{7,3},{8,4},{9,5},{1... | collective-permute-start | bytes 2801672 | tf_op jit(solution)/shard_map/ppermute | solution.py:38
  53.7 28.5 %collective-permute-start.13 = (bf16[64,7296]{1,0:T(8,128)(2,1)S(1)}, bf16[64,7296]{1,0:T(8,128)(2,1)S(1)}, u32[]{:S(2)}, u32[]{:S(2)}) collective-permute-start(bf16[64,7296]{1,0:T(8,128)(2,1)S(1)} %join.5.piece_b), channel_id=1, source_target_pairs={{0,4},{1,5},{2,6},{3,7},{4,8},{5,9},{6,10},{7,11},{8,12},{9,13},{1... | collective-permute-start | bytes 2801672 | tf_op jit(solution)/shard_map/ppermute | solution.py:38
  55.7 2.0 %copy-start.1 = (bf16[2,7168,128]{2,1,0:T(8,128)(2,1)S(1)}, bf16[2,7168,128]{2,1,0:T(8,128)(2,1)}, u32[]{:S(2)}) copy-start(bf16[2,7168,128]{2,1,0:T(8,128)(2,1)} %gate.1) | copy-start | bytes 11010052
  57.8 2.0 %copy-start.2 = (bf16[2,7168,128]{2,1,0:T(8,128)(2,1)S(1)}, bf16[2,7168,128]{2,1,0:T(8,128)(2,1)}, u32[]{:S(2)}) copy-start(bf16[2,7168,128]{2,1,0:T(8,128)(2,1)} %up.1) | copy-start | bytes 11010052
  61.1 4.2 %copy-start = (bf16[2,128,7168]{2,1,0:T(8,128)(2,1)S(1)}, bf16[2,128,7168]{2,1,0:T(8,128)(2,1)}, u32[]{:S(2)}) copy-start(bf16[2,128,7168]{2,1,0:T(8,128)(2,1)} %param.11) | copy-start | bytes 11010052
  71.1 16.3 %collective-permute-start.16 = (bf16[64,7168]{1,0:T(8,128)(2,1)S(1)}, bf16[64,7168]{1,0:T(8,128)(2,1)S(1)}, u32[]{:S(2)}, u32[]{:S(2)}) collective-permute-start(bf16[64,7168]{1,0:T(8,128)(2,1)S(1)} %get-tuple-element.16), channel_id=1, source_target_pairs={{0,4},{1,5},{2,6},{3,7},{4,8},{5,9},{6,10},{7,11},{8,12},{9,13},{1... | collective-permute-start | bytes 2752520 | tf_op jit(solution)/shard_map/ppermute | solution.py:38
  71.2 16.9 %collective-permute-start.20 = (bf16[64,7168]{1,0:T(8,128)(2,1)S(1)}, bf16[64,7168]{1,0:T(8,128)(2,1)S(1)}, u32[]{:S(2)}, u32[]{:S(2)}) collective-permute-start(bf16[64,7168]{1,0:T(8,128)(2,1)S(1)} %get-tuple-element.20), channel_id=1, source_target_pairs={{0,12},{1,13},{2,14},{3,15},{4,0},{5,1},{6,2},{7,3},{8,4},{9,5},{1... | collective-permute-start | bytes 2752520 | tf_op jit(solution)/shard_map/ppermute | solution.py:38
  80.4 16.4 %collective-permute-start.11 = (bf16[64,7168]{1,0:T(8,128)(2,1)S(1)}, bf16[64,7168]{1,0:T(8,128)(2,1)S(1)}, u32[]{:S(2)}, u32[]{:S(2)}) collective-permute-start(bf16[64,7168]{1,0:T(8,128)(2,1)S(1)} %get-tuple-element.14), channel_id=1, source_target_pairs={{0,12},{1,13},{2,14},{3,15},{4,0},{5,1},{6,2},{7,3},{8,4},{9,5},{1... | collective-permute-start | bytes 2752520 | tf_op jit(solution)/shard_map/ppermute | solution.py:38
  87.7 16.6 %collective-permute-start.17 = (bf16[64,7168]{1,0:T(8,128)(2,1)S(1)}, bf16[64,7168]{1,0:T(8,128)(2,1)S(1)}, u32[]{:S(2)}, u32[]{:S(2)}) collective-permute-start(bf16[64,7168]{1,0:T(8,128)(2,1)S(1)} %add.39), channel_id=1, source_target_pairs={{0,4},{1,5},{2,6},{3,7},{4,8},{5,9},{6,10},{7,11},{8,12},{9,13},{1... | collective-permute-start | bytes 2752520 | tf_op jit(solution)/shard_map/ppermute | solution.py:38
  88.0 34.0 %collective-permute-start.19 = (bf16[64,7168]{1,0:T(8,128)(2,1)S(1)}, bf16[64,7168]{1,0:T(8,128)(2,1)S(1)}, u32[]{:S(2)}, u32[]{:S(2)}) collective-permute-start(bf16[64,7168]{1,0:T(8,128)(2,1)S(1)} %get-tuple-element.18), channel_id=1, source_target_pairs={{0,4},{1,5},{2,6},{3,7},{4,8},{5,9},{6,10},{7,11},{8,12},{9,13},{1... | collective-permute-start | bytes 2752520 | tf_op jit(solution)/shard_map/ppermute | solution.py:38
  88.3 33.7 %collective-permute-start.21 = (bf16[64,7168]{1,0:T(8,128)(2,1)S(1)}, bf16[64,7168]{1,0:T(8,128)(2,1)S(1)}, u32[]{:S(2)}, u32[]{:S(2)}) collective-permute-start(bf16[64,7168]{1,0:T(8,128)(2,1)S(1)} %add.42), channel_id=1, source_target_pairs={{0,12},{1,13},{2,14},{3,15},{4,0},{5,1},{6,2},{7,3},{8,4},{9,5},{1... | collective-permute-start | bytes 2752520 | tf_op jit(solution)/shard_map/ppermute | solution.py:38
  104.4 19.3 %collective-permute-start.18 = (bf16[32,7168]{1,0:T(8,128)(2,1)S(1)}, bf16[32,7168]{1,0:T(8,128)(2,1)S(1)}, u32[]{:S(2)}, u32[]{:S(2)}) collective-permute-start(bf16[32,7168]{1,0:T(8,128)(2,1)S(1)} %add.41), channel_id=1, source_target_pairs={{0,1},{1,2},{2,3},{3,0},{4,5},{5,6},{6,7},{7,4},{8,9},{9,10},{10,1... | collective-permute-start | bytes 1376264 | tf_op jit(solution)/shard_map/ppermute | solution.py:38
  122.2 15.7 %collective-permute-start.22 = (bf16[32,7168]{1,0:T(8,128)(2,1)S(1)}, bf16[32,7168]{1,0:T(8,128)(2,1)S(1)}, u32[]{:S(2)}, u32[]{:S(2)}) collective-permute-start(bf16[32,7168]{1,0:T(8,128)(2,1)S(1)} %add.43), channel_id=1, source_target_pairs={{0,3},{1,0},{2,1},{3,2},{4,7},{5,4},{6,5},{7,6},{8,11},{9,8},{10,9... | collective-permute-start | bytes 1376264 | tf_op jit(solution)/shard_map/ppermute | solution.py:38
  122.5 15.4 %collective-permute-start.23 = (bf16[32,7168]{1,0:T(8,128)(2,1)S(1)}, bf16[32,7168]{1,0:T(8,128)(2,1)S(1)}, u32[]{:S(2)}, u32[]{:S(2)}) collective-permute-start(bf16[32,7168]{1,0:T(8,128)(2,1)S(1)} %add.44), channel_id=1, source_target_pairs={{0,2},{1,3},{2,0},{3,1},{4,6},{5,7},{6,4},{7,5},{8,10},{9,11},{10,... | collective-permute-start | bytes 1376264 | tf_op jit(solution)/shard_map/ppermute | solution.py:38
  138.0 6.1 %collective-permute-start.24 = (bf16[8,7168]{1,0:T(8,128)(2,1)S(1)}, bf16[8,7168]{1,0:T(8,128)(2,1)S(1)}, u32[]{:S(2)}, u32[]{:S(2)}) collective-permute-start(bf16[8,7168]{1,0:T(8,128)(2,1)S(1)} %add.46), channel_id=1, source_target_pairs={{0,32},{1,33},{2,34},{3,35},{4,36},{5,37},{6,38},{7,39},{8,40},{9,... | collective-permute-start | bytes 344072 | tf_op jit(solution)/shard_map/ppermute | solution.py:38
  139.3 4.9 %collective-permute-start.25 = (bf16[8,7168]{1,0:T(8,128)(2,1)S(1)}, bf16[8,7168]{1,0:T(8,128)(2,1)S(1)}, u32[]{:S(2)}, u32[]{:S(2)}) collective-permute-start(bf16[8,7168]{1,0:T(8,128)(2,1)S(1)} %add.47), channel_id=1, source_target_pairs={{0,96},{1,97},{2,98},{3,99},{4,100},{5,101},{6,102},{7,103},{8,104... | collective-permute-start | bytes 344072 | tf_op jit(solution)/shard_map/ppermute | solution.py:38
  141.5 6.4 %collective-permute-start.26 = (bf16[8,7168]{1,0:T(8,128)(2,1)S(1)}, bf16[8,7168]{1,0:T(8,128)(2,1)S(1)}, u32[]{:S(2)}, u32[]{:S(2)}) collective-permute-start(bf16[8,7168]{1,0:T(8,128)(2,1)S(1)} %add.48), channel_id=1, source_target_pairs={{0,64},{1,65},{2,66},{3,67},{4,68},{5,69},{6,70},{7,71},{8,72},{9,... | collective-permute-start | bytes 344072 | tf_op jit(solution)/shard_map/ppermute | solution.py:38
where the time goes:
time: 149 us
  waiting for transfers between devices  75.5 us (51%)
  starting transfers between devices  37.1 us (25%)
  Pallas kernels  28.9 us (19%)
  local copies, waits for them, and re-layouts  5.3 us (4%)
    ppermute x24, waiting for transfers between devices, send(): return lax.ppermute(value, AXES, pairs(phase, shift))  75.5 us
    ppermute x24, starting transfers between devices, send(): return lax.ppermute(value, AXES, pairs(phase, shift))  36.6 us
    pallas_call x4, Pallas kernels, experts_of(): pl.pallas_call(expert_kernel, out_shape=(shape, shape), in_specs=[VMEM] *...  21.8 us
    unnamed x8, local copies, waits for them, and re-layouts  5.3 us
    pallas_call x2, Pallas kernels, pack(): pl.pallas_call(pack_kernel, out_shape=jax.ShapeDtypeStruct((width, 2 * pe...  4.63 us
  transfers between devices with their start and end apart: 27, of which 14 were waited for; matrix products, arithmetic and copies ran while one was open for 1% of the time, Pallas kernels for 19%

commit v1 on v0

--- a/solution.py
+++ b/solution.py
@@ -76,9 +76,9 @@
     )(*arrays)
 
 
-def pack_kernel(gate, up, packed, sems):
+def pack_kernel(gate, up, down, packed, kept, sems):
     per_group, _, units = gate.shape
-    copies = []
+    copies = [pltpu.make_async_copy(down, kept, sems.at[2 * per_group])]
     for j, weight in enumerate((gate, up)):
         for e in range(per_group):
             k = j * per_group + e
@@ -131,17 +131,21 @@
     )(piece_a, piece_b, *weights)
 
 
-def pack(gate, up):
+def pack(gate, up, down):
     per_group, width, units = gate.shape
+    down = down.reshape(-1, width)
     return pl.pallas_call(
         pack_kernel,
-        out_shape=jax.ShapeDtypeStruct((width, 2 * per_group * units), gate.dtype),
-        in_specs=[HBM] * 2,
-        out_specs=VMEM,
-        scratch_shapes=[pltpu.SemaphoreType.DMA((2 * per_group,))],
+        out_shape=(
+            jax.ShapeDtypeStruct((width, 2 * per_group * units), gate.dtype),
+            jax.ShapeDtypeStruct(down.shape, down.dtype),
+        ),
+        in_specs=[HBM] * 3,
+        out_specs=(VMEM, VMEM),
+        scratch_shapes=[pltpu.SemaphoreType.DMA((2 * per_group + 1,))],
         compiler_params=pltpu.CompilerParams(vmem_limit_bytes=2 << 20),
         name="pack",
-    )(gate, up)
+    )(gate, up, down)
 
 
 def add_kernel(starts, *refs):
@@ -187,18 +191,18 @@
     spot = jnp.arange(2 * per_group * units)
     names = jnp.where(spot < per_group * units, row, row ^ 1) * per_group + spot // units % per_group
     spread = (jnp.arange(128)[:, None] == names[None, :]).astype(jnp.bfloat16)
+    block, spread = lax.optimization_barrier((block, spread))
 
     got = [send(block, 1, -k) for k in near]
-    weights = (
-        spread, pack(w_gate, w_up), pack(gate_other, up_other), w_down.reshape(-1, width), down_other.reshape(-1, width)
-    )
+    in_own, down_own = pack(w_gate, w_up, w_down)
+    in_other, down_other = pack(gate_other, up_other, down_other)
+    weights = (spread, in_own, in_other, down_own, down_other)
     a0 = join(8 * count, packed, (block, 0, 0), (got[0], 4 * count, 0))
     b0 = join(8 * count, packed, (got[1], 0, 0), (got[2], 4 * count, 0))
     am, bp = send(a0, 2, 1), send(b0, 2, -1)
     oa, ob = send(am, 2, 1), send(bp, 2, -1)
     bm, ap = send(b0, 2, 1), send(a0, 2, -1)
 
-    half = 8 * count
     sa0, sb0 = experts_of(a0, b0, weights)
     sam, sbp = experts_of(am, bp, weights)
     soa, sob = experts_of(oa, ob, weights)
@@ -208,16 +212,15 @@
     over_b = send(sob, 2, -1)
     direct_b = send(sbp, 2, 1)
     direct_a = send(sam, 2, -1)
-    relay_a = send(add(half, (sap, 0), (over_a, 0)), 2, 1)
-    relay_b = send(add(half, (sbm, 0), (over_b, 0)), 2, -1)
-
-    def group(at, *pieces):
-        return add(4 * count, *((piece, at) for piece in pieces))
-
-    got = [send(group(4 * count, sa0, direct_a, relay_a), 1, 1)]
-    got.append(send(group(0, sb0, direct_b, relay_b), 1, 3))
-    got.append(send(group(4 * count, sb0, direct_b, relay_b), 1, 2))
-    pieces = (group(0, sa0, direct_a, relay_a), *got)
+    part = 4 * count
+    relay1 = send(add(part, (sap, part), (over_a, part)), 2, 1)
+    relay2 = send(add(part, (sbm, part), (over_b, part)), 2, -1)
+    relay0 = send(add(part, (sap, 0), (over_a, 0)), 2, 1)
+    relay3 = send(add(part, (sbm, 0), (over_b, 0)), 2, -1)
+    got = [send(add(part, (sa0, part), (direct_a, part), (relay1, 0)), 1, 1)]
+    got.append(send(add(part, (sb0, part), (direct_b, part), (relay2, 0)), 1, 2))
+    got.append(send(add(part, (sb0, 0), (direct_b, 0), (relay3, 0)), 1, 3))
+    pieces = (add(part, (sa0, 0), (direct_a, 0), (relay0, 0)), *got)
     sums = [add(count, *((piece, k * count) for piece in pieces)) for k in range(4)]
     got = [send(sums[j], 0, k) for j, k in ((1, 1), (2, 3), (3, 2))]
     return add(count, *((piece, 0) for piece in (sums[0], *got)))

time: 149 us -> 139 us (0.933)
  the two profiles are of different devices: /device:TPU:24 before, /device:TPU:0 now
where the time goes in v1:
time: 139 us; the launch traced here: 138 us
  waiting for transfers between devices  68.8 us (49%)
  starting transfers between devices  42 us (30%)
  Pallas kernels  21 us (15%)
  local copies, waits for them, and re-layouts  4.98 us (4%)
  other arithmetic  1.48 us (1%)
    ppermute x26, waiting for transfers between devices, send(): return lax.ppermute(value, AXES, pairs(phase, shift))  68.7 us
    ppermute x26, starting transfers between devices, send(): return lax.ppermute(value, AXES, pairs(phase, shift))  41.5 us
    pallas_call x4, Pallas kernels, experts_of(): pl.pallas_call(expert_kernel, out_shape=(shape, shape), in_specs=[VMEM] *...  12.8 us
    pallas_call x2, Pallas kernels, pack(): pl.pallas_call(pack_kernel, out_shape=(jax.ShapeDtypeStruct((width, 2 * p...  5.8 us
    unnamed x8, local copies, waits for them, and re-layouts  4.98 us
  transfers between devices with their start and end apart: 29, of which 16 were waited for; matrix products, arithmetic and copies ran while one was open for 1% of the time, Pallas kernels for 15%

profile of v1, /device:TPU:0, one launch (start us, length us, event | category | flops | bytes accessed | tf_op | source)
XLA Modules:
  0.0 138.4 jit_solution(3692294785228489288)
XLA Ops:
  0.0 0.5 collective-permute-start.7
  0.5 0.7 convert_element_type.6
  1.2 0.8 pad_maximum_fusion.routing
  2.0 0.9 copy-done.3
  2.9 0.2 route.1.refs_0_
  3.1 3.1 %collective-permute-start.2 = (bf16[8,7296]{1,0:T(8,128)(2,1)S(1)}, bf16[8,7296]{1,0:T(8,128)(2,1)S(1)}, u32[]{:S(2)}, u32[]{:S(2)}) collective-permute-start(bf16[8,7296]{1,0:T(8,128)(2,1)S(1)} %route.1.refs_0_), channel_id=1, source_target_pairs={{0,64},{1,65},{2,66},{3,67},{4,68},{5,69},{6,70},{7,71},{8,72},{9,... | collective-permute-start | bytes 350216 | tf_op jit(solution)/shard_map/ppermute | solution.py:38
  6.2 0.6 collective-permute-start.1
  6.8 2.6 %collective-permute-done.2.refs_3_ = bf16[8,7296]{1,0:T(8,128)(2,1)S(1)} collective-permute-done((bf16[8,7296]{1,0:T(8,128)(2,1)S(1)}, bf16[8,7296]{1,0:T(8,128)(2,1)S(1)}, u32[]{:S(2)}, u32[]{:S(2)}) %collective-permute-start.2) | collective-permute-done | bytes 116768 | tf_op jit(solution)/shard_map/ppermute | solution.py:38
  9.4 2.9 %collective-permute-start = (bf16[8,7296]{1,0:T(8,128)(2,1)S(1)}, bf16[8,7296]{1,0:T(8,128)(2,1)S(1)}, u32[]{:S(2)}, u32[]{:S(2)}) collective-permute-start(bf16[8,7296]{1,0:T(8,128)(2,1)S(1)} %route.1.refs_0_), channel_id=1, source_target_pairs={{0,96},{1,97},{2,98},{3,99},{4,100},{5,101},{6,102},{7,103},{8,104... | collective-permute-start | bytes 350216 | tf_op jit(solution)/shard_map/ppermute | solution.py:38
  12.3 2.3 %collective-permute-done.refs_1_ = bf16[8,7296]{1,0:T(8,128)(2,1)S(1)} collective-permute-done((bf16[8,7296]{1,0:T(8,128)(2,1)S(1)}, bf16[8,7296]{1,0:T(8,128)(2,1)S(1)}, u32[]{:S(2)}, u32[]{:S(2)}) %collective-permute-start) | collective-permute-done | bytes 116768 | tf_op jit(solution)/shard_map/ppermute | solution.py:38
  14.7 3.1 %collective-permute-start.3 = (bf16[32,7296]{1,0:T(8,128)(2,1)S(1)}, bf16[32,7296]{1,0:T(8,128)(2,1)S(1)}, u32[]{:S(2)}, u32[]{:S(2)}) collective-permute-start(bf16[32,7296]{1,0:T(8,128)(2,1)S(1)} %join.3.refs_0_), channel_id=1, source_target_pairs={{0,3},{1,0},{2,1},{3,2},{4,7},{5,4},{6,5},{7,6},{8,11},{9,8},{10,9... | collective-permute-start | bytes 1400840 | tf_op jit(solution)/shard_map/ppermute | solution.py:38
  17.8 0.6 collective-permute-start.5
  18.4 10.5 %collective-permute-done.3.refs_1_ = bf16[32,7296]{1,0:T(8,128)(2,1)S(1)} collective-permute-done((bf16[32,7296]{1,0:T(8,128)(2,1)S(1)}, bf16[32,7296]{1,0:T(8,128)(2,1)S(1)}, u32[]{:S(2)}, u32[]{:S(2)}) %collective-permute-start.3) | collective-permute-done | bytes 466976 | tf_op jit(solution)/shard_map/ppermute | solution.py:38
  28.9 0.1 join.4.piece_a
  29.0 2.0 %collective-permute-start.9 = (bf16[64,7296]{1,0:T(8,128)(2,1)S(1)}, bf16[64,7296]{1,0:T(8,128)(2,1)S(1)}, u32[]{:S(2)}, u32[]{:S(2)}) collective-permute-start(bf16[64,7296]{1,0:T(8,128)(2,1)S(1)} %join.4.piece_a), channel_id=1, source_target_pairs={{0,4},{1,5},{2,6},{3,7},{4,8},{5,9},{6,10},{7,11},{8,12},{9,13},{1... | collective-permute-start | bytes 2801672 | tf_op jit(solution)/shard_map/ppermute | solution.py:38
  31.0 8.2 %collective-permute-done.4.refs_0_ = bf16[32,7296]{1,0:T(8,128)(2,1)S(1)} collective-permute-done((bf16[32,7296]{1,0:T(8,128)(2,1)S(1)}, bf16[32,7296]{1,0:T(8,128)(2,1)S(1)}, u32[]{:S(2)}, u32[]{:S(2)}) %collective-permute-start.4) | collective-permute-done | bytes 466976 | tf_op jit(solution)/shard_map/ppermute | solution.py:38
  39.1 0.1 join.5.piece_b
  39.2 4.1 %collective-permute-start.10 = (bf16[64,7296]{1,0:T(8,128)(2,1)S(1)}, bf16[64,7296]{1,0:T(8,128)(2,1)S(1)}, u32[]{:S(2)}, u32[]{:S(2)}) collective-permute-start(bf16[64,7296]{1,0:T(8,128)(2,1)S(1)} %join.5.piece_b), channel_id=1, source_target_pairs={{0,12},{1,13},{2,14},{3,15},{4,0},{5,1},{6,2},{7,3},{8,4},{9,5},{1... | collective-permute-start | bytes 2801672 | tf_op jit(solution)/shard_map/ppermute | solution.py:38
  43.3 4.4 %collective-permute-done.9.piece_a = bf16[64,7296]{1,0:T(8,128)(2,1)S(1)} collective-permute-done((bf16[64,7296]{1,0:T(8,128)(2,1)S(1)}, bf16[64,7296]{1,0:T(8,128)(2,1)S(1)}, u32[]{:S(2)}, u32[]{:S(2)}) %collective-permute-start.9) | collective-permute-done | bytes 933920 | tf_op jit(solution)/shard_map/ppermute | solution.py:38
  47.7 6.7 %collective-permute-done.10.piece_b = bf16[64,7296]{1,0:T(8,128)(2,1)S(1)} collective-permute-done((bf16[64,7296]{1,0:T(8,128)(2,1)S(1)}, bf16[64,7296]{1,0:T(8,128)(2,1)S(1)}, u32[]{:S(2)}, u32[]{:S(2)}) %collective-permute-start.10) | collective-permute-done | bytes 933920 | tf_op jit(solution)/shard_map/ppermute | solution.py:38
  54.4 3.7 %collective-permute-start.15 = (bf16[64,7296]{1,0:T(8,128)(2,1)S(1)}, bf16[64,7296]{1,0:T(8,128)(2,1)S(1)}, u32[]{:S(2)}, u32[]{:S(2)}) collective-permute-start(bf16[64,7296]{1,0:T(8,128)(2,1)S(1)} %collective-permute-done.10.piece_b), channel_id=1, source_target_pairs={{0,12},{1,13},{2,14},{3,15},{4,0},{5,1},{6,2},{7,3},{8,4},{9,5},{1... | collective-permute-start | bytes 2801672 | tf_op jit(solution)/shard_map/ppermute | solution.py:38
  58.1 2.0 %collective-permute-start.13 = (bf16[64,7296]{1,0:T(8,128)(2,1)S(1)}, bf16[64,7296]{1,0:T(8,128)(2,1)S(1)}, u32[]{:S(2)}, u32[]{:S(2)}) collective-permute-start(bf16[64,7296]{1,0:T(8,128)(2,1)S(1)} %join.5.piece_b), channel_id=1, source_target_pairs={{0,4},{1,5},{2,6},{3,7},{4,8},{5,9},{6,10},{7,11},{8,12},{9,13},{1... | collective-permute-start | bytes 2801672 | tf_op jit(solution)/shard_map/ppermute | solution.py:38
  60.1 2.0 %copy-done.1 = bf16[2,7168,128]{2,1,0:T(8,128)(2,1)S(1)} copy-done((bf16[2,7168,128]{2,1,0:T(8,128)(2,1)S(1)}, bf16[2,7168,128]{2,1,0:T(8,128)(2,1)}, u32[]{:S(2)}) %copy-start.1) | copy-done | bytes 3670040
  62.2 2.0 %copy-done.2 = bf16[2,128,7168]{2,1,0:T(8,128)(2,1)S(1)} copy-done((bf16[2,128,7168]{2,1,0:T(8,128)(2,1)S(1)}, bf16[2,128,7168]{2,1,0:T(8,128)(2,1)}, u32[]{:S(2)}) %copy-start.2) | copy-done | bytes 3670040
  64.2 1.6 %pack.2 = (bf16[7168,512]{1,0:T(8,128)(2,1)S(1)}, bf16[256,7168]{1,0:T(8,128)(2,1)S(1)}) custom-call(bf16[2,7168,128]{2,1,0:T(8,128)(2,1)S(1)} %copy-done, bf16[2,7168,128]{2,1,0:T(8,128)(2,1)S(1)} %copy-done.1, bf16[256,7168]{1,0:T(8,128)(2,1)S(1)} %bitcast.2), custom_call_target="tpu_custom_call" | custom-call | tf_op jit(solution)/shard_map/pack/pallas_call | solution.py:137
  65.8 4.2 %pack.3 = (bf16[7168,512]{1,0:T(8,128)(2,1)S(1)}, bf16[256,7168]{1,0:T(8,128)(2,1)S(1)}) custom-call(bf16[2,7168,128]{2,1,0:T(8,128)(2,1)} %collective-permute-done.6.gate, bf16[2,7168,128]{2,1,0:T(8,128)(2,1)} %collective-permute-done.7.up, bf16[256,7168]{1,0:T(8,128)(2,1)} %bitcast.1.down), custom_call_target="tpu_custom_call" | custom-call | tf_op jit(solution)/shard_map/pack/pallas_call | solution.py:137
  70.0 3.2 %experts.7 = (bf16[64,7168]{1,0:T(8,128)(2,1)S(1)}, bf16[64,7168]{1,0:T(8,128)(2,1)S(1)}) custom-call(bf16[64,7296]{1,0:T(8,128)(2,1)S(1)} %collective-permute-done.14.piece_a, bf16[64,7296]{1,0:T(8,128)(2,1)S(1)} %collective-permute-done.15.piece_b, bf16[128,512]{1,0:T(8,128)(2,1)S(1)} %fusion.spread, bf16[7168,512]{1,0:T(8,128)(2,1)S(1)} %get-tuple-element.21.in_own, ...), custom_call_target="tpu_custom_call" | custom-call | flops 2818572288 | bytes 3670016 | tf_op jit(solution)/shard_map/experts/pallas_call | solution.py:120
  73.3 0.1 collective-permute-start.16
  73.3 3.2 %collective-permute-start.21 = (bf16[64,7168]{1,0:T(8,128)(2,1)S(1)}, bf16[64,7168]{1,0:T(8,128)(2,1)S(1)}, u32[]{:S(2)}, u32[]{:S(2)}) collective-permute-start(bf16[64,7168]{1,0:T(8,128)(2,1)S(1)} %get-tuple-element.32), channel_id=1, source_target_pairs={{0,12},{1,13},{2,14},{3,15},{4,0},{5,1},{6,2},{7,3},{8,4},{9,5},{1... | collective-permute-start | bytes 2752520 | tf_op jit(solution)/shard_map/ppermute | solution.py:38
  76.6 3.2 %experts.5 = (bf16[64,7168]{1,0:T(8,128)(2,1)S(1)}, bf16[64,7168]{1,0:T(8,128)(2,1)S(1)}) custom-call(bf16[64,7296]{1,0:T(8,128)(2,1)S(1)} %collective-permute-done.9.piece_a, bf16[64,7296]{1,0:T(8,128)(2,1)S(1)} %collective-permute-done.10.piece_b, bf16[128,512]{1,0:T(8,128)(2,1)S(1)} %fusion.spread, bf16[7168,512]{1,0:T(8,128)(2,1)S(1)} %get-tuple-element.21.in_own, ...), custom_call_target="tpu_custom_call" | custom-call | flops 2818572288 | bytes 3670016 | tf_op jit(solution)/shard_map/experts/pallas_call | solution.py:120
  79.8 1.7 %collective-permute-start.11 = (bf16[64,7168]{1,0:T(8,128)(2,1)S(1)}, bf16[64,7168]{1,0:T(8,128)(2,1)S(1)}, u32[]{:S(2)}, u32[]{:S(2)}) collective-permute-start(bf16[64,7168]{1,0:T(8,128)(2,1)S(1)} %get-tuple-element.26), channel_id=1, source_target_pairs={{0,12},{1,13},{2,14},{3,15},{4,0},{5,1},{6,2},{7,3},{8,4},{9,5},{1... | collective-permute-start | bytes 2752520 | tf_op jit(solution)/shard_map/ppermute | solution.py:38
  81.5 0.4 collective-permute-start.20
  81.9 3.2 %experts.6 = (bf16[64,7168]{1,0:T(8,128)(2,1)S(1)}, bf16[64,7168]{1,0:T(8,128)(2,1)S(1)}) custom-call(bf16[64,7296]{1,0:T(8,128)(2,1)S(1)} %collective-permute-done.12.piece_a, bf16[64,7296]{1,0:T(8,128)(2,1)S(1)} %collective-permute-done.13.piece_b, bf16[128,512]{1,0:T(8,128)(2,1)S(1)} %fusion.spread, bf16[7168,512]{1,0:T(8,128)(2,1)S(1)} %get-tuple-element.21.in_own, ...), custom_call_target="tpu_custom_call" | custom-call | flops 2818572288 | bytes 3670016 | tf_op jit(solution)/shard_map/experts/pallas_call | solution.py:120
  85.1 2.8 %collective-permute-done.16.refs_1_ = bf16[64,7168]{1,0:T(8,128)(2,1)S(1)} collective-permute-done((bf16[64,7168]{1,0:T(8,128)(2,1)S(1)}, bf16[64,7168]{1,0:T(8,128)(2,1)S(1)}, u32[]{:S(2)}, u32[]{:S(2)}) %collective-permute-start.16) | collective-permute-done | bytes 917536 | tf_op jit(solution)/shard_map/ppermute | solution.py:38
  87.9 0.1 add.43
  88.0 0.1 collective-permute-start.18
  88.1 0.9 collective-permute-done.21.refs_1_
  89.0 0.1 add.45
  89.1 3.8 %collective-permute-start.22 = (bf16[32,7168]{1,0:T(8,128)(2,1)S(1)}, bf16[32,7168]{1,0:T(8,128)(2,1)S(1)}, u32[]{:S(2)}, u32[]{:S(2)}) collective-permute-start(bf16[32,7168]{1,0:T(8,128)(2,1)S(1)} %add.45), channel_id=1, source_target_pairs={{0,12},{1,13},{2,14},{3,15},{4,0},{5,1},{6,2},{7,3},{8,4},{9,5},{1... | collective-permute-start | bytes 1376264 | tf_op jit(solution)/shard_map/ppermute | solution.py:38
  92.9 0.1 add.47
  93.0 0.1 collective-permute-start.24
  93.1 3.2 %experts.4 = (bf16[64,7168]{1,0:T(8,128)(2,1)S(1)}, bf16[64,7168]{1,0:T(8,128)(2,1)S(1)}) custom-call(bf16[64,7296]{1,0:T(8,128)(2,1)S(1)} %join.4.piece_a, bf16[64,7296]{1,0:T(8,128)(2,1)S(1)} %join.5.piece_b, bf16[128,512]{1,0:T(8,128)(2,1)S(1)} %fusion.spread, bf16[7168,512]{1,0:T(8,128)(2,1)S(1)} %get-tuple-element.21.in_own, ...), custom_call_target="tpu_custom_call" | custom-call | flops 2818572288 | bytes 3670016 | tf_op jit(solution)/shard_map/experts/pallas_call | solution.py:120
  96.3 0.1 add.41
  96.4 2.4 %collective-permute-done.11.refs_1_ = bf16[64,7168]{1,0:T(8,128)(2,1)S(1)} collective-permute-done((bf16[64,7168]{1,0:T(8,128)(2,1)S(1)}, bf16[64,7168]{1,0:T(8,128)(2,1)S(1)}, u32[]{:S(2)}, u32[]{:S(2)}) %collective-permute-start.11) | collective-permute-done | bytes 917536 | tf_op jit(solution)/shard_map/ppermute | solution.py:38
  98.8 3.8 %collective-permute-done.18.refs_2_ = bf16[32,7168]{1,0:T(8,128)(2,1)S(1)} collective-permute-done((bf16[32,7168]{1,0:T(8,128)(2,1)S(1)}, bf16[32,7168]{1,0:T(8,128)(2,1)S(1)}, u32[]{:S(2)}, u32[]{:S(2)}) %collective-permute-start.18) | collective-permute-done | bytes 458784 | tf_op jit(solution)/shard_map/ppermute | solution.py:38
  102.7 0.2 add.44
  102.9 0.1 collective-permute-start.19
  102.9 0.8 collective-permute-done.22.refs_2_
  103.8 0.2 add.46
  103.9 2.7 %collective-permute-start.23 = (bf16[32,7168]{1,0:T(8,128)(2,1)S(1)}, bf16[32,7168]{1,0:T(8,128)(2,1)S(1)}, u32[]{:S(2)}, u32[]{:S(2)}) collective-permute-start(bf16[32,7168]{1,0:T(8,128)(2,1)S(1)} %add.46), channel_id=1, source_target_pairs={{0,2},{1,3},{2,0},{3,1},{4,6},{5,7},{6,4},{7,5},{8,10},{9,11},{10,... | collective-permute-start | bytes 1376264 | tf_op jit(solution)/shard_map/ppermute | solution.py:38
  106.7 9.6 %collective-permute-done.24.refs_2_ = bf16[32,7168]{1,0:T(8,128)(2,1)S(1)} collective-permute-done((bf16[32,7168]{1,0:T(8,128)(2,1)S(1)}, bf16[32,7168]{1,0:T(8,128)(2,1)S(1)}, u32[]{:S(2)}, u32[]{:S(2)}) %collective-permute-start.24) | collective-permute-done | bytes 458784 | tf_op jit(solution)/shard_map/ppermute | solution.py:38
  116.3 0.2 add.48
  116.4 1.6 %collective-permute-start.25 = (bf16[32,7168]{1,0:T(8,128)(2,1)S(1)}, bf16[32,7168]{1,0:T(8,128)(2,1)S(1)}, u32[]{:S(2)}, u32[]{:S(2)}) collective-permute-start(bf16[32,7168]{1,0:T(8,128)(2,1)S(1)} %add.48), channel_id=1, source_target_pairs={{0,3},{1,0},{2,1},{3,2},{4,7},{5,4},{6,5},{7,6},{8,11},{9,8},{10,9... | collective-permute-start | bytes 1376264 | tf_op jit(solution)/shard_map/ppermute | solution.py:38
  118.0 0.2 add.42.refs_0_
  118.2 9.3 %collective-permute-done.25.refs_3_ = bf16[32,7168]{1,0:T(8,128)(2,1)S(1)} collective-permute-done((bf16[32,7168]{1,0:T(8,128)(2,1)S(1)}, bf16[32,7168]{1,0:T(8,128)(2,1)S(1)}, u32[]{:S(2)}, u32[]{:S(2)}) %collective-permute-start.25) | collective-permute-done | bytes 458784 | tf_op jit(solution)/shard_map/ppermute | solution.py:38
  127.4 0.1 add.50
  127.5 1.8 %collective-permute-start.26 = (bf16[8,7168]{1,0:T(8,128)(2,1)S(1)}, bf16[8,7168]{1,0:T(8,128)(2,1)S(1)}, u32[]{:S(2)}, u32[]{:S(2)}) collective-permute-start(bf16[8,7168]{1,0:T(8,128)(2,1)S(1)} %add.50), channel_id=1, source_target_pairs={{0,32},{1,33},{2,34},{3,35},{4,36},{5,37},{6,38},{7,39},{8,40},{9,... | collective-permute-start | bytes 344072 | tf_op jit(solution)/shard_map/ppermute | solution.py:38
  129.3 2.0 %collective-permute-start.27 = (bf16[8,7168]{1,0:T(8,128)(2,1)S(1)}, bf16[8,7168]{1,0:T(8,128)(2,1)S(1)}, u32[]{:S(2)}, u32[]{:S(2)}) collective-permute-start(bf16[8,7168]{1,0:T(8,128)(2,1)S(1)} %add.51), channel_id=1, source_target_pairs={{0,96},{1,97},{2,98},{3,99},{4,100},{5,101},{6,102},{7,103},{8,104... | collective-permute-start | bytes 344072 | tf_op jit(solution)/shard_map/ppermute | solution.py:38
  131.3 0.1 add.52
  131.4 1.9 %collective-permute-start.28 = (bf16[8,7168]{1,0:T(8,128)(2,1)S(1)}, bf16[8,7168]{1,0:T(8,128)(2,1)S(1)}, u32[]{:S(2)}, u32[]{:S(2)}) collective-permute-start(bf16[8,7168]{1,0:T(8,128)(2,1)S(1)} %add.52), channel_id=1, source_target_pairs={{0,64},{1,65},{2,66},{3,67},{4,68},{5,69},{6,70},{7,71},{8,72},{9,... | collective-permute-start | bytes 344072 | tf_op jit(solution)/shard_map/ppermute | solution.py:38
  133.3 0.6 collective-permute-done.26.refs_1_
  133.9 0.3 collective-permute-done.27.refs_2_
  134.2 3.6 %collective-permute-done.28.refs_3_ = bf16[8,7168]{1,0:T(8,128)(2,1)S(1)} collective-permute-done((bf16[8,7168]{1,0:T(8,128)(2,1)S(1)}, bf16[8,7168]{1,0:T(8,128)(2,1)S(1)}, u32[]{:S(2)}, u32[]{:S(2)}) %collective-permute-start.28) | collective-permute-done | bytes 114720 | tf_op jit(solution)/shard_map/ppermute | solution.py:38
  137.7 0.7 add.53
  (29 shorter events, 0.3 us)
Async XLA Ops:
  0.0 58.1 %collective-permute-start.6 = (bf16[2,7168,128]{2,1,0:T(8,128)(2,1)}, bf16[2,7168,128]{2,1,0:T(8,128)(2,1)}, u32[]{:S(2)}, u32[]{:S(2)}) collective-permute-start(bf16[2,7168,128]{2,1,0:T(8,128)(2,1)} %gate.1), channel_id=1, source_target_pairs={{0,16},{1,17},{2,18},{3,19},{4,20},{5,21},{6,22},{7,23},{8,24},{9,... | collective-permute-start | bytes 11010056 | tf_op jit(solution)/shard_map/ppermute | solution.py:42
  0.0 58.1 %collective-permute-start.7 = (bf16[2,7168,128]{2,1,0:T(8,128)(2,1)}, bf16[2,7168,128]{2,1,0:T(8,128)(2,1)}, u32[]{:S(2)}, u32[]{:S(2)}) collective-permute-start(bf16[2,7168,128]{2,1,0:T(8,128)(2,1)} %up.1), channel_id=1, source_target_pairs={{0,16},{1,17},{2,18},{3,19},{4,20},{5,21},{6,22},{7,23},{8,24},{9,... | collective-permute-start | bytes 11010056 | tf_op jit(solution)/shard_map/ppermute | solution.py:42
  0.5 65.3 %collective-permute-start.8 = (bf16[2,128,7168]{2,1,0:T(8,128)(2,1)}, bf16[2,128,7168]{2,1,0:T(8,128)(2,1)}, u32[]{:S(2)}, u32[]{:S(2)}) collective-permute-start(bf16[2,128,7168]{2,1,0:T(8,128)(2,1)} %param.11), channel_id=1, source_target_pairs={{0,16},{1,17},{2,18},{3,19},{4,20},{5,21},{6,22},{7,23},{8,24},{9,... | collective-permute-start | bytes 11010056 | tf_op jit(solution)/shard_map/ppermute | solution.py:42
  2.0 0.9 copy-start.3
  3.1 6.3 %collective-permute-start.2 = (bf16[8,7296]{1,0:T(8,128)(2,1)S(1)}, bf16[8,7296]{1,0:T(8,128)(2,1)S(1)}, u32[]{:S(2)}, u32[]{:S(2)}) collective-permute-start(bf16[8,7296]{1,0:T(8,128)(2,1)S(1)} %route.1.refs_0_), channel_id=1, source_target_pairs={{0,64},{1,65},{2,66},{3,67},{4,68},{5,69},{6,70},{7,71},{8,72},{9,... | collective-permute-start | bytes 350216 | tf_op jit(solution)/shard_map/ppermute | solution.py:38
  6.2 6.1 %collective-permute-start.1 = (bf16[8,7296]{1,0:T(8,128)(2,1)S(1)}, bf16[8,7296]{1,0:T(8,128)(2,1)S(1)}, u32[]{:S(2)}, u32[]{:S(2)}) collective-permute-start(bf16[8,7296]{1,0:T(8,128)(2,1)S(1)} %route.1.refs_0_), channel_id=1, source_target_pairs={{0,32},{1,33},{2,34},{3,35},{4,36},{5,37},{6,38},{7,39},{8,40},{9,... | collective-permute-start | bytes 350216 | tf_op jit(solution)/shard_map/ppermute | solution.py:38
  6.8 53.3 %copy-start = (bf16[2,7168,128]{2,1,0:T(8,128)(2,1)S(1)}, bf16[2,7168,128]{2,1,0:T(8,128)(2,1)}, u32[]{:S(2)}) copy-start(bf16[2,7168,128]{2,1,0:T(8,128)(2,1)} %gate.1) | copy-start | bytes 11010052
  9.4 5.3 %collective-permute-start = (bf16[8,7296]{1,0:T(8,128)(2,1)S(1)}, bf16[8,7296]{1,0:T(8,128)(2,1)S(1)}, u32[]{:S(2)}, u32[]{:S(2)}) collective-permute-start(bf16[8,7296]{1,0:T(8,128)(2,1)S(1)} %route.1.refs_0_), channel_id=1, source_target_pairs={{0,96},{1,97},{2,98},{3,99},{4,100},{5,101},{6,102},{7,103},{8,104... | collective-permute-start | bytes 350216 | tf_op jit(solution)/shard_map/ppermute | solution.py:38
  14.7 14.2 %collective-permute-start.3 = (bf16[32,7296]{1,0:T(8,128)(2,1)S(1)}, bf16[32,7296]{1,0:T(8,128)(2,1)S(1)}, u32[]{:S(2)}, u32[]{:S(2)}) collective-permute-start(bf16[32,7296]{1,0:T(8,128)(2,1)S(1)} %join.3.refs_0_), channel_id=1, source_target_pairs={{0,3},{1,0},{2,1},{3,2},{4,7},{5,4},{6,5},{7,6},{8,11},{9,8},{10,9... | collective-permute-start | bytes 1400840 | tf_op jit(solution)/shard_map/ppermute | solution.py:38
  17.8 11.2 %collective-permute-start.5 = (bf16[32,7296]{1,0:T(8,128)(2,1)S(1)}, bf16[32,7296]{1,0:T(8,128)(2,1)S(1)}, u32[]{:S(2)}, u32[]{:S(2)}) collective-permute-start(bf16[32,7296]{1,0:T(8,128)(2,1)S(1)} %join.3.refs_0_), channel_id=1, source_target_pairs={{0,2},{1,3},{2,0},{3,1},{4,6},{5,7},{6,4},{7,5},{8,10},{9,11},{10,... | collective-permute-start | bytes 1400840 | tf_op jit(solution)/shard_map/ppermute | solution.py:38
  28.9 10.2 %collective-permute-start.4 = (bf16[32,7296]{1,0:T(8,128)(2,1)S(1)}, bf16[32,7296]{1,0:T(8,128)(2,1)S(1)}, u32[]{:S(2)}, u32[]{:S(2)}) collective-permute-start(bf16[32,7296]{1,0:T(8,128)(2,1)S(1)} %join.3.refs_0_), channel_id=1, source_target_pairs={{0,1},{1,2},{2,3},{3,0},{4,5},{5,6},{6,7},{7,4},{8,9},{9,10},{10,1... | collective-permute-start | bytes 1400840 | tf_op jit(solution)/shard_map/ppermute | solution.py:38
  29.0 18.7 %collective-permute-start.9 = (bf16[64,7296]{1,0:T(8,128)(2,1)S(1)}, bf16[64,7296]{1,0:T(8,128)(2,1)S(1)}, u32[]{:S(2)}, u32[]{:S(2)}) collective-permute-start(bf16[64,7296]{1,0:T(8,128)(2,1)S(1)} %join.4.piece_a), channel_id=1, source_target_pairs={{0,4},{1,5},{2,6},{3,7},{4,8},{5,9},{6,10},{7,11},{8,12},{9,13},{1... | collective-permute-start | bytes 2801672 | tf_op jit(solution)/shard_map/ppermute | solution.py:38
  39.2 15.2 %collective-permute-start.10 = (bf16[64,7296]{1,0:T(8,128)(2,1)S(1)}, bf16[64,7296]{1,0:T(8,128)(2,1)S(1)}, u32[]{:S(2)}, u32[]{:S(2)}) collective-permute-start(bf16[64,7296]{1,0:T(8,128)(2,1)S(1)} %join.5.piece_b), channel_id=1, source_target_pairs={{0,12},{1,13},{2,14},{3,15},{4,0},{5,1},{6,2},{7,3},{8,4},{9,5},{1... | collective-permute-start | bytes 2801672 | tf_op jit(solution)/shard_map/ppermute | solution.py:38
  47.7 22.4 %collective-permute-start.14 = (bf16[64,7296]{1,0:T(8,128)(2,1)S(1)}, bf16[64,7296]{1,0:T(8,128)(2,1)S(1)}, u32[]{:S(2)}, u32[]{:S(2)}) collective-permute-start(bf16[64,7296]{1,0:T(8,128)(2,1)S(1)} %collective-permute-done.9.piece_a), channel_id=1, source_target_pairs={{0,4},{1,5},{2,6},{3,7},{4,8},{5,9},{6,10},{7,11},{8,12},{9,13},{1... | collective-permute-start | bytes 2801672 | tf_op jit(solution)/shard_map/ppermute | solution.py:38
  54.4 15.6 %collective-permute-start.15 = (bf16[64,7296]{1,0:T(8,128)(2,1)S(1)}, bf16[64,7296]{1,0:T(8,128)(2,1)S(1)}, u32[]{:S(2)}, u32[]{:S(2)}) collective-permute-start(bf16[64,7296]{1,0:T(8,128)(2,1)S(1)} %collective-permute-done.10.piece_b), channel_id=1, source_target_pairs={{0,12},{1,13},{2,14},{3,15},{4,0},{5,1},{6,2},{7,3},{8,4},{9,5},{1... | collective-permute-start | bytes 2801672 | tf_op jit(solution)/shard_map/ppermute | solution.py:38
  58.1 23.4 %collective-permute-start.12 = (bf16[64,7296]{1,0:T(8,128)(2,1)S(1)}, bf16[64,7296]{1,0:T(8,128)(2,1)S(1)}, u32[]{:S(2)}, u32[]{:S(2)}) collective-permute-start(bf16[64,7296]{1,0:T(8,128)(2,1)S(1)} %join.4.piece_a), channel_id=1, source_target_pairs={{0,12},{1,13},{2,14},{3,15},{4,0},{5,1},{6,2},{7,3},{8,4},{9,5},{1... | collective-permute-start | bytes 2801672 | tf_op jit(solution)/shard_map/ppermute | solution.py:38
  58.1 23.8 %collective-permute-start.13 = (bf16[64,7296]{1,0:T(8,128)(2,1)S(1)}, bf16[64,7296]{1,0:T(8,128)(2,1)S(1)}, u32[]{:S(2)}, u32[]{:S(2)}) collective-permute-start(bf16[64,7296]{1,0:T(8,128)(2,1)S(1)} %join.5.piece_b), channel_id=1, source_target_pairs={{0,4},{1,5},{2,6},{3,7},{4,8},{5,9},{6,10},{7,11},{8,12},{9,13},{1... | collective-permute-start | bytes 2801672 | tf_op jit(solution)/shard_map/ppermute | solution.py:38
  60.1 2.0 %copy-start.1 = (bf16[2,7168,128]{2,1,0:T(8,128)(2,1)S(1)}, bf16[2,7168,128]{2,1,0:T(8,128)(2,1)}, u32[]{:S(2)}) copy-start(bf16[2,7168,128]{2,1,0:T(8,128)(2,1)} %up.1) | copy-start | bytes 11010052
  62.2 2.0 %copy-start.2 = (bf16[2,128,7168]{2,1,0:T(8,128)(2,1)S(1)}, bf16[2,128,7168]{2,1,0:T(8,128)(2,1)}, u32[]{:S(2)}) copy-start(bf16[2,128,7168]{2,1,0:T(8,128)(2,1)} %param.11) | copy-start | bytes 11010052
  73.3 14.7 %collective-permute-start.16 = (bf16[64,7168]{1,0:T(8,128)(2,1)S(1)}, bf16[64,7168]{1,0:T(8,128)(2,1)S(1)}, u32[]{:S(2)}, u32[]{:S(2)}) collective-permute-start(bf16[64,7168]{1,0:T(8,128)(2,1)S(1)} %get-tuple-element.28), channel_id=1, source_target_pairs={{0,4},{1,5},{2,6},{3,7},{4,8},{5,9},{6,10},{7,11},{8,12},{9,13},{1... | collective-permute-start | bytes 2752520 | tf_op jit(solution)/shard_map/ppermute | solution.py:38
  73.3 15.7 %collective-permute-start.21 = (bf16[64,7168]{1,0:T(8,128)(2,1)S(1)}, bf16[64,7168]{1,0:T(8,128)(2,1)S(1)}, u32[]{:S(2)}, u32[]{:S(2)}) collective-permute-start(bf16[64,7168]{1,0:T(8,128)(2,1)S(1)} %get-tuple-element.32), channel_id=1, source_target_pairs={{0,12},{1,13},{2,14},{3,15},{4,0},{5,1},{6,2},{7,3},{8,4},{9,5},{1... | collective-permute-start | bytes 2752520 | tf_op jit(solution)/shard_map/ppermute | solution.py:38
  79.8 19.1 %collective-permute-start.11 = (bf16[64,7168]{1,0:T(8,128)(2,1)S(1)}, bf16[64,7168]{1,0:T(8,128)(2,1)S(1)}, u32[]{:S(2)}, u32[]{:S(2)}) collective-permute-start(bf16[64,7168]{1,0:T(8,128)(2,1)S(1)} %get-tuple-element.26), channel_id=1, source_target_pairs={{0,12},{1,13},{2,14},{3,15},{4,0},{5,1},{6,2},{7,3},{8,4},{9,5},{1... | collective-permute-start | bytes 2752520 | tf_op jit(solution)/shard_map/ppermute | solution.py:38
  81.5 21.5 %collective-permute-start.20 = (bf16[64,7168]{1,0:T(8,128)(2,1)S(1)}, bf16[64,7168]{1,0:T(8,128)(2,1)S(1)}, u32[]{:S(2)}, u32[]{:S(2)}) collective-permute-start(bf16[64,7168]{1,0:T(8,128)(2,1)S(1)} %get-tuple-element.30), channel_id=1, source_target_pairs={{0,4},{1,5},{2,6},{3,7},{4,8},{5,9},{6,10},{7,11},{8,12},{9,13},{1... | collective-permute-start | bytes 2752520 | tf_op jit(solution)/shard_map/ppermute | solution.py:38
  88.0 14.6 %collective-permute-start.18 = (bf16[32,7168]{1,0:T(8,128)(2,1)S(1)}, bf16[32,7168]{1,0:T(8,128)(2,1)S(1)}, u32[]{:S(2)}, u32[]{:S(2)}) collective-permute-start(bf16[32,7168]{1,0:T(8,128)(2,1)S(1)} %add.43), channel_id=1, source_target_pairs={{0,4},{1,5},{2,6},{3,7},{4,8},{5,9},{6,10},{7,11},{8,12},{9,13},{1... | collective-permute-start | bytes 1376264 | tf_op jit(solution)/shard_map/ppermute | solution.py:38
  89.1 14.6 %collective-permute-start.22 = (bf16[32,7168]{1,0:T(8,128)(2,1)S(1)}, bf16[32,7168]{1,0:T(8,128)(2,1)S(1)}, u32[]{:S(2)}, u32[]{:S(2)}) collective-permute-start(bf16[32,7168]{1,0:T(8,128)(2,1)S(1)} %add.45), channel_id=1, source_target_pairs={{0,12},{1,13},{2,14},{3,15},{4,0},{5,1},{6,2},{7,3},{8,4},{9,5},{1... | collective-permute-start | bytes 1376264 | tf_op jit(solution)/shard_map/ppermute | solution.py:38
  93.0 23.3 %collective-permute-start.24 = (bf16[32,7168]{1,0:T(8,128)(2,1)S(1)}, bf16[32,7168]{1,0:T(8,128)(2,1)S(1)}, u32[]{:S(2)}, u32[]{:S(2)}) collective-permute-start(bf16[32,7168]{1,0:T(8,128)(2,1)S(1)} %add.47), channel_id=1, source_target_pairs={{0,12},{1,13},{2,14},{3,15},{4,0},{5,1},{6,2},{7,3},{8,4},{9,5},{1... | collective-permute-start | bytes 1376264 | tf_op jit(solution)/shard_map/ppermute | solution.py:38
  98.8 19.1 %collective-permute-start.17 = (bf16[32,7168]{1,0:T(8,128)(2,1)S(1)}, bf16[32,7168]{1,0:T(8,128)(2,1)S(1)}, u32[]{:S(2)}, u32[]{:S(2)}) collective-permute-start(bf16[32,7168]{1,0:T(8,128)(2,1)S(1)} %add.41), channel_id=1, source_target_pairs={{0,4},{1,5},{2,6},{3,7},{4,8},{5,9},{6,10},{7,11},{8,12},{9,13},{1... | collective-permute-start | bytes 1376264 | tf_op jit(solution)/shard_map/ppermute | solution.py:38
  102.9 15.3 %collective-permute-start.19 = (bf16[32,7168]{1,0:T(8,128)(2,1)S(1)}, bf16[32,7168]{1,0:T(8,128)(2,1)S(1)}, u32[]{:S(2)}, u32[]{:S(2)}) collective-permute-start(bf16[32,7168]{1,0:T(8,128)(2,1)S(1)} %add.44), channel_id=1, source_target_pairs={{0,1},{1,2},{2,3},{3,0},{4,5},{5,6},{6,7},{7,4},{8,9},{9,10},{10,1... | collective-permute-start | bytes 1376264 | tf_op jit(solution)/shard_map/ppermute | solution.py:38
  103.9 14.2 %collective-permute-start.23 = (bf16[32,7168]{1,0:T(8,128)(2,1)S(1)}, bf16[32,7168]{1,0:T(8,128)(2,1)S(1)}, u32[]{:S(2)}, u32[]{:S(2)}) collective-permute-start(bf16[32,7168]{1,0:T(8,128)(2,1)S(1)} %add.46), channel_id=1, source_target_pairs={{0,2},{1,3},{2,0},{3,1},{4,6},{5,7},{6,4},{7,5},{8,10},{9,11},{10,... | collective-permute-start | bytes 1376264 | tf_op jit(solution)/shard_map/ppermute | solution.py:38
  116.4 11.0 %collective-permute-start.25 = (bf16[32,7168]{1,0:T(8,128)(2,1)S(1)}, bf16[32,7168]{1,0:T(8,128)(2,1)S(1)}, u32[]{:S(2)}, u32[]{:S(2)}) collective-permute-start(bf16[32,7168]{1,0:T(8,128)(2,1)S(1)} %add.48), channel_id=1, source_target_pairs={{0,3},{1,0},{2,1},{3,2},{4,7},{5,4},{6,5},{7,6},{8,11},{9,8},{10,9... | collective-permute-start | bytes 1376264 | tf_op jit(solution)/shard_map/ppermute | solution.py:38
  127.5 6.4 %collective-permute-start.26 = (bf16[8,7168]{1,0:T(8,128)(2,1)S(1)}, bf16[8,7168]{1,0:T(8,128)(2,1)S(1)}, u32[]{:S(2)}, u32[]{:S(2)}) collective-permute-start(bf16[8,7168]{1,0:T(8,128)(2,1)S(1)} %add.50), channel_id=1, source_target_pairs={{0,32},{1,33},{2,34},{3,35},{4,36},{5,37},{6,38},{7,39},{8,40},{9,... | collective-permute-start | bytes 344072 | tf_op jit(solution)/shard_map/ppermute | solution.py:38
  129.3 4.9 %collective-permute-start.27 = (bf16[8,7168]{1,0:T(8,128)(2,1)S(1)}, bf16[8,7168]{1,0:T(8,128)(2,1)S(1)}, u32[]{:S(2)}, u32[]{:S(2)}) collective-permute-start(bf16[8,7168]{1,0:T(8,128)(2,1)S(1)} %add.51), channel_id=1, source_target_pairs={{0,96},{1,97},{2,98},{3,99},{4,100},{5,101},{6,102},{7,103},{8,104... | collective-permute-start | bytes 344072 | tf_op jit(solution)/shard_map/ppermute | solution.py:38
  131.4 6.4 %collective-permute-start.28 = (bf16[8,7168]{1,0:T(8,128)(2,1)S(1)}, bf16[8,7168]{1,0:T(8,128)(2,1)S(1)}, u32[]{:S(2)}, u32[]{:S(2)}) collective-permute-start(bf16[8,7168]{1,0:T(8,128)(2,1)S(1)} %add.52), channel_id=1, source_target_pairs={{0,64},{1,65},{2,66},{3,67},{4,68},{5,69},{6,70},{7,71},{8,72},{9,... | collective-permute-start | bytes 344072 | tf_op jit(solution)/shard_map/ppermute | solution.py:38

commit v2 on v1

--- a/solution.py
+++ b/solution.py
@@ -9,7 +9,7 @@
 
 
 AXES = ("row", "col")
-ORDER = (("x", "y", "z"), ("y", "z", "x"))
+ORDER = (("y", "z", "x"), ("x", "y", "z"))
 HBM = pl.BlockSpec(memory_space=pltpu.HBM)
 VMEM = pl.BlockSpec(memory_space=pltpu.VMEM)
 
@@ -42,19 +42,13 @@
     return lax.ppermute(value, AXES, [(i, i ^ 16) for i in range(128)])
 
 
-def route_kernel(tokens, routing, block):
-    width = tokens.shape[1]
-    logits = routing[:, :16]
-    names = lax.broadcasted_iota(jnp.int32, logits.shape, 1).astype(jnp.float32)
-    chosen = routing[:, 16:17] == names
-    for k in range(17, routing.shape[1]):
-        chosen = chosen | (routing[:, k : k + 1] == names)
-    scores = jnp.where(chosen, logits, -jnp.inf)
-    scores = jnp.exp(scores - jnp.max(scores, axis=1, keepdims=True))
-    probs = scores / jnp.sum(scores, axis=1, keepdims=True)
+def route_kernel(tokens, scores, block):
+    width, experts = tokens.shape[1], scores.shape[1]
+    probs = jnp.exp(scores[...] - jnp.max(scores[...], axis=1, keepdims=True))
+    probs = probs / jnp.sum(probs, axis=1, keepdims=True)
     block[:, :width] = tokens[...]
     block[:, width:] = jnp.zeros((block.shape[0], 128), block.dtype)
-    block[:, width : width + 16] = probs.astype(block.dtype)
+    block[:, width : width + experts] = probs.astype(block.dtype)
 
 
 def join_kernel(places, *refs):
@@ -175,7 +169,11 @@
     count, width = tokens.shape
     packed = width + 128
     near = (1, 3, 2)
-    routing = jnp.concatenate([router_logits, expert_ids.astype(jnp.float32)], axis=1)
+    experts = jnp.arange(router_logits.shape[1], dtype=jnp.int32)[None, :]
+    chosen = expert_ids[:, 0:1] == experts
+    for k in range(1, expert_ids.shape[1]):
+        chosen = chosen | (expert_ids[:, k : k + 1] == experts)
+    routing = jnp.where(chosen, router_logits, -jnp.inf)
     block = pl.pallas_call(
         route_kernel,
         out_shape=jax.ShapeDtypeStruct((count, packed), tokens.dtype),

time: 139 us -> 136 us (0.978)
  the two profiles are of different devices: /device:TPU:0 before, /device:TPU:6 now
where the time goes in v2:
time: 136 us
  waiting for transfers between devices  74.3 us (55%)
  starting transfers between devices  33.1 us (24%)
  Pallas kernels  21 us (15%)
  local copies, waits for them, and re-layouts  6.25 us (5%)
    ppermute x26, waiting for transfers between devices, send(): return lax.ppermute(value, AXES, pairs(phase, shift))  74.3 us
    ppermute x26, starting transfers between devices, send(): return lax.ppermute(value, AXES, pairs(phase, shift))  32.6 us
    pallas_call x4, Pallas kernels, experts_of(): pl.pallas_call(expert_kernel, out_shape=(shape, shape), in_specs=[VMEM] *...  12.8 us
    pallas_call x2, Pallas kernels, pack(): pl.pallas_call(pack_kernel, out_shape=(jax.ShapeDtypeStruct((width, 2 * p...  5.8 us
    unnamed x8, local copies, waits for them, and re-layouts  4.97 us
  transfers between devices with their start and end apart: 29, of which 17 were waited for; matrix products, arithmetic and copies ran while one was open for 2% of the time, Pallas kernels for 15%

profile of v2, /device:TPU:6, one launch (start us, length us, event | category | flops | bytes accessed | tf_op | source)
XLA Modules:
  0.0 135.7 jit_solution(2995375816410652203)
XLA Ops:
  0.0 0.5 collective-permute-start.7
  0.5 1.3 slice_reduce_fusion.7
  1.8 0.8 fusion.8.scores
  2.6 0.9 copy-done.3
  3.5 0.2 route.1.refs_0_
  3.6 3.2 %collective-permute-start.2 = (bf16[8,7296]{1,0:T(8,128)(2,1)S(1)}, bf16[8,7296]{1,0:T(8,128)(2,1)S(1)}, u32[]{:S(2)}, u32[]{:S(2)}) collective-permute-start(bf16[8,7296]{1,0:T(8,128)(2,1)S(1)} %route.1.refs_0_), channel_id=1, source_target_pairs={{0,2},{1,3},{2,0},{3,1},{4,6},{5,7},{6,4},{7,5},{8,10},{9,11},{10,... | collective-permute-start | bytes 350216 | tf_op jit(solution)/shard_map/ppermute | solution.py:38
  6.8 0.7 collective-permute-start.1
  7.5 2.4 %collective-permute-done.2.refs_3_ = bf16[8,7296]{1,0:T(8,128)(2,1)S(1)} collective-permute-done((bf16[8,7296]{1,0:T(8,128)(2,1)S(1)}, bf16[8,7296]{1,0:T(8,128)(2,1)S(1)}, u32[]{:S(2)}, u32[]{:S(2)}) %collective-permute-start.2) | collective-permute-done | bytes 116768 | tf_op jit(solution)/shard_map/ppermute | solution.py:38
  10.0 3.0 %collective-permute-start = (bf16[8,7296]{1,0:T(8,128)(2,1)S(1)}, bf16[8,7296]{1,0:T(8,128)(2,1)S(1)}, u32[]{:S(2)}, u32[]{:S(2)}) collective-permute-start(bf16[8,7296]{1,0:T(8,128)(2,1)S(1)} %route.1.refs_0_), channel_id=1, source_target_pairs={{0,3},{1,0},{2,1},{3,2},{4,7},{5,4},{6,5},{7,6},{8,11},{9,8},{10,9... | collective-permute-start | bytes 350216 | tf_op jit(solution)/shard_map/ppermute | solution.py:38
  13.0 2.3 %collective-permute-done.refs_1_ = bf16[8,7296]{1,0:T(8,128)(2,1)S(1)} collective-permute-done((bf16[8,7296]{1,0:T(8,128)(2,1)S(1)}, bf16[8,7296]{1,0:T(8,128)(2,1)S(1)}, u32[]{:S(2)}, u32[]{:S(2)}) %collective-permute-start) | collective-permute-done | bytes 116768 | tf_op jit(solution)/shard_map/ppermute | solution.py:38
  15.4 4.1 %collective-permute-start.3 = (bf16[32,7296]{1,0:T(8,128)(2,1)S(1)}, bf16[32,7296]{1,0:T(8,128)(2,1)S(1)}, u32[]{:S(2)}, u32[]{:S(2)}) collective-permute-start(bf16[32,7296]{1,0:T(8,128)(2,1)S(1)} %join.3.refs_0_), channel_id=1, source_target_pairs={{0,12},{1,13},{2,14},{3,15},{4,0},{5,1},{6,2},{7,3},{8,4},{9,5},{1... | collective-permute-start | bytes 1400840 | tf_op jit(solution)/shard_map/ppermute | solution.py:38
  19.5 11.1 %collective-permute-done.3.refs_1_ = bf16[32,7296]{1,0:T(8,128)(2,1)S(1)} collective-permute-done((bf16[32,7296]{1,0:T(8,128)(2,1)S(1)}, bf16[32,7296]{1,0:T(8,128)(2,1)S(1)}, u32[]{:S(2)}, u32[]{:S(2)}) %collective-permute-start.3) | collective-permute-done | bytes 466976 | tf_op jit(solution)/shard_map/ppermute | solution.py:38
  30.6 0.1 join.4.piece_a
  30.7 0.5 collective-permute-start.9
  31.2 14.6 %collective-permute-done.4.refs_0_ = bf16[32,7296]{1,0:T(8,128)(2,1)S(1)} collective-permute-done((bf16[32,7296]{1,0:T(8,128)(2,1)S(1)}, bf16[32,7296]{1,0:T(8,128)(2,1)S(1)}, u32[]{:S(2)}, u32[]{:S(2)}) %collective-permute-start.4) | collective-permute-done | bytes 466976 | tf_op jit(solution)/shard_map/ppermute | solution.py:38
  45.8 0.1 join.5.piece_b
  45.9 0.9 collective-permute-start.10
  46.8 2.4 %collective-permute-start.14 = (bf16[64,7296]{1,0:T(8,128)(2,1)S(1)}, bf16[64,7296]{1,0:T(8,128)(2,1)S(1)}, u32[]{:S(2)}, u32[]{:S(2)}) collective-permute-start(bf16[64,7296]{1,0:T(8,128)(2,1)S(1)} %collective-permute-done.9.piece_a), channel_id=1, source_target_pairs={{0,32},{1,33},{2,34},{3,35},{4,36},{5,37},{6,38},{7,39},{8,40},{9,... | collective-permute-start | bytes 2801672 | tf_op jit(solution)/shard_map/ppermute | solution.py:38
  49.2 11.5 %collective-permute-done.10.piece_b = bf16[64,7296]{1,0:T(8,128)(2,1)S(1)} collective-permute-done((bf16[64,7296]{1,0:T(8,128)(2,1)S(1)}, bf16[64,7296]{1,0:T(8,128)(2,1)S(1)}, u32[]{:S(2)}, u32[]{:S(2)}) %collective-permute-start.10) | collective-permute-done | bytes 933920 | tf_op jit(solution)/shard_map/ppermute | solution.py:38
  60.7 0.2 collective-permute-start.12
  60.9 3.2 %collective-permute-start.13 = (bf16[64,7296]{1,0:T(8,128)(2,1)S(1)}, bf16[64,7296]{1,0:T(8,128)(2,1)S(1)}, u32[]{:S(2)}, u32[]{:S(2)}) collective-permute-start(bf16[64,7296]{1,0:T(8,128)(2,1)S(1)} %join.5.piece_b), channel_id=1, source_target_pairs={{0,32},{1,33},{2,34},{3,35},{4,36},{5,37},{6,38},{7,39},{8,40},{9,... | collective-permute-start | bytes 2801672 | tf_op jit(solution)/shard_map/ppermute | solution.py:38
  64.1 2.0 %copy-done.1 = bf16[2,7168,128]{2,1,0:T(8,128)(2,1)S(1)} copy-done((bf16[2,7168,128]{2,1,0:T(8,128)(2,1)S(1)}, bf16[2,7168,128]{2,1,0:T(8,128)(2,1)}, u32[]{:S(2)}) %copy-start.1) | copy-done | bytes 3670040
  66.1 2.0 %copy-done.2 = bf16[2,128,7168]{2,1,0:T(8,128)(2,1)S(1)} copy-done((bf16[2,128,7168]{2,1,0:T(8,128)(2,1)S(1)}, bf16[2,128,7168]{2,1,0:T(8,128)(2,1)}, u32[]{:S(2)}) %copy-start.2) | copy-done | bytes 3670040
  68.1 1.6 %pack.2 = (bf16[7168,512]{1,0:T(8,128)(2,1)S(1)}, bf16[256,7168]{1,0:T(8,128)(2,1)S(1)}) custom-call(bf16[2,7168,128]{2,1,0:T(8,128)(2,1)S(1)} %copy-done, bf16[2,7168,128]{2,1,0:T(8,128)(2,1)S(1)} %copy-done.1, bf16[256,7168]{1,0:T(8,128)(2,1)S(1)} %bitcast.2), custom_call_target="tpu_custom_call" | custom-call | tf_op jit(solution)/shard_map/pack/pallas_call | solution.py:131
  69.7 4.2 %pack.3 = (bf16[7168,512]{1,0:T(8,128)(2,1)S(1)}, bf16[256,7168]{1,0:T(8,128)(2,1)S(1)}) custom-call(bf16[2,7168,128]{2,1,0:T(8,128)(2,1)} %collective-permute-done.6.gate, bf16[2,7168,128]{2,1,0:T(8,128)(2,1)} %collective-permute-done.7.up, bf16[256,7168]{1,0:T(8,128)(2,1)} %bitcast.1.down), custom_call_target="tpu_custom_call" | custom-call | tf_op jit(solution)/shard_map/pack/pallas_call | solution.py:131
  74.0 1.5 %collective-permute-done.15.piece_b = bf16[64,7296]{1,0:T(8,128)(2,1)S(1)} collective-permute-done((bf16[64,7296]{1,0:T(8,128)(2,1)S(1)}, bf16[64,7296]{1,0:T(8,128)(2,1)S(1)}, u32[]{:S(2)}, u32[]{:S(2)}) %collective-permute-start.15) | collective-permute-done | bytes 933920 | tf_op jit(solution)/shard_map/ppermute | solution.py:38
  75.5 3.2 %experts.7 = (bf16[64,7168]{1,0:T(8,128)(2,1)S(1)}, bf16[64,7168]{1,0:T(8,128)(2,1)S(1)}) custom-call(bf16[64,7296]{1,0:T(8,128)(2,1)S(1)} %collective-permute-done.14.piece_a, bf16[64,7296]{1,0:T(8,128)(2,1)S(1)} %collective-permute-done.15.piece_b, bf16[128,512]{1,0:T(8,128)(2,1)S(1)} %fusion.spread, bf16[7168,512]{1,0:T(8,128)(2,1)S(1)} %get-tuple-element.21.in_own, ...), custom_call_target="tpu_custom_call" | custom-call | flops 2818572288 | bytes 3670016 | tf_op jit(solution)/shard_map/experts/pallas_call | solution.py:114
  78.7 0.5 collective-permute-start.16
  79.2 1.6 %collective-permute-start.21 = (bf16[64,7168]{1,0:T(8,128)(2,1)S(1)}, bf16[64,7168]{1,0:T(8,128)(2,1)S(1)}, u32[]{:S(2)}, u32[]{:S(2)}) collective-permute-start(bf16[64,7168]{1,0:T(8,128)(2,1)S(1)} %get-tuple-element.32), channel_id=1, source_target_pairs={{0,96},{1,97},{2,98},{3,99},{4,100},{5,101},{6,102},{7,103},{8,104... | collective-permute-start | bytes 2752520 | tf_op jit(solution)/shard_map/ppermute | solution.py:38
  80.8 3.2 %experts.5 = (bf16[64,7168]{1,0:T(8,128)(2,1)S(1)}, bf16[64,7168]{1,0:T(8,128)(2,1)S(1)}) custom-call(bf16[64,7296]{1,0:T(8,128)(2,1)S(1)} %collective-permute-done.9.piece_a, bf16[64,7296]{1,0:T(8,128)(2,1)S(1)} %collective-permute-done.10.piece_b, bf16[128,512]{1,0:T(8,128)(2,1)S(1)} %fusion.spread, bf16[7168,512]{1,0:T(8,128)(2,1)S(1)} %get-tuple-element.21.in_own, ...), custom_call_target="tpu_custom_call" | custom-call | flops 2818572288 | bytes 3670016 | tf_op jit(solution)/shard_map/experts/pallas_call | solution.py:114
  84.0 0.1 collective-permute-start.11
  84.1 1.4 %collective-permute-done.12.piece_a = bf16[64,7296]{1,0:T(8,128)(2,1)S(1)} collective-permute-done((bf16[64,7296]{1,0:T(8,128)(2,1)S(1)}, bf16[64,7296]{1,0:T(8,128)(2,1)S(1)}, u32[]{:S(2)}, u32[]{:S(2)}) %collective-permute-start.12) | collective-permute-done | bytes 933920 | tf_op jit(solution)/shard_map/ppermute | solution.py:38
  85.5 1.8 %collective-permute-start.20 = (bf16[64,7168]{1,0:T(8,128)(2,1)S(1)}, bf16[64,7168]{1,0:T(8,128)(2,1)S(1)}, u32[]{:S(2)}, u32[]{:S(2)}) collective-permute-start(bf16[64,7168]{1,0:T(8,128)(2,1)S(1)} %get-tuple-element.30), channel_id=1, source_target_pairs={{0,32},{1,33},{2,34},{3,35},{4,36},{5,37},{6,38},{7,39},{8,40},{9,... | collective-permute-start | bytes 2752520 | tf_op jit(solution)/shard_map/ppermute | solution.py:38
  87.3 3.2 %experts.6 = (bf16[64,7168]{1,0:T(8,128)(2,1)S(1)}, bf16[64,7168]{1,0:T(8,128)(2,1)S(1)}) custom-call(bf16[64,7296]{1,0:T(8,128)(2,1)S(1)} %collective-permute-done.12.piece_a, bf16[64,7296]{1,0:T(8,128)(2,1)S(1)} %collective-permute-done.13.piece_b, bf16[128,512]{1,0:T(8,128)(2,1)S(1)} %fusion.spread, bf16[7168,512]{1,0:T(8,128)(2,1)S(1)} %get-tuple-element.21.in_own, ...), custom_call_target="tpu_custom_call" | custom-call | flops 2818572288 | bytes 3670016 | tf_op jit(solution)/shard_map/experts/pallas_call | solution.py:114
  90.6 1.6 %collective-permute-done.16.refs_1_ = bf16[64,7168]{1,0:T(8,128)(2,1)S(1)} collective-permute-done((bf16[64,7168]{1,0:T(8,128)(2,1)S(1)}, bf16[64,7168]{1,0:T(8,128)(2,1)S(1)}, u32[]{:S(2)}, u32[]{:S(2)}) %collective-permute-start.16) | collective-permute-done | bytes 917536 | tf_op jit(solution)/shard_map/ppermute | solution.py:38
  92.2 0.1 add.51
  92.3 1.7 %collective-permute-start.18 = (bf16[32,7168]{1,0:T(8,128)(2,1)S(1)}, bf16[32,7168]{1,0:T(8,128)(2,1)S(1)}, u32[]{:S(2)}, u32[]{:S(2)}) collective-permute-start(bf16[32,7168]{1,0:T(8,128)(2,1)S(1)} %add.51), channel_id=1, source_target_pairs={{0,32},{1,33},{2,34},{3,35},{4,36},{5,37},{6,38},{7,39},{8,40},{9,... | collective-permute-start | bytes 1376264 | tf_op jit(solution)/shard_map/ppermute | solution.py:38
  94.0 1.4 collective-permute-done.21.refs_1_
  95.4 0.1 add.53
  95.5 0.1 collective-permute-start.22
  95.5 0.1 add.55
  95.7 0.1 collective-permute-start.24
  95.7 3.2 %experts.4 = (bf16[64,7168]{1,0:T(8,128)(2,1)S(1)}, bf16[64,7168]{1,0:T(8,128)(2,1)S(1)}) custom-call(bf16[64,7296]{1,0:T(8,128)(2,1)S(1)} %join.4.piece_a, bf16[64,7296]{1,0:T(8,128)(2,1)S(1)} %join.5.piece_b, bf16[128,512]{1,0:T(8,128)(2,1)S(1)} %fusion.spread, bf16[7168,512]{1,0:T(8,128)(2,1)S(1)} %get-tuple-element.21.in_own, ...), custom_call_target="tpu_custom_call" | custom-call | flops 2818572288 | bytes 3670016 | tf_op jit(solution)/shard_map/experts/pallas_call | solution.py:114
  99.0 0.1 add.49
  99.1 6.1 %collective-permute-done.11.refs_1_ = bf16[64,7168]{1,0:T(8,128)(2,1)S(1)} collective-permute-done((bf16[64,7168]{1,0:T(8,128)(2,1)S(1)}, bf16[64,7168]{1,0:T(8,128)(2,1)S(1)}, u32[]{:S(2)}, u32[]{:S(2)}) %collective-permute-start.11) | collective-permute-done | bytes 917536 | tf_op jit(solution)/shard_map/ppermute | solution.py:38
  105.2 1.7 %collective-permute-done.18.refs_2_ = bf16[32,7168]{1,0:T(8,128)(2,1)S(1)} collective-permute-done((bf16[32,7168]{1,0:T(8,128)(2,1)S(1)}, bf16[32,7168]{1,0:T(8,128)(2,1)S(1)}, u32[]{:S(2)}, u32[]{:S(2)}) %collective-permute-start.18) | collective-permute-done | bytes 458784 | tf_op jit(solution)/shard_map/ppermute | solution.py:38
  106.9 0.2 add.52
  107.1 0.1 collective-permute-start.19
  107.2 2.9 %collective-permute-done.22.refs_2_ = bf16[32,7168]{1,0:T(8,128)(2,1)S(1)} collective-permute-done((bf16[32,7168]{1,0:T(8,128)(2,1)S(1)}, bf16[32,7168]{1,0:T(8,128)(2,1)S(1)}, u32[]{:S(2)}, u32[]{:S(2)}) %collective-permute-start.22) | collective-permute-done | bytes 458784 | tf_op jit(solution)/shard_map/ppermute | solution.py:38
  110.1 0.2 add.54
  110.3 1.1 collective-permute-start.23
  111.4 3.7 %collective-permute-done.24.refs_2_ = bf16[32,7168]{1,0:T(8,128)(2,1)S(1)} collective-permute-done((bf16[32,7168]{1,0:T(8,128)(2,1)S(1)}, bf16[32,7168]{1,0:T(8,128)(2,1)S(1)}, u32[]{:S(2)}, u32[]{:S(2)}) %collective-permute-start.24) | collective-permute-done | bytes 458784 | tf_op jit(solution)/shard_map/ppermute | solution.py:38
  115.0 0.2 add.56
  115.2 2.1 %collective-permute-start.25 = (bf16[32,7168]{1,0:T(8,128)(2,1)S(1)}, bf16[32,7168]{1,0:T(8,128)(2,1)S(1)}, u32[]{:S(2)}, u32[]{:S(2)}) collective-permute-start(bf16[32,7168]{1,0:T(8,128)(2,1)S(1)} %add.56), channel_id=1, source_target_pairs={{0,12},{1,13},{2,14},{3,15},{4,0},{5,1},{6,2},{7,3},{8,4},{9,5},{1... | collective-permute-start | bytes 1376264 | tf_op jit(solution)/shard_map/ppermute | solution.py:38
  117.3 0.2 add.50.refs_0_
  117.5 4.6 %collective-permute-done.23.refs_2_ = bf16[32,7168]{1,0:T(8,128)(2,1)S(1)} collective-permute-done((bf16[32,7168]{1,0:T(8,128)(2,1)S(1)}, bf16[32,7168]{1,0:T(8,128)(2,1)S(1)}, u32[]{:S(2)}, u32[]{:S(2)}) %collective-permute-start.23) | collective-permute-done | bytes 458784 | tf_op jit(solution)/shard_map/ppermute | solution.py:38
  122.0 2.6 %collective-permute-done.25.refs_3_ = bf16[32,7168]{1,0:T(8,128)(2,1)S(1)} collective-permute-done((bf16[32,7168]{1,0:T(8,128)(2,1)S(1)}, bf16[32,7168]{1,0:T(8,128)(2,1)S(1)}, u32[]{:S(2)}, u32[]{:S(2)}) %collective-permute-start.25) | collective-permute-done | bytes 458784 | tf_op jit(solution)/shard_map/ppermute | solution.py:38
  124.6 0.1 add.58
  124.7 1.1 collective-permute-start.26
  125.8 2.7 %collective-permute-start.27 = (bf16[8,7168]{1,0:T(8,128)(2,1)S(1)}, bf16[8,7168]{1,0:T(8,128)(2,1)S(1)}, u32[]{:S(2)}, u32[]{:S(2)}) collective-permute-start(bf16[8,7168]{1,0:T(8,128)(2,1)S(1)} %add.59), channel_id=1, source_target_pairs={{0,3},{1,0},{2,1},{3,2},{4,7},{5,4},{6,5},{7,6},{8,11},{9,8},{10,9... | collective-permute-start | bytes 344072 | tf_op jit(solution)/shard_map/ppermute | solution.py:38
  128.6 1.5 %collective-permute-start.28 = (bf16[8,7168]{1,0:T(8,128)(2,1)S(1)}, bf16[8,7168]{1,0:T(8,128)(2,1)S(1)}, u32[]{:S(2)}, u32[]{:S(2)}) collective-permute-start(bf16[8,7168]{1,0:T(8,128)(2,1)S(1)} %add.60), channel_id=1, source_target_pairs={{0,2},{1,3},{2,0},{3,1},{4,6},{5,7},{6,4},{7,5},{8,10},{9,11},{10,... | collective-permute-start | bytes 344072 | tf_op jit(solution)/shard_map/ppermute | solution.py:38
  130.2 1.0 collective-permute-done.26.refs_1_
  131.1 3.8 %collective-permute-done.28.refs_3_ = bf16[8,7168]{1,0:T(8,128)(2,1)S(1)} collective-permute-done((bf16[8,7168]{1,0:T(8,128)(2,1)S(1)}, bf16[8,7168]{1,0:T(8,128)(2,1)S(1)}, u32[]{:S(2)}, u32[]{:S(2)}) %collective-permute-start.28) | collective-permute-done | bytes 114720 | tf_op jit(solution)/shard_map/ppermute | solution.py:38
  135.0 0.7 add.61
  (29 shorter events, 0.3 us)
Async XLA Ops:
  0.0 60.7 %collective-permute-start.6 = (bf16[2,7168,128]{2,1,0:T(8,128)(2,1)}, bf16[2,7168,128]{2,1,0:T(8,128)(2,1)}, u32[]{:S(2)}, u32[]{:S(2)}) collective-permute-start(bf16[2,7168,128]{2,1,0:T(8,128)(2,1)} %gate.1), channel_id=1, source_target_pairs={{0,16},{1,17},{2,18},{3,19},{4,20},{5,21},{6,22},{7,23},{8,24},{9,... | collective-permute-start | bytes 11010056 | tf_op jit(solution)/shard_map/ppermute | solution.py:42
  0.0 60.9 %collective-permute-start.7 = (bf16[2,7168,128]{2,1,0:T(8,128)(2,1)}, bf16[2,7168,128]{2,1,0:T(8,128)(2,1)}, u32[]{:S(2)}, u32[]{:S(2)}) collective-permute-start(bf16[2,7168,128]{2,1,0:T(8,128)(2,1)} %up.1), channel_id=1, source_target_pairs={{0,16},{1,17},{2,18},{3,19},{4,20},{5,21},{6,22},{7,23},{8,24},{9,... | collective-permute-start | bytes 11010056 | tf_op jit(solution)/shard_map/ppermute | solution.py:42
  0.5 69.2 %collective-permute-start.8 = (bf16[2,128,7168]{2,1,0:T(8,128)(2,1)}, bf16[2,128,7168]{2,1,0:T(8,128)(2,1)}, u32[]{:S(2)}, u32[]{:S(2)}) collective-permute-start(bf16[2,128,7168]{2,1,0:T(8,128)(2,1)} %param.11), channel_id=1, source_target_pairs={{0,16},{1,17},{2,18},{3,19},{4,20},{5,21},{6,22},{7,23},{8,24},{9,... | collective-permute-start | bytes 11010056 | tf_op jit(solution)/shard_map/ppermute | solution.py:42
  2.6 0.9 copy-start.3
  3.6 6.3 %collective-permute-start.2 = (bf16[8,7296]{1,0:T(8,128)(2,1)S(1)}, bf16[8,7296]{1,0:T(8,128)(2,1)S(1)}, u32[]{:S(2)}, u32[]{:S(2)}) collective-permute-start(bf16[8,7296]{1,0:T(8,128)(2,1)S(1)} %route.1.refs_0_), channel_id=1, source_target_pairs={{0,2},{1,3},{2,0},{3,1},{4,6},{5,7},{6,4},{7,5},{8,10},{9,11},{10,... | collective-permute-start | bytes 350216 | tf_op jit(solution)/shard_map/ppermute | solution.py:38
  6.8 6.2 %collective-permute-start.1 = (bf16[8,7296]{1,0:T(8,128)(2,1)S(1)}, bf16[8,7296]{1,0:T(8,128)(2,1)S(1)}, u32[]{:S(2)}, u32[]{:S(2)}) collective-permute-start(bf16[8,7296]{1,0:T(8,128)(2,1)S(1)} %route.1.refs_0_), channel_id=1, source_target_pairs={{0,1},{1,2},{2,3},{3,0},{4,5},{5,6},{6,7},{7,4},{8,9},{9,10},{10,1... | collective-permute-start | bytes 350216 | tf_op jit(solution)/shard_map/ppermute | solution.py:38
  7.5 56.6 %copy-start = (bf16[2,7168,128]{2,1,0:T(8,128)(2,1)S(1)}, bf16[2,7168,128]{2,1,0:T(8,128)(2,1)}, u32[]{:S(2)}) copy-start(bf16[2,7168,128]{2,1,0:T(8,128)(2,1)} %gate.1) | copy-start | bytes 11010052
  10.0 5.4 %collective-permute-start = (bf16[8,7296]{1,0:T(8,128)(2,1)S(1)}, bf16[8,7296]{1,0:T(8,128)(2,1)S(1)}, u32[]{:S(2)}, u32[]{:S(2)}) collective-permute-start(bf16[8,7296]{1,0:T(8,128)(2,1)S(1)} %route.1.refs_0_), channel_id=1, source_target_pairs={{0,3},{1,0},{2,1},{3,2},{4,7},{5,4},{6,5},{7,6},{8,11},{9,8},{10,9... | collective-permute-start | bytes 350216 | tf_op jit(solution)/shard_map/ppermute | solution.py:38
  15.4 15.2 %collective-permute-start.3 = (bf16[32,7296]{1,0:T(8,128)(2,1)S(1)}, bf16[32,7296]{1,0:T(8,128)(2,1)S(1)}, u32[]{:S(2)}, u32[]{:S(2)}) collective-permute-start(bf16[32,7296]{1,0:T(8,128)(2,1)S(1)} %join.3.refs_0_), channel_id=1, source_target_pairs={{0,12},{1,13},{2,14},{3,15},{4,0},{5,1},{6,2},{7,3},{8,4},{9,5},{1... | collective-permute-start | bytes 1400840 | tf_op jit(solution)/shard_map/ppermute | solution.py:38
  19.5 11.2 %collective-permute-start.5 = (bf16[32,7296]{1,0:T(8,128)(2,1)S(1)}, bf16[32,7296]{1,0:T(8,128)(2,1)S(1)}, u32[]{:S(2)}, u32[]{:S(2)}) collective-permute-start(bf16[32,7296]{1,0:T(8,128)(2,1)S(1)} %join.3.refs_0_), channel_id=1, source_target_pairs={{0,8},{1,9},{2,10},{3,11},{4,12},{5,13},{6,14},{7,15},{8,0},{9,1},... | collective-permute-start | bytes 1400840 | tf_op jit(solution)/shard_map/ppermute | solution.py:38
  30.6 15.2 %collective-permute-start.4 = (bf16[32,7296]{1,0:T(8,128)(2,1)S(1)}, bf16[32,7296]{1,0:T(8,128)(2,1)S(1)}, u32[]{:S(2)}, u32[]{:S(2)}) collective-permute-start(bf16[32,7296]{1,0:T(8,128)(2,1)S(1)} %join.3.refs_0_), channel_id=1, source_target_pairs={{0,4},{1,5},{2,6},{3,7},{4,8},{5,9},{6,10},{7,11},{8,12},{9,13},{1... | collective-permute-start | bytes 1400840 | tf_op jit(solution)/shard_map/ppermute | solution.py:38
  30.7 16.1 %collective-permute-start.9 = (bf16[64,7296]{1,0:T(8,128)(2,1)S(1)}, bf16[64,7296]{1,0:T(8,128)(2,1)S(1)}, u32[]{:S(2)}, u32[]{:S(2)}) collective-permute-start(bf16[64,7296]{1,0:T(8,128)(2,1)S(1)} %join.4.piece_a), channel_id=1, source_target_pairs={{0,32},{1,33},{2,34},{3,35},{4,36},{5,37},{6,38},{7,39},{8,40},{9,... | collective-permute-start | bytes 2801672 | tf_op jit(solution)/shard_map/ppermute | solution.py:38
  45.9 14.8 %collective-permute-start.10 = (bf16[64,7296]{1,0:T(8,128)(2,1)S(1)}, bf16[64,7296]{1,0:T(8,128)(2,1)S(1)}, u32[]{:S(2)}, u32[]{:S(2)}) collective-permute-start(bf16[64,7296]{1,0:T(8,128)(2,1)S(1)} %join.5.piece_b), channel_id=1, source_target_pairs={{0,96},{1,97},{2,98},{3,99},{4,100},{5,101},{6,102},{7,103},{8,104... | collective-permute-start | bytes 2801672 | tf_op jit(solution)/shard_map/ppermute | solution.py:38
  46.8 27.2 %collective-permute-start.14 = (bf16[64,7296]{1,0:T(8,128)(2,1)S(1)}, bf16[64,7296]{1,0:T(8,128)(2,1)S(1)}, u32[]{:S(2)}, u32[]{:S(2)}) collective-permute-start(bf16[64,7296]{1,0:T(8,128)(2,1)S(1)} %collective-permute-done.9.piece_a), channel_id=1, source_target_pairs={{0,32},{1,33},{2,34},{3,35},{4,36},{5,37},{6,38},{7,39},{8,40},{9,... | collective-permute-start | bytes 2801672 | tf_op jit(solution)/shard_map/ppermute | solution.py:38
  60.7 14.8 %collective-permute-start.15 = (bf16[64,7296]{1,0:T(8,128)(2,1)S(1)}, bf16[64,7296]{1,0:T(8,128)(2,1)S(1)}, u32[]{:S(2)}, u32[]{:S(2)}) collective-permute-start(bf16[64,7296]{1,0:T(8,128)(2,1)S(1)} %collective-permute-done.10.piece_b), channel_id=1, source_target_pairs={{0,96},{1,97},{2,98},{3,99},{4,100},{5,101},{6,102},{7,103},{8,104... | collective-permute-start | bytes 2801672 | tf_op jit(solution)/shard_map/ppermute | solution.py:38
  60.7 24.8 %collective-permute-start.12 = (bf16[64,7296]{1,0:T(8,128)(2,1)S(1)}, bf16[64,7296]{1,0:T(8,128)(2,1)S(1)}, u32[]{:S(2)}, u32[]{:S(2)}) collective-permute-start(bf16[64,7296]{1,0:T(8,128)(2,1)S(1)} %join.4.piece_a), channel_id=1, source_target_pairs={{0,96},{1,97},{2,98},{3,99},{4,100},{5,101},{6,102},{7,103},{8,104... | collective-permute-start | bytes 2801672 | tf_op jit(solution)/shard_map/ppermute | solution.py:38
  60.9 26.4 %collective-permute-start.13 = (bf16[64,7296]{1,0:T(8,128)(2,1)S(1)}, bf16[64,7296]{1,0:T(8,128)(2,1)S(1)}, u32[]{:S(2)}, u32[]{:S(2)}) collective-permute-start(bf16[64,7296]{1,0:T(8,128)(2,1)S(1)} %join.5.piece_b), channel_id=1, source_target_pairs={{0,32},{1,33},{2,34},{3,35},{4,36},{5,37},{6,38},{7,39},{8,40},{9,... | collective-permute-start | bytes 2801672 | tf_op jit(solution)/shard_map/ppermute | solution.py:38
  64.1 2.0 %copy-start.1 = (bf16[2,7168,128]{2,1,0:T(8,128)(2,1)S(1)}, bf16[2,7168,128]{2,1,0:T(8,128)(2,1)}, u32[]{:S(2)}) copy-start(bf16[2,7168,128]{2,1,0:T(8,128)(2,1)} %up.1) | copy-start | bytes 11010052
  66.1 2.0 %copy-start.2 = (bf16[2,128,7168]{2,1,0:T(8,128)(2,1)S(1)}, bf16[2,128,7168]{2,1,0:T(8,128)(2,1)}, u32[]{:S(2)}) copy-start(bf16[2,128,7168]{2,1,0:T(8,128)(2,1)} %param.11) | copy-start | bytes 11010052
  78.7 13.5 %collective-permute-start.16 = (bf16[64,7168]{1,0:T(8,128)(2,1)S(1)}, bf16[64,7168]{1,0:T(8,128)(2,1)S(1)}, u32[]{:S(2)}, u32[]{:S(2)}) collective-permute-start(bf16[64,7168]{1,0:T(8,128)(2,1)S(1)} %get-tuple-element.28), channel_id=1, source_target_pairs={{0,32},{1,33},{2,34},{3,35},{4,36},{5,37},{6,38},{7,39},{8,40},{9,... | collective-permute-start | bytes 2752520 | tf_op jit(solution)/shard_map/ppermute | solution.py:38
  79.2 16.1 %collective-permute-start.21 = (bf16[64,7168]{1,0:T(8,128)(2,1)S(1)}, bf16[64,7168]{1,0:T(8,128)(2,1)S(1)}, u32[]{:S(2)}, u32[]{:S(2)}) collective-permute-start(bf16[64,7168]{1,0:T(8,128)(2,1)S(1)} %get-tuple-element.32), channel_id=1, source_target_pairs={{0,96},{1,97},{2,98},{3,99},{4,100},{5,101},{6,102},{7,103},{8,104... | collective-permute-start | bytes 2752520 | tf_op jit(solution)/shard_map/ppermute | solution.py:38
  84.0 21.2 %collective-permute-start.11 = (bf16[64,7168]{1,0:T(8,128)(2,1)S(1)}, bf16[64,7168]{1,0:T(8,128)(2,1)S(1)}, u32[]{:S(2)}, u32[]{:S(2)}) collective-permute-start(bf16[64,7168]{1,0:T(8,128)(2,1)S(1)} %get-tuple-element.26), channel_id=1, source_target_pairs={{0,96},{1,97},{2,98},{3,99},{4,100},{5,101},{6,102},{7,103},{8,104... | collective-permute-start | bytes 2752520 | tf_op jit(solution)/shard_map/ppermute | solution.py:38
  85.5 21.7 %collective-permute-start.20 = (bf16[64,7168]{1,0:T(8,128)(2,1)S(1)}, bf16[64,7168]{1,0:T(8,128)(2,1)S(1)}, u32[]{:S(2)}, u32[]{:S(2)}) collective-permute-start(bf16[64,7168]{1,0:T(8,128)(2,1)S(1)} %get-tuple-element.30), channel_id=1, source_target_pairs={{0,32},{1,33},{2,34},{3,35},{4,36},{5,37},{6,38},{7,39},{8,40},{9,... | collective-permute-start | bytes 2752520 | tf_op jit(solution)/shard_map/ppermute | solution.py:38
  92.3 14.6 %collective-permute-start.18 = (bf16[32,7168]{1,0:T(8,128)(2,1)S(1)}, bf16[32,7168]{1,0:T(8,128)(2,1)S(1)}, u32[]{:S(2)}, u32[]{:S(2)}) collective-permute-start(bf16[32,7168]{1,0:T(8,128)(2,1)S(1)} %add.51), channel_id=1, source_target_pairs={{0,32},{1,33},{2,34},{3,35},{4,36},{5,37},{6,38},{7,39},{8,40},{9,... | collective-permute-start | bytes 1376264 | tf_op jit(solution)/shard_map/ppermute | solution.py:38
  95.5 14.6 %collective-permute-start.22 = (bf16[32,7168]{1,0:T(8,128)(2,1)S(1)}, bf16[32,7168]{1,0:T(8,128)(2,1)S(1)}, u32[]{:S(2)}, u32[]{:S(2)}) collective-permute-start(bf16[32,7168]{1,0:T(8,128)(2,1)S(1)} %add.53), channel_id=1, source_target_pairs={{0,96},{1,97},{2,98},{3,99},{4,100},{5,101},{6,102},{7,103},{8,104... | collective-permute-start | bytes 1376264 | tf_op jit(solution)/shard_map/ppermute | solution.py:38
  95.7 19.4 %collective-permute-start.24 = (bf16[32,7168]{1,0:T(8,128)(2,1)S(1)}, bf16[32,7168]{1,0:T(8,128)(2,1)S(1)}, u32[]{:S(2)}, u32[]{:S(2)}) collective-permute-start(bf16[32,7168]{1,0:T(8,128)(2,1)S(1)} %add.55), channel_id=1, source_target_pairs={{0,96},{1,97},{2,98},{3,99},{4,100},{5,101},{6,102},{7,103},{8,104... | collective-permute-start | bytes 1376264 | tf_op jit(solution)/shard_map/ppermute | solution.py:38
  105.2 12.1 %collective-permute-start.17 = (bf16[32,7168]{1,0:T(8,128)(2,1)S(1)}, bf16[32,7168]{1,0:T(8,128)(2,1)S(1)}, u32[]{:S(2)}, u32[]{:S(2)}) collective-permute-start(bf16[32,7168]{1,0:T(8,128)(2,1)S(1)} %add.49), channel_id=1, source_target_pairs={{0,32},{1,33},{2,34},{3,35},{4,36},{5,37},{6,38},{7,39},{8,40},{9,... | collective-permute-start | bytes 1376264 | tf_op jit(solution)/shard_map/ppermute | solution.py:38
  107.1 10.4 %collective-permute-start.19 = (bf16[32,7168]{1,0:T(8,128)(2,1)S(1)}, bf16[32,7168]{1,0:T(8,128)(2,1)S(1)}, u32[]{:S(2)}, u32[]{:S(2)}) collective-permute-start(bf16[32,7168]{1,0:T(8,128)(2,1)S(1)} %add.52), channel_id=1, source_target_pairs={{0,4},{1,5},{2,6},{3,7},{4,8},{5,9},{6,10},{7,11},{8,12},{9,13},{1... | collective-permute-start | bytes 1376264 | tf_op jit(solution)/shard_map/ppermute | solution.py:38
  110.3 11.8 %collective-permute-start.23 = (bf16[32,7168]{1,0:T(8,128)(2,1)S(1)}, bf16[32,7168]{1,0:T(8,128)(2,1)S(1)}, u32[]{:S(2)}, u32[]{:S(2)}) collective-permute-start(bf16[32,7168]{1,0:T(8,128)(2,1)S(1)} %add.54), channel_id=1, source_target_pairs={{0,8},{1,9},{2,10},{3,11},{4,12},{5,13},{6,14},{7,15},{8,0},{9,1},... | collective-permute-start | bytes 1376264 | tf_op jit(solution)/shard_map/ppermute | solution.py:38
  115.2 9.4 %collective-permute-start.25 = (bf16[32,7168]{1,0:T(8,128)(2,1)S(1)}, bf16[32,7168]{1,0:T(8,128)(2,1)S(1)}, u32[]{:S(2)}, u32[]{:S(2)}) collective-permute-start(bf16[32,7168]{1,0:T(8,128)(2,1)S(1)} %add.56), channel_id=1, source_target_pairs={{0,12},{1,13},{2,14},{3,15},{4,0},{5,1},{6,2},{7,3},{8,4},{9,5},{1... | collective-permute-start | bytes 1376264 | tf_op jit(solution)/shard_map/ppermute | solution.py:38
  124.7 6.5 %collective-permute-start.26 = (bf16[8,7168]{1,0:T(8,128)(2,1)S(1)}, bf16[8,7168]{1,0:T(8,128)(2,1)S(1)}, u32[]{:S(2)}, u32[]{:S(2)}) collective-permute-start(bf16[8,7168]{1,0:T(8,128)(2,1)S(1)} %add.58), channel_id=1, source_target_pairs={{0,1},{1,2},{2,3},{3,0},{4,5},{5,6},{6,7},{7,4},{8,9},{9,10},{10,1... | collective-permute-start | bytes 344072 | tf_op jit(solution)/shard_map/ppermute | solution.py:38
  125.8 5.4 %collective-permute-start.27 = (bf16[8,7168]{1,0:T(8,128)(2,1)S(1)}, bf16[8,7168]{1,0:T(8,128)(2,1)S(1)}, u32[]{:S(2)}, u32[]{:S(2)}) collective-permute-start(bf16[8,7168]{1,0:T(8,128)(2,1)S(1)} %add.59), channel_id=1, source_target_pairs={{0,3},{1,0},{2,1},{3,2},{4,7},{5,4},{6,5},{7,6},{8,11},{9,8},{10,9... | collective-permute-start | bytes 344072 | tf_op jit(solution)/shard_map/ppermute | solution.py:38
  128.6 6.4 %collective-permute-start.28 = (bf16[8,7168]{1,0:T(8,128)(2,1)S(1)}, bf16[8,7168]{1,0:T(8,128)(2,1)S(1)}, u32[]{:S(2)}, u32[]{:S(2)}) collective-permute-start(bf16[8,7168]{1,0:T(8,128)(2,1)S(1)} %add.60), channel_id=1, source_target_pairs={{0,2},{1,3},{2,0},{3,1},{4,6},{5,7},{6,4},{7,5},{8,10},{9,11},{10,... | collective-permute-start | bytes 344072 | tf_op jit(solution)/shard_map/ppermute | solution.py:38

commit v3 on v1

--- a/solution.py
+++ b/solution.py
@@ -9,7 +9,7 @@
 
 
 AXES = ("row", "col")
-ORDER = (("x", "y", "z"), ("y", "z", "x"))
+ORDER = (("y", "z", "x"), ("x", "y", "z"))
 HBM = pl.BlockSpec(memory_space=pltpu.HBM)
 VMEM = pl.BlockSpec(memory_space=pltpu.VMEM)
 
@@ -29,7 +29,7 @@
             at = place(row, col)
             to = dict(at)
             axis = ORDER[at["core"]][phase]
-            to[axis] = (to[axis] + shift) % 4
+            to[axis] = to[axis] ^ shift
             moves.append((index(at), index(to)))
     return moves
 
@@ -44,17 +44,18 @@
 
 def route_kernel(tokens, routing, block):
     width = tokens.shape[1]
-    logits = routing[:, :16]
+    experts = 16
+    logits = routing[:, :experts]
     names = lax.broadcasted_iota(jnp.int32, logits.shape, 1).astype(jnp.float32)
-    chosen = routing[:, 16:17] == names
-    for k in range(17, routing.shape[1]):
+    chosen = routing[:, experts : experts + 1] == names
+    for k in range(experts + 1, routing.shape[1]):
         chosen = chosen | (routing[:, k : k + 1] == names)
     scores = jnp.where(chosen, logits, -jnp.inf)
     scores = jnp.exp(scores - jnp.max(scores, axis=1, keepdims=True))
     probs = scores / jnp.sum(scores, axis=1, keepdims=True)
     block[:, :width] = tokens[...]
     block[:, width:] = jnp.zeros((block.shape[0], 128), block.dtype)
-    block[:, width : width + 16] = probs.astype(block.dtype)
+    block[:, width : width + experts] = probs.astype(block.dtype)
 
 
 def join_kernel(places, *refs):
@@ -184,7 +185,7 @@
         compiler_params=pltpu.CompilerParams(vmem_limit_bytes=2 << 20),
         name="route",
     )(tokens, routing)
-    got = [send(block, 0, -k) for k in near]
+    got = [send(block, 0, k) for k in near]
     gate_other, up_other, down_other = swap(w_gate), swap(w_up), swap(w_down)
     block = join(4 * count, packed, *((piece, k * count, 0) for k, piece in enumerate([block, *got])))
     row = lax.axis_index("row")
@@ -193,30 +194,31 @@
     spread = (jnp.arange(128)[:, None] == names[None, :]).astype(jnp.bfloat16)
     block, spread = lax.optimization_barrier((block, spread))
 
-    got = [send(block, 1, -k) for k in near]
+    got = [send(block, 1, k) for k in near]
     in_own, down_own = pack(w_gate, w_up, w_down)
     in_other, down_other = pack(gate_other, up_other, down_other)
     weights = (spread, in_own, in_other, down_own, down_other)
     a0 = join(8 * count, packed, (block, 0, 0), (got[0], 4 * count, 0))
     b0 = join(8 * count, packed, (got[1], 0, 0), (got[2], 4 * count, 0))
-    am, bp = send(a0, 2, 1), send(b0, 2, -1)
-    oa, ob = send(am, 2, 1), send(bp, 2, -1)
-    bm, ap = send(b0, 2, 1), send(a0, 2, -1)
+    am, bp = send(a0, 2, 1), send(b0, 2, 3)
+    oa, ob = send(am, 2, 3), send(bp, 2, 1)
+    bm, ap = send(b0, 2, 1), send(a0, 2, 3)
 
     sa0, sb0 = experts_of(a0, b0, weights)
     sam, sbp = experts_of(am, bp, weights)
     soa, sob = experts_of(oa, ob, weights)
     sap, sbm = experts_of(ap, bm, weights)
 
-    over_a = send(soa, 2, 1)
-    over_b = send(sob, 2, -1)
-    direct_b = send(sbp, 2, 1)
-    direct_a = send(sam, 2, -1)
+    over_a = send(soa, 2, 3)
+    over_b = send(sob, 2, 1)
+    direct_b = send(sbm, 2, 1)
+    direct_a = send(sap, 2, 3)
+
     part = 4 * count
-    relay1 = send(add(part, (sap, part), (over_a, part)), 2, 1)
-    relay2 = send(add(part, (sbm, part), (over_b, part)), 2, -1)
-    relay0 = send(add(part, (sap, 0), (over_a, 0)), 2, 1)
-    relay3 = send(add(part, (sbm, 0), (over_b, 0)), 2, -1)
+    relay1 = send(add(part, (sam, part), (over_a, part)), 2, 1)
+    relay2 = send(add(part, (sbp, part), (over_b, part)), 2, 3)
+    relay0 = send(add(part, (sam, 0), (over_a, 0)), 2, 1)
+    relay3 = send(add(part, (sbp, 0), (over_b, 0)), 2, 3)
     got = [send(add(part, (sa0, part), (direct_a, part), (relay1, 0)), 1, 1)]
     got.append(send(add(part, (sb0, part), (direct_b, part), (relay2, 0)), 1, 2))
     got.append(send(add(part, (sb0, 0), (direct_b, 0), (relay3, 0)), 1, 3))

time: 139 us -> 130 us (0.935)
  waiting for transfers between devices: 68.8 us -> 54.5 us
  starting transfers between devices: 42 us -> 47.5 us
    ppermute x26, waiting for transfers between devices: 68.7 us -> 54.5 us  [send(): return lax.ppermute(value, AXES, pairs(phase, shift))]
    ppermute x26, starting transfers between devices: 41.5 us -> 46.9 us  [send(): return lax.ppermute(value, AXES, pairs(phase, shift))]
  transfers between devices with their start and end apart: 29 -> 29, of which waited for: 16 -> 17; matrix products, arithmetic and copies ran while one was open for 1% -> 1% of each run, Pallas kernels for 15% -> 16%
where the time goes in v3:
time: 130 us
  waiting for transfers between devices  54.5 us (42%)
  starting transfers between devices  47.5 us (37%)
  Pallas kernels  21 us (16%)
  local copies, waits for them, and re-layouts  4.98 us (4%)
  other arithmetic  1.48 us (1%)
    ppermute x26, waiting for transfers between devices, send(): return lax.ppermute(value, AXES, pairs(phase, shift))  54.5 us
    ppermute x26, starting transfers between devices, send(): return lax.ppermute(value, AXES, pairs(phase, shift))  46.9 us
    pallas_call x4, Pallas kernels, experts_of(): pl.pallas_call(expert_kernel, out_shape=(shape, shape), in_specs=[VMEM] *...  12.8 us
    pallas_call x2, Pallas kernels, pack(): pl.pallas_call(pack_kernel, out_shape=(jax.ShapeDtypeStruct((width, 2 * p...  5.8 us
    unnamed x8, local copies, waits for them, and re-layouts  4.98 us
  transfers between devices with their start and end apart: 29, of which 17 were waited for; matrix products, arithmetic and copies ran while one was open for 1% of the time, Pallas kernels for 16%

profile of v3, /device:TPU:0, one launch (start us, length us, event | category | flops | bytes accessed | tf_op | source)
XLA Modules:
  0.0 129.7 jit_solution(5936431757441848018)
XLA Ops:
  0.0 0.5 collective-permute-start.7
  0.5 0.7 convert_element_type.6
  1.2 0.8 pad_maximum_fusion.routing
  2.0 0.9 copy-done.3
  2.9 0.2 route.1.refs_0_
  3.1 3.3 %collective-permute-start.2 = (bf16[8,7296]{1,0:T(8,128)(2,1)S(1)}, bf16[8,7296]{1,0:T(8,128)(2,1)S(1)}, u32[]{:S(2)}, u32[]{:S(2)}) collective-permute-start(bf16[8,7296]{1,0:T(8,128)(2,1)S(1)} %route.1.refs_0_), channel_id=1, source_target_pairs={{0,2},{1,3},{2,0},{3,1},{4,6},{5,7},{6,4},{7,5},{8,10},{9,11},{10,... | collective-permute-start | bytes 350216 | tf_op jit(solution)/shard_map/ppermute | solution.py:38
  6.4 1.1 collective-permute-start.1
  7.5 1.9 %collective-permute-done.2.refs_3_ = bf16[8,7296]{1,0:T(8,128)(2,1)S(1)} collective-permute-done((bf16[8,7296]{1,0:T(8,128)(2,1)S(1)}, bf16[8,7296]{1,0:T(8,128)(2,1)S(1)}, u32[]{:S(2)}, u32[]{:S(2)}) %collective-permute-start.2) | collective-permute-done | bytes 116768 | tf_op jit(solution)/shard_map/ppermute | solution.py:38
  9.4 1.7 %collective-permute-start = (bf16[8,7296]{1,0:T(8,128)(2,1)S(1)}, bf16[8,7296]{1,0:T(8,128)(2,1)S(1)}, u32[]{:S(2)}, u32[]{:S(2)}) collective-permute-start(bf16[8,7296]{1,0:T(8,128)(2,1)S(1)} %route.1.refs_0_), channel_id=1, source_target_pairs={{0,1},{1,0},{2,3},{3,2},{4,5},{5,4},{6,7},{7,6},{8,9},{9,8},{10,11... | collective-permute-start | bytes 350216 | tf_op jit(solution)/shard_map/ppermute | solution.py:38
  11.2 1.2 collective-permute-done.1.refs_2_
  12.4 1.8 %collective-permute-done.refs_1_ = bf16[8,7296]{1,0:T(8,128)(2,1)S(1)} collective-permute-done((bf16[8,7296]{1,0:T(8,128)(2,1)S(1)}, bf16[8,7296]{1,0:T(8,128)(2,1)S(1)}, u32[]{:S(2)}, u32[]{:S(2)}) %collective-permute-start) | collective-permute-done | bytes 116768 | tf_op jit(solution)/shard_map/ppermute | solution.py:38
  14.3 2.1 %collective-permute-start.3 = (bf16[32,7296]{1,0:T(8,128)(2,1)S(1)}, bf16[32,7296]{1,0:T(8,128)(2,1)S(1)}, u32[]{:S(2)}, u32[]{:S(2)}) collective-permute-start(bf16[32,7296]{1,0:T(8,128)(2,1)S(1)} %join.3.refs_0_), channel_id=1, source_target_pairs={{0,4},{1,5},{2,6},{3,7},{4,0},{5,1},{6,2},{7,3},{8,12},{9,13},{10,... | collective-permute-start | bytes 1400840 | tf_op jit(solution)/shard_map/ppermute | solution.py:38
  16.4 3.6 %collective-permute-start.5 = (bf16[32,7296]{1,0:T(8,128)(2,1)S(1)}, bf16[32,7296]{1,0:T(8,128)(2,1)S(1)}, u32[]{:S(2)}, u32[]{:S(2)}) collective-permute-start(bf16[32,7296]{1,0:T(8,128)(2,1)S(1)} %join.3.refs_0_), channel_id=1, source_target_pairs={{0,8},{1,9},{2,10},{3,11},{4,12},{5,13},{6,14},{7,15},{8,0},{9,1},... | collective-permute-start | bytes 1400840 | tf_op jit(solution)/shard_map/ppermute | solution.py:38
  20.0 3.0 %collective-permute-done.3.refs_1_ = bf16[32,7296]{1,0:T(8,128)(2,1)S(1)} collective-permute-done((bf16[32,7296]{1,0:T(8,128)(2,1)S(1)}, bf16[32,7296]{1,0:T(8,128)(2,1)S(1)}, u32[]{:S(2)}, u32[]{:S(2)}) %collective-permute-start.3) | collective-permute-done | bytes 466976 | tf_op jit(solution)/shard_map/ppermute | solution.py:38
  22.9 4.1 %collective-permute-start.4 = (bf16[32,7296]{1,0:T(8,128)(2,1)S(1)}, bf16[32,7296]{1,0:T(8,128)(2,1)S(1)}, u32[]{:S(2)}, u32[]{:S(2)}) collective-permute-start(bf16[32,7296]{1,0:T(8,128)(2,1)S(1)} %join.3.refs_0_), channel_id=1, source_target_pairs={{0,12},{1,13},{2,14},{3,15},{4,8},{5,9},{6,10},{7,11},{8,4},{9,5},... | collective-permute-start | bytes 1400840 | tf_op jit(solution)/shard_map/ppermute | solution.py:38
  27.1 0.1 join.4.piece_a
  27.1 4.5 %collective-permute-done.5.refs_1_ = bf16[32,7296]{1,0:T(8,128)(2,1)S(1)} collective-permute-done((bf16[32,7296]{1,0:T(8,128)(2,1)S(1)}, bf16[32,7296]{1,0:T(8,128)(2,1)S(1)}, u32[]{:S(2)}, u32[]{:S(2)}) %collective-permute-start.5) | collective-permute-done | bytes 466976 | tf_op jit(solution)/shard_map/ppermute | solution.py:38
  31.6 1.5 %collective-permute-start.12 = (bf16[64,7296]{1,0:T(8,128)(2,1)S(1)}, bf16[64,7296]{1,0:T(8,128)(2,1)S(1)}, u32[]{:S(2)}, u32[]{:S(2)}) collective-permute-start(bf16[64,7296]{1,0:T(8,128)(2,1)S(1)} %join.4.piece_a), channel_id=1, source_target_pairs={{0,32},{1,33},{2,34},{3,35},{4,36},{5,37},{6,38},{7,39},{8,40},{9,... | collective-permute-start | bytes 2801672 | tf_op jit(solution)/shard_map/ppermute | solution.py:38
  33.1 3.4 %collective-permute-done.4.refs_0_ = bf16[32,7296]{1,0:T(8,128)(2,1)S(1)} collective-permute-done((bf16[32,7296]{1,0:T(8,128)(2,1)S(1)}, bf16[32,7296]{1,0:T(8,128)(2,1)S(1)}, u32[]{:S(2)}, u32[]{:S(2)}) %collective-permute-start.4) | collective-permute-done | bytes 466976 | tf_op jit(solution)/shard_map/ppermute | solution.py:38
  36.6 2.8 %collective-permute-start.13 = (bf16[64,7296]{1,0:T(8,128)(2,1)S(1)}, bf16[64,7296]{1,0:T(8,128)(2,1)S(1)}, u32[]{:S(2)}, u32[]{:S(2)}) collective-permute-start(bf16[64,7296]{1,0:T(8,128)(2,1)S(1)} %join.5.piece_b), channel_id=1, source_target_pairs={{0,96},{1,97},{2,98},{3,99},{4,100},{5,101},{6,102},{7,103},{8,104... | collective-permute-start | bytes 2801672 | tf_op jit(solution)/shard_map/ppermute | solution.py:38
  39.4 5.8 %collective-permute-done.12.piece_a = bf16[64,7296]{1,0:T(8,128)(2,1)S(1)} collective-permute-done((bf16[64,7296]{1,0:T(8,128)(2,1)S(1)}, bf16[64,7296]{1,0:T(8,128)(2,1)S(1)}, u32[]{:S(2)}, u32[]{:S(2)}) %collective-permute-start.12) | collective-permute-done | bytes 933920 | tf_op jit(solution)/shard_map/ppermute | solution.py:38
  45.2 2.8 %collective-permute-start.14 = (bf16[64,7296]{1,0:T(8,128)(2,1)S(1)}, bf16[64,7296]{1,0:T(8,128)(2,1)S(1)}, u32[]{:S(2)}, u32[]{:S(2)}) collective-permute-start(bf16[64,7296]{1,0:T(8,128)(2,1)S(1)} %collective-permute-done.12.piece_a), channel_id=1, source_target_pairs={{0,96},{1,97},{2,98},{3,99},{4,100},{5,101},{6,102},{7,103},{8,104... | collective-permute-start | bytes 2801672 | tf_op jit(solution)/shard_map/ppermute | solution.py:38
  47.9 3.5 %collective-permute-done.13.piece_b = bf16[64,7296]{1,0:T(8,128)(2,1)S(1)} collective-permute-done((bf16[64,7296]{1,0:T(8,128)(2,1)S(1)}, bf16[64,7296]{1,0:T(8,128)(2,1)S(1)}, u32[]{:S(2)}, u32[]{:S(2)}) %collective-permute-start.13) | collective-permute-done | bytes 933920 | tf_op jit(solution)/shard_map/ppermute | solution.py:38
  51.4 0.3 collective-permute-start.15
  51.7 2.5 %collective-permute-start.9 = (bf16[64,7296]{1,0:T(8,128)(2,1)S(1)}, bf16[64,7296]{1,0:T(8,128)(2,1)S(1)}, u32[]{:S(2)}, u32[]{:S(2)}) collective-permute-start(bf16[64,7296]{1,0:T(8,128)(2,1)S(1)} %join.4.piece_a), channel_id=1, source_target_pairs={{0,96},{1,97},{2,98},{3,99},{4,100},{5,101},{6,102},{7,103},{8,104... | collective-permute-start | bytes 2801672 | tf_op jit(solution)/shard_map/ppermute | solution.py:38
  54.2 1.4 %collective-permute-start.10 = (bf16[64,7296]{1,0:T(8,128)(2,1)S(1)}, bf16[64,7296]{1,0:T(8,128)(2,1)S(1)}, u32[]{:S(2)}, u32[]{:S(2)}) collective-permute-start(bf16[64,7296]{1,0:T(8,128)(2,1)S(1)} %join.5.piece_b), channel_id=1, source_target_pairs={{0,32},{1,33},{2,34},{3,35},{4,36},{5,37},{6,38},{7,39},{8,40},{9,... | collective-permute-start | bytes 2801672 | tf_op jit(solution)/shard_map/ppermute | solution.py:38
  55.6 2.0 %copy-done.1 = bf16[2,7168,128]{2,1,0:T(8,128)(2,1)S(1)} copy-done((bf16[2,7168,128]{2,1,0:T(8,128)(2,1)S(1)}, bf16[2,7168,128]{2,1,0:T(8,128)(2,1)}, u32[]{:S(2)}) %copy-start.1) | copy-done | bytes 3670040
  57.7 2.0 %copy-done.2 = bf16[2,128,7168]{2,1,0:T(8,128)(2,1)S(1)} copy-done((bf16[2,128,7168]{2,1,0:T(8,128)(2,1)S(1)}, bf16[2,128,7168]{2,1,0:T(8,128)(2,1)}, u32[]{:S(2)}) %copy-start.2) | copy-done | bytes 3670040
  59.7 1.6 %pack.2 = (bf16[7168,512]{1,0:T(8,128)(2,1)S(1)}, bf16[256,7168]{1,0:T(8,128)(2,1)S(1)}) custom-call(bf16[2,7168,128]{2,1,0:T(8,128)(2,1)S(1)} %copy-done, bf16[2,7168,128]{2,1,0:T(8,128)(2,1)S(1)} %copy-done.1, bf16[256,7168]{1,0:T(8,128)(2,1)S(1)} %bitcast.2), custom_call_target="tpu_custom_call" | custom-call | tf_op jit(solution)/shard_map/pack/pallas_call | solution.py:138
  61.3 4.2 %pack.3 = (bf16[7168,512]{1,0:T(8,128)(2,1)S(1)}, bf16[256,7168]{1,0:T(8,128)(2,1)S(1)}) custom-call(bf16[2,7168,128]{2,1,0:T(8,128)(2,1)} %collective-permute-done.6.gate, bf16[2,7168,128]{2,1,0:T(8,128)(2,1)} %collective-permute-done.7.up, bf16[256,7168]{1,0:T(8,128)(2,1)} %bitcast.1.down), custom_call_target="tpu_custom_call" | custom-call | tf_op jit(solution)/shard_map/pack/pallas_call | solution.py:138
  65.6 3.2 %experts.7 = (bf16[64,7168]{1,0:T(8,128)(2,1)S(1)}, bf16[64,7168]{1,0:T(8,128)(2,1)S(1)}) custom-call(bf16[64,7296]{1,0:T(8,128)(2,1)S(1)} %collective-permute-done.14.piece_a, bf16[64,7296]{1,0:T(8,128)(2,1)S(1)} %collective-permute-done.15.piece_b, bf16[128,512]{1,0:T(8,128)(2,1)S(1)} %fusion.spread, bf16[7168,512]{1,0:T(8,128)(2,1)S(1)} %get-tuple-element.21.in_own, ...), custom_call_target="tpu_custom_call" | custom-call | flops 2818572288 | bytes 3670016 | tf_op jit(solution)/shard_map/experts/pallas_call | solution.py:121
  68.8 2.3 %collective-permute-start.16 = (bf16[64,7168]{1,0:T(8,128)(2,1)S(1)}, bf16[64,7168]{1,0:T(8,128)(2,1)S(1)}, u32[]{:S(2)}, u32[]{:S(2)}) collective-permute-start(bf16[64,7168]{1,0:T(8,128)(2,1)S(1)} %get-tuple-element.28), channel_id=1, source_target_pairs={{0,96},{1,97},{2,98},{3,99},{4,100},{5,101},{6,102},{7,103},{8,104... | collective-permute-start | bytes 2752520 | tf_op jit(solution)/shard_map/ppermute | solution.py:38
  71.1 0.4 collective-permute-done.9.piece_a
  71.5 3.6 %collective-permute-done.10.piece_b = bf16[64,7296]{1,0:T(8,128)(2,1)S(1)} collective-permute-done((bf16[64,7296]{1,0:T(8,128)(2,1)S(1)}, bf16[64,7296]{1,0:T(8,128)(2,1)S(1)}, u32[]{:S(2)}, u32[]{:S(2)}) %collective-permute-start.10) | collective-permute-done | bytes 933920 | tf_op jit(solution)/shard_map/ppermute | solution.py:38
  75.0 3.2 %experts.5 = (bf16[64,7168]{1,0:T(8,128)(2,1)S(1)}, bf16[64,7168]{1,0:T(8,128)(2,1)S(1)}) custom-call(bf16[64,7296]{1,0:T(8,128)(2,1)S(1)} %collective-permute-done.9.piece_a, bf16[64,7296]{1,0:T(8,128)(2,1)S(1)} %collective-permute-done.10.piece_b, bf16[128,512]{1,0:T(8,128)(2,1)S(1)} %fusion.spread, bf16[7168,512]{1,0:T(8,128)(2,1)S(1)} %get-tuple-element.21.in_own, ...), custom_call_target="tpu_custom_call" | custom-call | flops 2818572288 | bytes 3670016 | tf_op jit(solution)/shard_map/experts/pallas_call | solution.py:121
  78.2 3.0 %collective-permute-start.11 = (bf16[64,7168]{1,0:T(8,128)(2,1)S(1)}, bf16[64,7168]{1,0:T(8,128)(2,1)S(1)}, u32[]{:S(2)}, u32[]{:S(2)}) collective-permute-start(bf16[64,7168]{1,0:T(8,128)(2,1)S(1)} %get-tuple-element.26), channel_id=1, source_target_pairs={{0,96},{1,97},{2,98},{3,99},{4,100},{5,101},{6,102},{7,103},{8,104... | collective-permute-start | bytes 2752520 | tf_op jit(solution)/shard_map/ppermute | solution.py:38
  81.3 3.2 %experts.6 = (bf16[64,7168]{1,0:T(8,128)(2,1)S(1)}, bf16[64,7168]{1,0:T(8,128)(2,1)S(1)}) custom-call(bf16[64,7296]{1,0:T(8,128)(2,1)S(1)} %collective-permute-done.12.piece_a, bf16[64,7296]{1,0:T(8,128)(2,1)S(1)} %collective-permute-done.13.piece_b, bf16[128,512]{1,0:T(8,128)(2,1)S(1)} %fusion.spread, bf16[7168,512]{1,0:T(8,128)(2,1)S(1)} %get-tuple-element.21.in_own, ...), custom_call_target="tpu_custom_call" | custom-call | flops 2818572288 | bytes 3670016 | tf_op jit(solution)/shard_map/experts/pallas_call | solution.py:121
  84.5 0.1 add.43
  84.6 2.1 %collective-permute-start.18 = (bf16[32,7168]{1,0:T(8,128)(2,1)S(1)}, bf16[32,7168]{1,0:T(8,128)(2,1)S(1)}, u32[]{:S(2)}, u32[]{:S(2)}) collective-permute-start(bf16[32,7168]{1,0:T(8,128)(2,1)S(1)} %add.43), channel_id=1, source_target_pairs={{0,32},{1,33},{2,34},{3,35},{4,36},{5,37},{6,38},{7,39},{8,40},{9,... | collective-permute-start | bytes 1376264 | tf_op jit(solution)/shard_map/ppermute | solution.py:38
  86.7 0.1 add.45
  86.8 1.0 collective-permute-start.22
  87.8 0.1 add.47
  87.9 2.4 %collective-permute-start.24 = (bf16[32,7168]{1,0:T(8,128)(2,1)S(1)}, bf16[32,7168]{1,0:T(8,128)(2,1)S(1)}, u32[]{:S(2)}, u32[]{:S(2)}) collective-permute-start(bf16[32,7168]{1,0:T(8,128)(2,1)S(1)} %add.47), channel_id=1, source_target_pairs={{0,96},{1,97},{2,98},{3,99},{4,100},{5,101},{6,102},{7,103},{8,104... | collective-permute-start | bytes 1376264 | tf_op jit(solution)/shard_map/ppermute | solution.py:38
  90.3 3.2 %experts.4 = (bf16[64,7168]{1,0:T(8,128)(2,1)S(1)}, bf16[64,7168]{1,0:T(8,128)(2,1)S(1)}) custom-call(bf16[64,7296]{1,0:T(8,128)(2,1)S(1)} %join.4.piece_a, bf16[64,7296]{1,0:T(8,128)(2,1)S(1)} %join.5.piece_b, bf16[128,512]{1,0:T(8,128)(2,1)S(1)} %fusion.spread, bf16[7168,512]{1,0:T(8,128)(2,1)S(1)} %get-tuple-element.21.in_own, ...), custom_call_target="tpu_custom_call" | custom-call | flops 2818572288 | bytes 3670016 | tf_op jit(solution)/shard_map/experts/pallas_call | solution.py:121
  93.5 0.1 add.41
  93.6 0.1 collective-permute-start.17
  93.7 5.9 %collective-permute-done.18.refs_2_ = bf16[32,7168]{1,0:T(8,128)(2,1)S(1)} collective-permute-done((bf16[32,7168]{1,0:T(8,128)(2,1)S(1)}, bf16[32,7168]{1,0:T(8,128)(2,1)S(1)}, u32[]{:S(2)}, u32[]{:S(2)}) %collective-permute-start.18) | collective-permute-done | bytes 458784 | tf_op jit(solution)/shard_map/ppermute | solution.py:38
  99.6 0.2 add.44
  99.8 0.1 collective-permute-start.19
  99.9 0.2 add.46
  100.1 1.8 %collective-permute-start.23 = (bf16[32,7168]{1,0:T(8,128)(2,1)S(1)}, bf16[32,7168]{1,0:T(8,128)(2,1)S(1)}, u32[]{:S(2)}, u32[]{:S(2)}) collective-permute-start(bf16[32,7168]{1,0:T(8,128)(2,1)S(1)} %add.46), channel_id=1, source_target_pairs={{0,8},{1,9},{2,10},{3,11},{4,12},{5,13},{6,14},{7,15},{8,0},{9,1},... | collective-permute-start | bytes 1376264 | tf_op jit(solution)/shard_map/ppermute | solution.py:38
  101.9 1.2 collective-permute-done.24.refs_2_
  103.1 0.2 add.48
  103.3 1.8 %collective-permute-start.25 = (bf16[32,7168]{1,0:T(8,128)(2,1)S(1)}, bf16[32,7168]{1,0:T(8,128)(2,1)S(1)}, u32[]{:S(2)}, u32[]{:S(2)}) collective-permute-start(bf16[32,7168]{1,0:T(8,128)(2,1)S(1)} %add.48), channel_id=1, source_target_pairs={{0,12},{1,13},{2,14},{3,15},{4,8},{5,9},{6,10},{7,11},{8,4},{9,5},... | collective-permute-start | bytes 1376264 | tf_op jit(solution)/shard_map/ppermute | solution.py:38
  105.1 0.2 add.42.refs_0_
  105.2 3.1 %collective-permute-done.19.refs_1_ = bf16[32,7168]{1,0:T(8,128)(2,1)S(1)} collective-permute-done((bf16[32,7168]{1,0:T(8,128)(2,1)S(1)}, bf16[32,7168]{1,0:T(8,128)(2,1)S(1)}, u32[]{:S(2)}, u32[]{:S(2)}) %collective-permute-start.19) | collective-permute-done | bytes 458784 | tf_op jit(solution)/shard_map/ppermute | solution.py:38
  108.3 4.8 %collective-permute-done.23.refs_2_ = bf16[32,7168]{1,0:T(8,128)(2,1)S(1)} collective-permute-done((bf16[32,7168]{1,0:T(8,128)(2,1)S(1)}, bf16[32,7168]{1,0:T(8,128)(2,1)S(1)}, u32[]{:S(2)}, u32[]{:S(2)}) %collective-permute-start.23) | collective-permute-done | bytes 458784 | tf_op jit(solution)/shard_map/ppermute | solution.py:38
  113.1 4.8 %collective-permute-done.25.refs_3_ = bf16[32,7168]{1,0:T(8,128)(2,1)S(1)} collective-permute-done((bf16[32,7168]{1,0:T(8,128)(2,1)S(1)}, bf16[32,7168]{1,0:T(8,128)(2,1)S(1)}, u32[]{:S(2)}, u32[]{:S(2)}) %collective-permute-start.25) | collective-permute-done | bytes 458784 | tf_op jit(solution)/shard_map/ppermute | solution.py:38
  118.0 1.7 %collective-permute-start.26 = (bf16[8,7168]{1,0:T(8,128)(2,1)S(1)}, bf16[8,7168]{1,0:T(8,128)(2,1)S(1)}, u32[]{:S(2)}, u32[]{:S(2)}) collective-permute-start(bf16[8,7168]{1,0:T(8,128)(2,1)S(1)} %add.50), channel_id=1, source_target_pairs={{0,1},{1,0},{2,3},{3,2},{4,5},{5,4},{6,7},{7,6},{8,9},{9,8},{10,11... | collective-permute-start | bytes 344072 | tf_op jit(solution)/shard_map/ppermute | solution.py:38
  119.8 2.8 %collective-permute-start.27 = (bf16[8,7168]{1,0:T(8,128)(2,1)S(1)}, bf16[8,7168]{1,0:T(8,128)(2,1)S(1)}, u32[]{:S(2)}, u32[]{:S(2)}) collective-permute-start(bf16[8,7168]{1,0:T(8,128)(2,1)S(1)} %add.51), channel_id=1, source_target_pairs={{0,3},{1,2},{2,1},{3,0},{4,7},{5,6},{6,5},{7,4},{8,11},{9,10},{10,... | collective-permute-start | bytes 344072 | tf_op jit(solution)/shard_map/ppermute | solution.py:38
  122.6 0.7 collective-permute-start.28
  123.3 2.5 %collective-permute-done.27.refs_2_ = bf16[8,7168]{1,0:T(8,128)(2,1)S(1)} collective-permute-done((bf16[8,7168]{1,0:T(8,128)(2,1)S(1)}, bf16[8,7168]{1,0:T(8,128)(2,1)S(1)}, u32[]{:S(2)}, u32[]{:S(2)}) %collective-permute-start.27) | collective-permute-done | bytes 114720 | tf_op jit(solution)/shard_map/ppermute | solution.py:38
  125.8 3.1 %collective-permute-done.28.refs_3_ = bf16[8,7168]{1,0:T(8,128)(2,1)S(1)} collective-permute-done((bf16[8,7168]{1,0:T(8,128)(2,1)S(1)}, bf16[8,7168]{1,0:T(8,128)(2,1)S(1)}, u32[]{:S(2)}, u32[]{:S(2)}) %collective-permute-start.28) | collective-permute-done | bytes 114720 | tf_op jit(solution)/shard_map/ppermute | solution.py:38
  129.0 0.7 add.53
  (29 shorter events, 0.4 us)
Async XLA Ops:
  0.0 51.7 %collective-permute-start.6 = (bf16[2,7168,128]{2,1,0:T(8,128)(2,1)}, bf16[2,7168,128]{2,1,0:T(8,128)(2,1)}, u32[]{:S(2)}, u32[]{:S(2)}) collective-permute-start(bf16[2,7168,128]{2,1,0:T(8,128)(2,1)} %gate.1), channel_id=1, source_target_pairs={{0,16},{1,17},{2,18},{3,19},{4,20},{5,21},{6,22},{7,23},{8,24},{9,... | collective-permute-start | bytes 11010056 | tf_op jit(solution)/shard_map/ppermute | solution.py:42
  0.0 54.2 %collective-permute-start.7 = (bf16[2,7168,128]{2,1,0:T(8,128)(2,1)}, bf16[2,7168,128]{2,1,0:T(8,128)(2,1)}, u32[]{:S(2)}, u32[]{:S(2)}) collective-permute-start(bf16[2,7168,128]{2,1,0:T(8,128)(2,1)} %up.1), channel_id=1, source_target_pairs={{0,16},{1,17},{2,18},{3,19},{4,20},{5,21},{6,22},{7,23},{8,24},{9,... | collective-permute-start | bytes 11010056 | tf_op jit(solution)/shard_map/ppermute | solution.py:42
  0.5 60.8 %collective-permute-start.8 = (bf16[2,128,7168]{2,1,0:T(8,128)(2,1)}, bf16[2,128,7168]{2,1,0:T(8,128)(2,1)}, u32[]{:S(2)}, u32[]{:S(2)}) collective-permute-start(bf16[2,128,7168]{2,1,0:T(8,128)(2,1)} %param.11), channel_id=1, source_target_pairs={{0,16},{1,17},{2,18},{3,19},{4,20},{5,21},{6,22},{7,23},{8,24},{9,... | collective-permute-start | bytes 11010056 | tf_op jit(solution)/shard_map/ppermute | solution.py:42
  2.0 0.9 copy-start.3
  3.1 6.3 %collective-permute-start.2 = (bf16[8,7296]{1,0:T(8,128)(2,1)S(1)}, bf16[8,7296]{1,0:T(8,128)(2,1)S(1)}, u32[]{:S(2)}, u32[]{:S(2)}) collective-permute-start(bf16[8,7296]{1,0:T(8,128)(2,1)S(1)} %route.1.refs_0_), channel_id=1, source_target_pairs={{0,2},{1,3},{2,0},{3,1},{4,6},{5,7},{6,4},{7,5},{8,10},{9,11},{10,... | collective-permute-start | bytes 350216 | tf_op jit(solution)/shard_map/ppermute | solution.py:38
  6.4 6.0 %collective-permute-start.1 = (bf16[8,7296]{1,0:T(8,128)(2,1)S(1)}, bf16[8,7296]{1,0:T(8,128)(2,1)S(1)}, u32[]{:S(2)}, u32[]{:S(2)}) collective-permute-start(bf16[8,7296]{1,0:T(8,128)(2,1)S(1)} %route.1.refs_0_), channel_id=1, source_target_pairs={{0,3},{1,2},{2,1},{3,0},{4,7},{5,6},{6,5},{7,4},{8,11},{9,10},{10,... | collective-permute-start | bytes 350216 | tf_op jit(solution)/shard_map/ppermute | solution.py:38
  7.5 48.2 %copy-start = (bf16[2,7168,128]{2,1,0:T(8,128)(2,1)S(1)}, bf16[2,7168,128]{2,1,0:T(8,128)(2,1)}, u32[]{:S(2)}) copy-start(bf16[2,7168,128]{2,1,0:T(8,128)(2,1)} %gate.1) | copy-start | bytes 11010052
  9.4 4.8 %collective-permute-start = (bf16[8,7296]{1,0:T(8,128)(2,1)S(1)}, bf16[8,7296]{1,0:T(8,128)(2,1)S(1)}, u32[]{:S(2)}, u32[]{:S(2)}) collective-permute-start(bf16[8,7296]{1,0:T(8,128)(2,1)S(1)} %route.1.refs_0_), channel_id=1, source_target_pairs={{0,1},{1,0},{2,3},{3,2},{4,5},{5,4},{6,7},{7,6},{8,9},{9,8},{10,11... | collective-permute-start | bytes 350216 | tf_op jit(solution)/shard_map/ppermute | solution.py:38
  14.3 8.7 %collective-permute-start.3 = (bf16[32,7296]{1,0:T(8,128)(2,1)S(1)}, bf16[32,7296]{1,0:T(8,128)(2,1)S(1)}, u32[]{:S(2)}, u32[]{:S(2)}) collective-permute-start(bf16[32,7296]{1,0:T(8,128)(2,1)S(1)} %join.3.refs_0_), channel_id=1, source_target_pairs={{0,4},{1,5},{2,6},{3,7},{4,0},{5,1},{6,2},{7,3},{8,12},{9,13},{10,... | collective-permute-start | bytes 1400840 | tf_op jit(solution)/shard_map/ppermute | solution.py:38
  16.4 15.2 %collective-permute-start.5 = (bf16[32,7296]{1,0:T(8,128)(2,1)S(1)}, bf16[32,7296]{1,0:T(8,128)(2,1)S(1)}, u32[]{:S(2)}, u32[]{:S(2)}) collective-permute-start(bf16[32,7296]{1,0:T(8,128)(2,1)S(1)} %join.3.refs_0_), channel_id=1, source_target_pairs={{0,8},{1,9},{2,10},{3,11},{4,12},{5,13},{6,14},{7,15},{8,0},{9,1},... | collective-permute-start | bytes 1400840 | tf_op jit(solution)/shard_map/ppermute | solution.py:38
  22.9 13.6 %collective-permute-start.4 = (bf16[32,7296]{1,0:T(8,128)(2,1)S(1)}, bf16[32,7296]{1,0:T(8,128)(2,1)S(1)}, u32[]{:S(2)}, u32[]{:S(2)}) collective-permute-start(bf16[32,7296]{1,0:T(8,128)(2,1)S(1)} %join.3.refs_0_), channel_id=1, source_target_pairs={{0,12},{1,13},{2,14},{3,15},{4,8},{5,9},{6,10},{7,11},{8,4},{9,5},... | collective-permute-start | bytes 1400840 | tf_op jit(solution)/shard_map/ppermute | solution.py:38
  31.6 13.6 %collective-permute-start.12 = (bf16[64,7296]{1,0:T(8,128)(2,1)S(1)}, bf16[64,7296]{1,0:T(8,128)(2,1)S(1)}, u32[]{:S(2)}, u32[]{:S(2)}) collective-permute-start(bf16[64,7296]{1,0:T(8,128)(2,1)S(1)} %join.4.piece_a), channel_id=1, source_target_pairs={{0,32},{1,33},{2,34},{3,35},{4,36},{5,37},{6,38},{7,39},{8,40},{9,... | collective-permute-start | bytes 2801672 | tf_op jit(solution)/shard_map/ppermute | solution.py:38
  36.6 14.9 %collective-permute-start.13 = (bf16[64,7296]{1,0:T(8,128)(2,1)S(1)}, bf16[64,7296]{1,0:T(8,128)(2,1)S(1)}, u32[]{:S(2)}, u32[]{:S(2)}) collective-permute-start(bf16[64,7296]{1,0:T(8,128)(2,1)S(1)} %join.5.piece_b), channel_id=1, source_target_pairs={{0,96},{1,97},{2,98},{3,99},{4,100},{5,101},{6,102},{7,103},{8,104... | collective-permute-start | bytes 2801672 | tf_op jit(solution)/shard_map/ppermute | solution.py:38
  45.2 20.4 %collective-permute-start.14 = (bf16[64,7296]{1,0:T(8,128)(2,1)S(1)}, bf16[64,7296]{1,0:T(8,128)(2,1)S(1)}, u32[]{:S(2)}, u32[]{:S(2)}) collective-permute-start(bf16[64,7296]{1,0:T(8,128)(2,1)S(1)} %collective-permute-done.12.piece_a), channel_id=1, source_target_pairs={{0,96},{1,97},{2,98},{3,99},{4,100},{5,101},{6,102},{7,103},{8,104... | collective-permute-start | bytes 2801672 | tf_op jit(solution)/shard_map/ppermute | solution.py:38
  51.4 14.1 %collective-permute-start.15 = (bf16[64,7296]{1,0:T(8,128)(2,1)S(1)}, bf16[64,7296]{1,0:T(8,128)(2,1)S(1)}, u32[]{:S(2)}, u32[]{:S(2)}) collective-permute-start(bf16[64,7296]{1,0:T(8,128)(2,1)S(1)} %collective-permute-done.13.piece_b), channel_id=1, source_target_pairs={{0,32},{1,33},{2,34},{3,35},{4,36},{5,37},{6,38},{7,39},{8,40},{9,... | collective-permute-start | bytes 2801672 | tf_op jit(solution)/shard_map/ppermute | solution.py:38
  51.7 19.7 %collective-permute-start.9 = (bf16[64,7296]{1,0:T(8,128)(2,1)S(1)}, bf16[64,7296]{1,0:T(8,128)(2,1)S(1)}, u32[]{:S(2)}, u32[]{:S(2)}) collective-permute-start(bf16[64,7296]{1,0:T(8,128)(2,1)S(1)} %join.4.piece_a), channel_id=1, source_target_pairs={{0,96},{1,97},{2,98},{3,99},{4,100},{5,101},{6,102},{7,103},{8,104... | collective-permute-start | bytes 2801672 | tf_op jit(solution)/shard_map/ppermute | solution.py:38
  54.2 20.8 %collective-permute-start.10 = (bf16[64,7296]{1,0:T(8,128)(2,1)S(1)}, bf16[64,7296]{1,0:T(8,128)(2,1)S(1)}, u32[]{:S(2)}, u32[]{:S(2)}) collective-permute-start(bf16[64,7296]{1,0:T(8,128)(2,1)S(1)} %join.5.piece_b), channel_id=1, source_target_pairs={{0,32},{1,33},{2,34},{3,35},{4,36},{5,37},{6,38},{7,39},{8,40},{9,... | collective-permute-start | bytes 2801672 | tf_op jit(solution)/shard_map/ppermute | solution.py:38
  55.6 2.0 %copy-start.1 = (bf16[2,7168,128]{2,1,0:T(8,128)(2,1)S(1)}, bf16[2,7168,128]{2,1,0:T(8,128)(2,1)}, u32[]{:S(2)}) copy-start(bf16[2,7168,128]{2,1,0:T(8,128)(2,1)} %up.1) | copy-start | bytes 11010052
  57.7 2.0 %copy-start.2 = (bf16[2,128,7168]{2,1,0:T(8,128)(2,1)S(1)}, bf16[2,128,7168]{2,1,0:T(8,128)(2,1)}, u32[]{:S(2)}) copy-start(bf16[2,128,7168]{2,1,0:T(8,128)(2,1)} %param.11) | copy-start | bytes 11010052
  68.8 15.7 %collective-permute-start.16 = (bf16[64,7168]{1,0:T(8,128)(2,1)S(1)}, bf16[64,7168]{1,0:T(8,128)(2,1)S(1)}, u32[]{:S(2)}, u32[]{:S(2)}) collective-permute-start(bf16[64,7168]{1,0:T(8,128)(2,1)S(1)} %get-tuple-element.28), channel_id=1, source_target_pairs={{0,96},{1,97},{2,98},{3,99},{4,100},{5,101},{6,102},{7,103},{8,104... | collective-permute-start | bytes 2752520 | tf_op jit(solution)/shard_map/ppermute | solution.py:38
  71.1 15.6 %collective-permute-start.21 = (bf16[64,7168]{1,0:T(8,128)(2,1)S(1)}, bf16[64,7168]{1,0:T(8,128)(2,1)S(1)}, u32[]{:S(2)}, u32[]{:S(2)}) collective-permute-start(bf16[64,7168]{1,0:T(8,128)(2,1)S(1)} %get-tuple-element.32), channel_id=1, source_target_pairs={{0,32},{1,33},{2,34},{3,35},{4,36},{5,37},{6,38},{7,39},{8,40},{9,... | collective-permute-start | bytes 2752520 | tf_op jit(solution)/shard_map/ppermute | solution.py:38
  78.2 15.4 %collective-permute-start.11 = (bf16[64,7168]{1,0:T(8,128)(2,1)S(1)}, bf16[64,7168]{1,0:T(8,128)(2,1)S(1)}, u32[]{:S(2)}, u32[]{:S(2)}) collective-permute-start(bf16[64,7168]{1,0:T(8,128)(2,1)S(1)} %get-tuple-element.26), channel_id=1, source_target_pairs={{0,96},{1,97},{2,98},{3,99},{4,100},{5,101},{6,102},{7,103},{8,104... | collective-permute-start | bytes 2752520 | tf_op jit(solution)/shard_map/ppermute | solution.py:38
  81.3 18.6 %collective-permute-start.20 = (bf16[64,7168]{1,0:T(8,128)(2,1)S(1)}, bf16[64,7168]{1,0:T(8,128)(2,1)S(1)}, u32[]{:S(2)}, u32[]{:S(2)}) collective-permute-start(bf16[64,7168]{1,0:T(8,128)(2,1)S(1)} %get-tuple-element.30), channel_id=1, source_target_pairs={{0,32},{1,33},{2,34},{3,35},{4,36},{5,37},{6,38},{7,39},{8,40},{9,... | collective-permute-start | bytes 2752520 | tf_op jit(solution)/shard_map/ppermute | solution.py:38
  84.6 15.0 %collective-permute-start.18 = (bf16[32,7168]{1,0:T(8,128)(2,1)S(1)}, bf16[32,7168]{1,0:T(8,128)(2,1)S(1)}, u32[]{:S(2)}, u32[]{:S(2)}) collective-permute-start(bf16[32,7168]{1,0:T(8,128)(2,1)S(1)} %add.43), channel_id=1, source_target_pairs={{0,32},{1,33},{2,34},{3,35},{4,36},{5,37},{6,38},{7,39},{8,40},{9,... | collective-permute-start | bytes 1376264 | tf_op jit(solution)/shard_map/ppermute | solution.py:38
  86.8 13.1 %collective-permute-start.22 = (bf16[32,7168]{1,0:T(8,128)(2,1)S(1)}, bf16[32,7168]{1,0:T(8,128)(2,1)S(1)}, u32[]{:S(2)}, u32[]{:S(2)}) collective-permute-start(bf16[32,7168]{1,0:T(8,128)(2,1)S(1)} %add.45), channel_id=1, source_target_pairs={{0,96},{1,97},{2,98},{3,99},{4,100},{5,101},{6,102},{7,103},{8,104... | collective-permute-start | bytes 1376264 | tf_op jit(solution)/shard_map/ppermute | solution.py:38
  87.9 15.2 %collective-permute-start.24 = (bf16[32,7168]{1,0:T(8,128)(2,1)S(1)}, bf16[32,7168]{1,0:T(8,128)(2,1)S(1)}, u32[]{:S(2)}, u32[]{:S(2)}) collective-permute-start(bf16[32,7168]{1,0:T(8,128)(2,1)S(1)} %add.47), channel_id=1, source_target_pairs={{0,96},{1,97},{2,98},{3,99},{4,100},{5,101},{6,102},{7,103},{8,104... | collective-permute-start | bytes 1376264 | tf_op jit(solution)/shard_map/ppermute | solution.py:38
  93.6 11.4 %collective-permute-start.17 = (bf16[32,7168]{1,0:T(8,128)(2,1)S(1)}, bf16[32,7168]{1,0:T(8,128)(2,1)S(1)}, u32[]{:S(2)}, u32[]{:S(2)}) collective-permute-start(bf16[32,7168]{1,0:T(8,128)(2,1)S(1)} %add.41), channel_id=1, source_target_pairs={{0,32},{1,33},{2,34},{3,35},{4,36},{5,37},{6,38},{7,39},{8,40},{9,... | collective-permute-start | bytes 1376264 | tf_op jit(solution)/shard_map/ppermute | solution.py:38
  99.8 8.6 %collective-permute-start.19 = (bf16[32,7168]{1,0:T(8,128)(2,1)S(1)}, bf16[32,7168]{1,0:T(8,128)(2,1)S(1)}, u32[]{:S(2)}, u32[]{:S(2)}) collective-permute-start(bf16[32,7168]{1,0:T(8,128)(2,1)S(1)} %add.44), channel_id=1, source_target_pairs={{0,4},{1,5},{2,6},{3,7},{4,0},{5,1},{6,2},{7,3},{8,12},{9,13},{10,... | collective-permute-start | bytes 1376264 | tf_op jit(solution)/shard_map/ppermute | solution.py:38
  100.1 13.1 %collective-permute-start.23 = (bf16[32,7168]{1,0:T(8,128)(2,1)S(1)}, bf16[32,7168]{1,0:T(8,128)(2,1)S(1)}, u32[]{:S(2)}, u32[]{:S(2)}) collective-permute-start(bf16[32,7168]{1,0:T(8,128)(2,1)S(1)} %add.46), channel_id=1, source_target_pairs={{0,8},{1,9},{2,10},{3,11},{4,12},{5,13},{6,14},{7,15},{8,0},{9,1},... | collective-permute-start | bytes 1376264 | tf_op jit(solution)/shard_map/ppermute | solution.py:38
  103.3 14.6 %collective-permute-start.25 = (bf16[32,7168]{1,0:T(8,128)(2,1)S(1)}, bf16[32,7168]{1,0:T(8,128)(2,1)S(1)}, u32[]{:S(2)}, u32[]{:S(2)}) collective-permute-start(bf16[32,7168]{1,0:T(8,128)(2,1)S(1)} %add.48), channel_id=1, source_target_pairs={{0,12},{1,13},{2,14},{3,15},{4,8},{5,9},{6,10},{7,11},{8,4},{9,5},... | collective-permute-start | bytes 1376264 | tf_op jit(solution)/shard_map/ppermute | solution.py:38
  118.0 5.3 %collective-permute-start.26 = (bf16[8,7168]{1,0:T(8,128)(2,1)S(1)}, bf16[8,7168]{1,0:T(8,128)(2,1)S(1)}, u32[]{:S(2)}, u32[]{:S(2)}) collective-permute-start(bf16[8,7168]{1,0:T(8,128)(2,1)S(1)} %add.50), channel_id=1, source_target_pairs={{0,1},{1,0},{2,3},{3,2},{4,5},{5,4},{6,7},{7,6},{8,9},{9,8},{10,11... | collective-permute-start | bytes 344072 | tf_op jit(solution)/shard_map/ppermute | solution.py:38
  119.8 6.1 %collective-permute-start.27 = (bf16[8,7168]{1,0:T(8,128)(2,1)S(1)}, bf16[8,7168]{1,0:T(8,128)(2,1)S(1)}, u32[]{:S(2)}, u32[]{:S(2)}) collective-permute-start(bf16[8,7168]{1,0:T(8,128)(2,1)S(1)} %add.51), channel_id=1, source_target_pairs={{0,3},{1,2},{2,1},{3,0},{4,7},{5,6},{6,5},{7,4},{8,11},{9,10},{10,... | collective-permute-start | bytes 344072 | tf_op jit(solution)/shard_map/ppermute | solution.py:38
  122.6 6.4 %collective-permute-start.28 = (bf16[8,7168]{1,0:T(8,128)(2,1)S(1)}, bf16[8,7168]{1,0:T(8,128)(2,1)S(1)}, u32[]{:S(2)}, u32[]{:S(2)}) collective-permute-start(bf16[8,7168]{1,0:T(8,128)(2,1)S(1)} %add.52), channel_id=1, source_target_pairs={{0,2},{1,3},{2,0},{3,1},{4,6},{5,7},{6,4},{7,5},{8,10},{9,11},{10,... | collective-permute-start | bytes 344072 | tf_op jit(solution)/shard_map/ppermute | solution.py:38

commit v4 on v3

--- a/solution.py
+++ b/solution.py
@@ -91,10 +91,12 @@
         copy.wait()
 
 
-def expert_kernel(piece_a, piece_b, spread, in_own, in_other, down_own, down_other, out_a, out_b, rows):
-    half, width = out_a.shape
-    rows[:half, :] = piece_a[...]
-    rows[half:, :] = piece_b[...]
+def expert_kernel(count, *refs):
+    pieces, (spread, in_own, in_other, down_own, down_other) = refs[:count], refs[count : count + 5]
+    outs, rows = refs[count + 5 : -1], refs[-1]
+    half, width = outs[0].shape
+    for k, piece in enumerate(pieces):
+        rows[k * half : (k + 1) * half, :] = piece[...]
     weight = jnp.dot(rows[:, width:], spread[...], preferred_element_type=jnp.float32)
     hidden = []
     for k, w_in in enumerate((in_own, in_other)):
@@ -108,28 +110,29 @@
         cols = slice(j * step, (j + 1) * step)
         part = jnp.dot(hidden[0], down_own[:, cols], preferred_element_type=jnp.float32)
         part = part + jnp.dot(hidden[1], down_other[:, cols], preferred_element_type=jnp.float32)
-        part = part.astype(out_a.dtype)
-        out_a[:, cols] = part[:half]
-        out_b[:, cols] = part[half:]
-
-
-def experts_of(piece_a, piece_b, weights):
-    half, packed = piece_a.shape
+        part = part.astype(rows.dtype)
+        for k, out in enumerate(outs):
+            out[:, cols] = part[k * half : (k + 1) * half]
+
+
+def experts_of(pieces, weights):
+    count = len(pieces)
+    half, packed = pieces[0].shape
     width = packed - 128
-    kind = piece_a.dtype
+    kind = pieces[0].dtype
     shape = jax.ShapeDtypeStruct((half, width), kind)
     return pl.pallas_call(
-        expert_kernel,
-        out_shape=(shape, shape),
-        in_specs=[VMEM] * 7,
-        out_specs=(VMEM,) * 2,
-        scratch_shapes=[pltpu.VMEM((2 * half, packed), kind)],
+        functools.partial(expert_kernel, count),
+        out_shape=(shape,) * count,
+        in_specs=[VMEM] * (count + 5),
+        out_specs=(VMEM,) * count,
+        scratch_shapes=[pltpu.VMEM((count * half, packed), kind)],
         compiler_params=pltpu.CompilerParams(vmem_limit_bytes=12 << 20),
         cost_estimate=pl.CostEstimate(
             flops=4 * half * width * 1536, bytes_accessed=half * width * 8, transcendentals=half * 1024
         ),
         name="experts",
-    )(piece_a, piece_b, *weights)
+    )(*pieces, *weights)
 
 
 def pack(gate, up, down):
@@ -204,10 +207,11 @@
     oa, ob = send(am, 2, 3), send(bp, 2, 1)
     bm, ap = send(b0, 2, 1), send(a0, 2, 3)
 
-    sa0, sb0 = experts_of(a0, b0, weights)
-    sam, sbp = experts_of(am, bp, weights)
-    soa, sob = experts_of(oa, ob, weights)
-    sap, sbm = experts_of(ap, bm, weights)
+    sa0, sb0 = experts_of((a0, b0), weights)
+    sam, sbp = experts_of((am, bp), weights)
+    (soa,) = experts_of((oa,), weights)
+    (sob,) = experts_of((ob,), weights)
+    sap, sbm = experts_of((ap, bm), weights)
 
     over_a = send(soa, 2, 3)
     over_b = send(sob, 2, 1)

time: 130 us -> 132 us (1.015)
  Pallas kernels: 21 us -> 25.9 us
  waiting for transfers between devices: 54.5 us -> 51.8 us
    pallas_call x4 -> x5, Pallas kernels: 12.8 us -> 17.7 us  [experts_of(): pl.pallas_call(functools.partial(expert_kernel, count), out_shape=(shape,...]
    ppermute x26, waiting for transfers between devices: 54.5 us -> 51.8 us  [send(): return lax.ppermute(value, AXES, pairs(phase, shift))]
  transfers between devices with their start and end apart: 29 -> 29, of which waited for: 17 -> 16; matrix products, arithmetic and copies ran while one was open for 1% -> 1% of each run, Pallas kernels for 16% -> 19%
where the time goes in v4:
time: 132 us
  waiting for transfers between devices  51.8 us (39%)
  starting transfers between devices  47.8 us (36%)
  Pallas kernels  25.9 us (20%)
  local copies, waits for them, and re-layouts  4.98 us (4%)
  other arithmetic  1.48 us (1%)
    ppermute x26, waiting for transfers between devices, send(): return lax.ppermute(value, AXES, pairs(phase, shift))  51.8 us
    ppermute x26, starting transfers between devices, send(): return lax.ppermute(value, AXES, pairs(phase, shift))  47.2 us
    pallas_call x5, Pallas kernels, experts_of(): pl.pallas_call(functools.partial(expert_kernel, count), out_shape=(shape,...  17.7 us
    pallas_call x2, Pallas kernels, pack(): pl.pallas_call(pack_kernel, out_shape=(jax.ShapeDtypeStruct((width, 2 * p...  5.8 us
    unnamed x8, local copies, waits for them, and re-layouts  4.98 us
  transfers between devices with their start and end apart: 29, of which 16 were waited for; matrix products, arithmetic and copies ran while one was open for 1% of the time, Pallas kernels for 19%

profile of v4, /device:TPU:0, one launch (start us, length us, event | category | flops | bytes accessed | tf_op | source)
XLA Modules:
  0.0 132.2 jit_solution(5266445454555117070)
XLA Ops:
  0.0 0.5 collective-permute-start.7
  0.5 0.7 convert_element_type.6
  1.2 0.8 pad_maximum_fusion.routing
  2.0 0.9 copy-done.3
  2.9 0.2 route.1.refs_0_
  3.1 3.3 %collective-permute-start.2 = (bf16[8,7296]{1,0:T(8,128)(2,1)S(1)}, bf16[8,7296]{1,0:T(8,128)(2,1)S(1)}, u32[]{:S(2)}, u32[]{:S(2)}) collective-permute-start(bf16[8,7296]{1,0:T(8,128)(2,1)S(1)} %route.1.refs_0_), channel_id=1, source_target_pairs={{0,2},{1,3},{2,0},{3,1},{4,6},{5,7},{6,4},{7,5},{8,10},{9,11},{10,... | collective-permute-start | bytes 350216 | tf_op jit(solution)/shard_map/ppermute | solution.py:38
  6.4 1.1 collective-permute-start.1
  7.5 1.9 %collective-permute-done.2.refs_3_ = bf16[8,7296]{1,0:T(8,128)(2,1)S(1)} collective-permute-done((bf16[8,7296]{1,0:T(8,128)(2,1)S(1)}, bf16[8,7296]{1,0:T(8,128)(2,1)S(1)}, u32[]{:S(2)}, u32[]{:S(2)}) %collective-permute-start.2) | collective-permute-done | bytes 116768 | tf_op jit(solution)/shard_map/ppermute | solution.py:38
  9.4 1.7 %collective-permute-start = (bf16[8,7296]{1,0:T(8,128)(2,1)S(1)}, bf16[8,7296]{1,0:T(8,128)(2,1)S(1)}, u32[]{:S(2)}, u32[]{:S(2)}) collective-permute-start(bf16[8,7296]{1,0:T(8,128)(2,1)S(1)} %route.1.refs_0_), channel_id=1, source_target_pairs={{0,1},{1,0},{2,3},{3,2},{4,5},{5,4},{6,7},{7,6},{8,9},{9,8},{10,11... | collective-permute-start | bytes 350216 | tf_op jit(solution)/shard_map/ppermute | solution.py:38
  11.2 1.2 collective-permute-done.1.refs_2_
  12.4 1.8 %collective-permute-done.refs_1_ = bf16[8,7296]{1,0:T(8,128)(2,1)S(1)} collective-permute-done((bf16[8,7296]{1,0:T(8,128)(2,1)S(1)}, bf16[8,7296]{1,0:T(8,128)(2,1)S(1)}, u32[]{:S(2)}, u32[]{:S(2)}) %collective-permute-start) | collective-permute-done | bytes 116768 | tf_op jit(solution)/shard_map/ppermute | solution.py:38
  14.3 2.1 %collective-permute-start.3 = (bf16[32,7296]{1,0:T(8,128)(2,1)S(1)}, bf16[32,7296]{1,0:T(8,128)(2,1)S(1)}, u32[]{:S(2)}, u32[]{:S(2)}) collective-permute-start(bf16[32,7296]{1,0:T(8,128)(2,1)S(1)} %join.3.refs_0_), channel_id=1, source_target_pairs={{0,4},{1,5},{2,6},{3,7},{4,0},{5,1},{6,2},{7,3},{8,12},{9,13},{10,... | collective-permute-start | bytes 1400840 | tf_op jit(solution)/shard_map/ppermute | solution.py:38
  16.4 3.6 %collective-permute-start.5 = (bf16[32,7296]{1,0:T(8,128)(2,1)S(1)}, bf16[32,7296]{1,0:T(8,128)(2,1)S(1)}, u32[]{:S(2)}, u32[]{:S(2)}) collective-permute-start(bf16[32,7296]{1,0:T(8,128)(2,1)S(1)} %join.3.refs_0_), channel_id=1, source_target_pairs={{0,8},{1,9},{2,10},{3,11},{4,12},{5,13},{6,14},{7,15},{8,0},{9,1},... | collective-permute-start | bytes 1400840 | tf_op jit(solution)/shard_map/ppermute | solution.py:38
  20.0 3.0 %collective-permute-done.3.refs_1_ = bf16[32,7296]{1,0:T(8,128)(2,1)S(1)} collective-permute-done((bf16[32,7296]{1,0:T(8,128)(2,1)S(1)}, bf16[32,7296]{1,0:T(8,128)(2,1)S(1)}, u32[]{:S(2)}, u32[]{:S(2)}) %collective-permute-start.3) | collective-permute-done | bytes 466976 | tf_op jit(solution)/shard_map/ppermute | solution.py:38
  22.9 4.1 %collective-permute-start.4 = (bf16[32,7296]{1,0:T(8,128)(2,1)S(1)}, bf16[32,7296]{1,0:T(8,128)(2,1)S(1)}, u32[]{:S(2)}, u32[]{:S(2)}) collective-permute-start(bf16[32,7296]{1,0:T(8,128)(2,1)S(1)} %join.3.refs_0_), channel_id=1, source_target_pairs={{0,12},{1,13},{2,14},{3,15},{4,8},{5,9},{6,10},{7,11},{8,4},{9,5},... | collective-permute-start | bytes 1400840 | tf_op jit(solution)/shard_map/ppermute | solution.py:38
  27.1 4.5 %collective-permute-done.5.refs_1_ = bf16[32,7296]{1,0:T(8,128)(2,1)S(1)} collective-permute-done((bf16[32,7296]{1,0:T(8,128)(2,1)S(1)}, bf16[32,7296]{1,0:T(8,128)(2,1)S(1)}, u32[]{:S(2)}, u32[]{:S(2)}) %collective-permute-start.5) | collective-permute-done | bytes 466976 | tf_op jit(solution)/shard_map/ppermute | solution.py:38
  31.6 1.5 %collective-permute-start.12 = (bf16[64,7296]{1,0:T(8,128)(2,1)S(1)}, bf16[64,7296]{1,0:T(8,128)(2,1)S(1)}, u32[]{:S(2)}, u32[]{:S(2)}) collective-permute-start(bf16[64,7296]{1,0:T(8,128)(2,1)S(1)} %join.4.refs_0_), channel_id=1, source_target_pairs={{0,32},{1,33},{2,34},{3,35},{4,36},{5,37},{6,38},{7,39},{8,40},{9,... | collective-permute-start | bytes 2801672 | tf_op jit(solution)/shard_map/ppermute | solution.py:38
  33.1 3.4 %collective-permute-done.4.refs_0_ = bf16[32,7296]{1,0:T(8,128)(2,1)S(1)} collective-permute-done((bf16[32,7296]{1,0:T(8,128)(2,1)S(1)}, bf16[32,7296]{1,0:T(8,128)(2,1)S(1)}, u32[]{:S(2)}, u32[]{:S(2)}) %collective-permute-start.4) | collective-permute-done | bytes 466976 | tf_op jit(solution)/shard_map/ppermute | solution.py:38
  36.6 2.8 %collective-permute-start.13 = (bf16[64,7296]{1,0:T(8,128)(2,1)S(1)}, bf16[64,7296]{1,0:T(8,128)(2,1)S(1)}, u32[]{:S(2)}, u32[]{:S(2)}) collective-permute-start(bf16[64,7296]{1,0:T(8,128)(2,1)S(1)} %join.5.refs_1_), channel_id=1, source_target_pairs={{0,96},{1,97},{2,98},{3,99},{4,100},{5,101},{6,102},{7,103},{8,104... | collective-permute-start | bytes 2801672 | tf_op jit(solution)/shard_map/ppermute | solution.py:38
  39.4 5.8 %collective-permute-done.12.refs_0_ = bf16[64,7296]{1,0:T(8,128)(2,1)S(1)} collective-permute-done((bf16[64,7296]{1,0:T(8,128)(2,1)S(1)}, bf16[64,7296]{1,0:T(8,128)(2,1)S(1)}, u32[]{:S(2)}, u32[]{:S(2)}) %collective-permute-start.12) | collective-permute-done | bytes 933920 | tf_op jit(solution)/shard_map/ppermute | solution.py:38
  45.2 2.8 %collective-permute-start.14 = (bf16[64,7296]{1,0:T(8,128)(2,1)S(1)}, bf16[64,7296]{1,0:T(8,128)(2,1)S(1)}, u32[]{:S(2)}, u32[]{:S(2)}) collective-permute-start(bf16[64,7296]{1,0:T(8,128)(2,1)S(1)} %collective-permute-done.12.refs_0_), channel_id=1, source_target_pairs={{0,96},{1,97},{2,98},{3,99},{4,100},{5,101},{6,102},{7,103},{8,104... | collective-permute-start | bytes 2801672 | tf_op jit(solution)/shard_map/ppermute | solution.py:38
  47.9 3.5 %collective-permute-done.13.refs_1_ = bf16[64,7296]{1,0:T(8,128)(2,1)S(1)} collective-permute-done((bf16[64,7296]{1,0:T(8,128)(2,1)S(1)}, bf16[64,7296]{1,0:T(8,128)(2,1)S(1)}, u32[]{:S(2)}, u32[]{:S(2)}) %collective-permute-start.13) | collective-permute-done | bytes 933920 | tf_op jit(solution)/shard_map/ppermute | solution.py:38
  51.4 0.3 collective-permute-start.20
  51.7 2.5 %collective-permute-start.9 = (bf16[64,7296]{1,0:T(8,128)(2,1)S(1)}, bf16[64,7296]{1,0:T(8,128)(2,1)S(1)}, u32[]{:S(2)}, u32[]{:S(2)}) collective-permute-start(bf16[64,7296]{1,0:T(8,128)(2,1)S(1)} %join.4.refs_0_), channel_id=1, source_target_pairs={{0,96},{1,97},{2,98},{3,99},{4,100},{5,101},{6,102},{7,103},{8,104... | collective-permute-start | bytes 2801672 | tf_op jit(solution)/shard_map/ppermute | solution.py:38
  54.2 1.4 %collective-permute-start.10 = (bf16[64,7296]{1,0:T(8,128)(2,1)S(1)}, bf16[64,7296]{1,0:T(8,128)(2,1)S(1)}, u32[]{:S(2)}, u32[]{:S(2)}) collective-permute-start(bf16[64,7296]{1,0:T(8,128)(2,1)S(1)} %join.5.refs_1_), channel_id=1, source_target_pairs={{0,32},{1,33},{2,34},{3,35},{4,36},{5,37},{6,38},{7,39},{8,40},{9,... | collective-permute-start | bytes 2801672 | tf_op jit(solution)/shard_map/ppermute | solution.py:38
  55.6 2.0 %copy-done.1 = bf16[2,7168,128]{2,1,0:T(8,128)(2,1)S(1)} copy-done((bf16[2,7168,128]{2,1,0:T(8,128)(2,1)S(1)}, bf16[2,7168,128]{2,1,0:T(8,128)(2,1)}, u32[]{:S(2)}) %copy-start.1) | copy-done | bytes 3670040
  57.7 2.0 %copy-done.2 = bf16[2,128,7168]{2,1,0:T(8,128)(2,1)S(1)} copy-done((bf16[2,128,7168]{2,1,0:T(8,128)(2,1)S(1)}, bf16[2,128,7168]{2,1,0:T(8,128)(2,1)}, u32[]{:S(2)}) %copy-start.2) | copy-done | bytes 3670040
  59.7 1.6 %pack.2 = (bf16[7168,512]{1,0:T(8,128)(2,1)S(1)}, bf16[256,7168]{1,0:T(8,128)(2,1)S(1)}) custom-call(bf16[2,7168,128]{2,1,0:T(8,128)(2,1)S(1)} %copy-done, bf16[2,7168,128]{2,1,0:T(8,128)(2,1)S(1)} %copy-done.1, bf16[256,7168]{1,0:T(8,128)(2,1)S(1)} %bitcast.2), custom_call_target="tpu_custom_call" | custom-call | tf_op jit(solution)/shard_map/pack/pallas_call | solution.py:141
  61.3 4.2 %pack.3 = (bf16[7168,512]{1,0:T(8,128)(2,1)S(1)}, bf16[256,7168]{1,0:T(8,128)(2,1)S(1)}) custom-call(bf16[2,7168,128]{2,1,0:T(8,128)(2,1)} %collective-permute-done.6.gate, bf16[2,7168,128]{2,1,0:T(8,128)(2,1)} %collective-permute-done.7.up, bf16[256,7168]{1,0:T(8,128)(2,1)} %bitcast.1.down), custom_call_target="tpu_custom_call" | custom-call | tf_op jit(solution)/shard_map/pack/pallas_call | solution.py:141
  65.6 4.0 %experts.8 = bf16[64,7168]{1,0:T(8,128)(2,1)S(1)} custom-call(bf16[64,7296]{1,0:T(8,128)(2,1)S(1)} %collective-permute-done.14.refs_0_, bf16[128,512]{1,0:T(8,128)(2,1)S(1)} %fusion.refs_2_.refs_1_, bf16[7168,512]{1,0:T(8,128)(2,1)S(1)} %get-tuple-element.19.refs_3_.refs_2_, bf16[7168,512]{1,0:T(8,128)(2,1)S(1)} %get-tuple-element.20.refs_4_.refs_3_, ...), custom_call_target="tpu_custom_call" | custom-call | flops 2818572288 | bytes 3670016 | tf_op jit(solution)/shard_map/experts/pallas_call | solution.py:124
  69.6 0.8 collective-permute-start.15
  70.4 4.0 %experts.9 = bf16[64,7168]{1,0:T(8,128)(2,1)S(1)} custom-call(bf16[64,7296]{1,0:T(8,128)(2,1)S(1)} %collective-permute-done.20.refs_0_, bf16[128,512]{1,0:T(8,128)(2,1)S(1)} %fusion.refs_2_.refs_1_, bf16[7168,512]{1,0:T(8,128)(2,1)S(1)} %get-tuple-element.19.refs_3_.refs_2_, bf16[7168,512]{1,0:T(8,128)(2,1)S(1)} %get-tuple-element.20.refs_4_.refs_3_, ...), custom_call_target="tpu_custom_call" | custom-call | flops 2818572288 | bytes 3670016 | tf_op jit(solution)/shard_map/experts/pallas_call | solution.py:124
  74.4 0.3 collective-permute-start.21
  74.8 0.3 collective-permute-done.10.refs_1_
  75.0 3.2 %experts.6 = (bf16[64,7168]{1,0:T(8,128)(2,1)S(1)}, bf16[64,7168]{1,0:T(8,128)(2,1)S(1)}) custom-call(bf16[64,7296]{1,0:T(8,128)(2,1)S(1)} %collective-permute-done.9.refs_0_, bf16[64,7296]{1,0:T(8,128)(2,1)S(1)} %collective-permute-done.10.refs_1_, bf16[128,512]{1,0:T(8,128)(2,1)S(1)} %fusion.refs_2_.refs_1_, ...), custom_call_target="tpu_custom_call" | custom-call | flops 2818572288 | bytes 3670016 | tf_op jit(solution)/shard_map/experts/pallas_call | solution.py:124
  78.2 2.8 %collective-permute-start.11 = (bf16[64,7168]{1,0:T(8,128)(2,1)S(1)}, bf16[64,7168]{1,0:T(8,128)(2,1)S(1)}, u32[]{:S(2)}, u32[]{:S(2)}) collective-permute-start(bf16[64,7168]{1,0:T(8,128)(2,1)S(1)} %get-tuple-element.24), channel_id=1, source_target_pairs={{0,96},{1,97},{2,98},{3,99},{4,100},{5,101},{6,102},{7,103},{8,104... | collective-permute-start | bytes 2752520 | tf_op jit(solution)/shard_map/ppermute | solution.py:38
  81.1 0.9 collective-permute-start.19
  82.0 3.2 %experts.7 = (bf16[64,7168]{1,0:T(8,128)(2,1)S(1)}, bf16[64,7168]{1,0:T(8,128)(2,1)S(1)}) custom-call(bf16[64,7296]{1,0:T(8,128)(2,1)S(1)} %collective-permute-done.12.refs_0_, bf16[64,7296]{1,0:T(8,128)(2,1)S(1)} %collective-permute-done.13.refs_1_, bf16[128,512]{1,0:T(8,128)(2,1)S(1)} %fusion.refs_2_.refs_1_, ...), custom_call_target="tpu_custom_call" | custom-call | flops 2818572288 | bytes 3670016 | tf_op jit(solution)/shard_map/experts/pallas_call | solution.py:124
  85.2 0.1 add.43
  85.3 1.2 collective-permute-start.17
  86.5 1.6 %collective-permute-done.21.refs_1_ = bf16[64,7168]{1,0:T(8,128)(2,1)S(1)} collective-permute-done((bf16[64,7168]{1,0:T(8,128)(2,1)S(1)}, bf16[64,7168]{1,0:T(8,128)(2,1)S(1)}, u32[]{:S(2)}, u32[]{:S(2)}) %collective-permute-start.21) | collective-permute-done | bytes 917536 | tf_op jit(solution)/shard_map/ppermute | solution.py:38
  88.1 0.1 add.45
  88.2 2.6 %collective-permute-start.22 = (bf16[32,7168]{1,0:T(8,128)(2,1)S(1)}, bf16[32,7168]{1,0:T(8,128)(2,1)S(1)}, u32[]{:S(2)}, u32[]{:S(2)}) collective-permute-start(bf16[32,7168]{1,0:T(8,128)(2,1)S(1)} %add.45), channel_id=1, source_target_pairs={{0,96},{1,97},{2,98},{3,99},{4,100},{5,101},{6,102},{7,103},{8,104... | collective-permute-start | bytes 1376264 | tf_op jit(solution)/shard_map/ppermute | solution.py:38
  90.8 0.1 add.47
  90.9 0.8 collective-permute-start.24
  91.7 3.2 %experts.5 = (bf16[64,7168]{1,0:T(8,128)(2,1)S(1)}, bf16[64,7168]{1,0:T(8,128)(2,1)S(1)}) custom-call(bf16[64,7296]{1,0:T(8,128)(2,1)S(1)} %join.4.refs_0_, bf16[64,7296]{1,0:T(8,128)(2,1)S(1)} %join.5.refs_1_, bf16[128,512]{1,0:T(8,128)(2,1)S(1)} %fusion.refs_2_.refs_1_, bf16[7168,512]{1,0:T(8,128)(2,1)S(1)} %get-tuple-element.19.refs_3_.refs_2_, ...), custom_call_target="tpu_custom_call" | custom-call | flops 2818572288 | bytes 3670016 | tf_op jit(solution)/shard_map/experts/pallas_call | solution.py:124
  94.9 0.1 add.41
  95.1 7.7 %collective-permute-done.17.refs_2_ = bf16[32,7168]{1,0:T(8,128)(2,1)S(1)} collective-permute-done((bf16[32,7168]{1,0:T(8,128)(2,1)S(1)}, bf16[32,7168]{1,0:T(8,128)(2,1)S(1)}, u32[]{:S(2)}, u32[]{:S(2)}) %collective-permute-start.17) | collective-permute-done | bytes 458784 | tf_op jit(solution)/shard_map/ppermute | solution.py:38
  102.8 0.2 add.44
  103.0 0.1 collective-permute-start.18
  103.1 0.2 add.46
  103.3 1.8 %collective-permute-start.23 = (bf16[32,7168]{1,0:T(8,128)(2,1)S(1)}, bf16[32,7168]{1,0:T(8,128)(2,1)S(1)}, u32[]{:S(2)}, u32[]{:S(2)}) collective-permute-start(bf16[32,7168]{1,0:T(8,128)(2,1)S(1)} %add.46), channel_id=1, source_target_pairs={{0,8},{1,9},{2,10},{3,11},{4,12},{5,13},{6,14},{7,15},{8,0},{9,1},... | collective-permute-start | bytes 1376264 | tf_op jit(solution)/shard_map/ppermute | solution.py:38
  105.1 0.2 add.48
  105.3 3.0 %collective-permute-start.25 = (bf16[32,7168]{1,0:T(8,128)(2,1)S(1)}, bf16[32,7168]{1,0:T(8,128)(2,1)S(1)}, u32[]{:S(2)}, u32[]{:S(2)}) collective-permute-start(bf16[32,7168]{1,0:T(8,128)(2,1)S(1)} %add.48), channel_id=1, source_target_pairs={{0,12},{1,13},{2,14},{3,15},{4,8},{5,9},{6,10},{7,11},{8,4},{9,5},... | collective-permute-start | bytes 1376264 | tf_op jit(solution)/shard_map/ppermute | solution.py:38
  108.3 0.2 add.42.refs_0_
  108.5 3.1 %collective-permute-done.18.refs_1_ = bf16[32,7168]{1,0:T(8,128)(2,1)S(1)} collective-permute-done((bf16[32,7168]{1,0:T(8,128)(2,1)S(1)}, bf16[32,7168]{1,0:T(8,128)(2,1)S(1)}, u32[]{:S(2)}, u32[]{:S(2)}) %collective-permute-start.18) | collective-permute-done | bytes 458784 | tf_op jit(solution)/shard_map/ppermute | solution.py:38
  111.6 4.8 %collective-permute-done.23.refs_2_ = bf16[32,7168]{1,0:T(8,128)(2,1)S(1)} collective-permute-done((bf16[32,7168]{1,0:T(8,128)(2,1)S(1)}, bf16[32,7168]{1,0:T(8,128)(2,1)S(1)}, u32[]{:S(2)}, u32[]{:S(2)}) %collective-permute-start.23) | collective-permute-done | bytes 458784 | tf_op jit(solution)/shard_map/ppermute | solution.py:38
  116.3 3.6 %collective-permute-done.25.refs_3_ = bf16[32,7168]{1,0:T(8,128)(2,1)S(1)} collective-permute-done((bf16[32,7168]{1,0:T(8,128)(2,1)S(1)}, bf16[32,7168]{1,0:T(8,128)(2,1)S(1)}, u32[]{:S(2)}, u32[]{:S(2)}) %collective-permute-start.25) | collective-permute-done | bytes 458784 | tf_op jit(solution)/shard_map/ppermute | solution.py:38
  120.0 1.7 %collective-permute-start.26 = (bf16[8,7168]{1,0:T(8,128)(2,1)S(1)}, bf16[8,7168]{1,0:T(8,128)(2,1)S(1)}, u32[]{:S(2)}, u32[]{:S(2)}) collective-permute-start(bf16[8,7168]{1,0:T(8,128)(2,1)S(1)} %add.50), channel_id=1, source_target_pairs={{0,1},{1,0},{2,3},{3,2},{4,5},{5,4},{6,7},{7,6},{8,9},{9,8},{10,11... | collective-permute-start | bytes 344072 | tf_op jit(solution)/shard_map/ppermute | solution.py:38
  121.8 3.2 %collective-permute-start.27 = (bf16[8,7168]{1,0:T(8,128)(2,1)S(1)}, bf16[8,7168]{1,0:T(8,128)(2,1)S(1)}, u32[]{:S(2)}, u32[]{:S(2)}) collective-permute-start(bf16[8,7168]{1,0:T(8,128)(2,1)S(1)} %add.51), channel_id=1, source_target_pairs={{0,3},{1,2},{2,1},{3,0},{4,7},{5,6},{6,5},{7,4},{8,11},{9,10},{10,... | collective-permute-start | bytes 344072 | tf_op jit(solution)/shard_map/ppermute | solution.py:38
  125.1 0.7 collective-permute-start.28
  125.9 2.8 %collective-permute-done.27.refs_2_ = bf16[8,7168]{1,0:T(8,128)(2,1)S(1)} collective-permute-done((bf16[8,7168]{1,0:T(8,128)(2,1)S(1)}, bf16[8,7168]{1,0:T(8,128)(2,1)S(1)}, u32[]{:S(2)}, u32[]{:S(2)}) %collective-permute-start.27) | collective-permute-done | bytes 114720 | tf_op jit(solution)/shard_map/ppermute | solution.py:38
  128.6 2.9 %collective-permute-done.28.refs_3_ = bf16[8,7168]{1,0:T(8,128)(2,1)S(1)} collective-permute-done((bf16[8,7168]{1,0:T(8,128)(2,1)S(1)}, bf16[8,7168]{1,0:T(8,128)(2,1)S(1)}, u32[]{:S(2)}, u32[]{:S(2)}) %collective-permute-start.28) | collective-permute-done | bytes 114720 | tf_op jit(solution)/shard_map/ppermute | solution.py:38
  131.5 0.7 add.53
  (30 shorter events, 0.6 us)
Async XLA Ops:
  0.0 51.7 %collective-permute-start.6 = (bf16[2,7168,128]{2,1,0:T(8,128)(2,1)}, bf16[2,7168,128]{2,1,0:T(8,128)(2,1)}, u32[]{:S(2)}, u32[]{:S(2)}) collective-permute-start(bf16[2,7168,128]{2,1,0:T(8,128)(2,1)} %gate.1), channel_id=1, source_target_pairs={{0,16},{1,17},{2,18},{3,19},{4,20},{5,21},{6,22},{7,23},{8,24},{9,... | collective-permute-start | bytes 11010056 | tf_op jit(solution)/shard_map/ppermute | solution.py:42
  0.0 54.2 %collective-permute-start.7 = (bf16[2,7168,128]{2,1,0:T(8,128)(2,1)}, bf16[2,7168,128]{2,1,0:T(8,128)(2,1)}, u32[]{:S(2)}, u32[]{:S(2)}) collective-permute-start(bf16[2,7168,128]{2,1,0:T(8,128)(2,1)} %up.1), channel_id=1, source_target_pairs={{0,16},{1,17},{2,18},{3,19},{4,20},{5,21},{6,22},{7,23},{8,24},{9,... | collective-permute-start | bytes 11010056 | tf_op jit(solution)/shard_map/ppermute | solution.py:42
  0.5 60.8 %collective-permute-start.8 = (bf16[2,128,7168]{2,1,0:T(8,128)(2,1)}, bf16[2,128,7168]{2,1,0:T(8,128)(2,1)}, u32[]{:S(2)}, u32[]{:S(2)}) collective-permute-start(bf16[2,128,7168]{2,1,0:T(8,128)(2,1)} %param.11), channel_id=1, source_target_pairs={{0,16},{1,17},{2,18},{3,19},{4,20},{5,21},{6,22},{7,23},{8,24},{9,... | collective-permute-start | bytes 11010056 | tf_op jit(solution)/shard_map/ppermute | solution.py:42
  2.0 0.9 copy-start.3
  3.1 6.3 %collective-permute-start.2 = (bf16[8,7296]{1,0:T(8,128)(2,1)S(1)}, bf16[8,7296]{1,0:T(8,128)(2,1)S(1)}, u32[]{:S(2)}, u32[]{:S(2)}) collective-permute-start(bf16[8,7296]{1,0:T(8,128)(2,1)S(1)} %route.1.refs_0_), channel_id=1, source_target_pairs={{0,2},{1,3},{2,0},{3,1},{4,6},{5,7},{6,4},{7,5},{8,10},{9,11},{10,... | collective-permute-start | bytes 350216 | tf_op jit(solution)/shard_map/ppermute | solution.py:38
  6.4 6.0 %collective-permute-start.1 = (bf16[8,7296]{1,0:T(8,128)(2,1)S(1)}, bf16[8,7296]{1,0:T(8,128)(2,1)S(1)}, u32[]{:S(2)}, u32[]{:S(2)}) collective-permute-start(bf16[8,7296]{1,0:T(8,128)(2,1)S(1)} %route.1.refs_0_), channel_id=1, source_target_pairs={{0,3},{1,2},{2,1},{3,0},{4,7},{5,6},{6,5},{7,4},{8,11},{9,10},{10,... | collective-permute-start | bytes 350216 | tf_op jit(solution)/shard_map/ppermute | solution.py:38
  7.5 48.2 %copy-start = (bf16[2,7168,128]{2,1,0:T(8,128)(2,1)S(1)}, bf16[2,7168,128]{2,1,0:T(8,128)(2,1)}, u32[]{:S(2)}) copy-start(bf16[2,7168,128]{2,1,0:T(8,128)(2,1)} %gate.1) | copy-start | bytes 11010052
  9.4 4.8 %collective-permute-start = (bf16[8,7296]{1,0:T(8,128)(2,1)S(1)}, bf16[8,7296]{1,0:T(8,128)(2,1)S(1)}, u32[]{:S(2)}, u32[]{:S(2)}) collective-permute-start(bf16[8,7296]{1,0:T(8,128)(2,1)S(1)} %route.1.refs_0_), channel_id=1, source_target_pairs={{0,1},{1,0},{2,3},{3,2},{4,5},{5,4},{6,7},{7,6},{8,9},{9,8},{10,11... | collective-permute-start | bytes 350216 | tf_op jit(solution)/shard_map/ppermute | solution.py:38
  14.3 8.7 %collective-permute-start.3 = (bf16[32,7296]{1,0:T(8,128)(2,1)S(1)}, bf16[32,7296]{1,0:T(8,128)(2,1)S(1)}, u32[]{:S(2)}, u32[]{:S(2)}) collective-permute-start(bf16[32,7296]{1,0:T(8,128)(2,1)S(1)} %join.3.refs_0_), channel_id=1, source_target_pairs={{0,4},{1,5},{2,6},{3,7},{4,0},{5,1},{6,2},{7,3},{8,12},{9,13},{10,... | collective-permute-start | bytes 1400840 | tf_op jit(solution)/shard_map/ppermute | solution.py:38
  16.4 15.2 %collective-permute-start.5 = (bf16[32,7296]{1,0:T(8,128)(2,1)S(1)}, bf16[32,7296]{1,0:T(8,128)(2,1)S(1)}, u32[]{:S(2)}, u32[]{:S(2)}) collective-permute-start(bf16[32,7296]{1,0:T(8,128)(2,1)S(1)} %join.3.refs_0_), channel_id=1, source_target_pairs={{0,8},{1,9},{2,10},{3,11},{4,12},{5,13},{6,14},{7,15},{8,0},{9,1},... | collective-permute-start | bytes 1400840 | tf_op jit(solution)/shard_map/ppermute | solution.py:38
  22.9 13.6 %collective-permute-start.4 = (bf16[32,7296]{1,0:T(8,128)(2,1)S(1)}, bf16[32,7296]{1,0:T(8,128)(2,1)S(1)}, u32[]{:S(2)}, u32[]{:S(2)}) collective-permute-start(bf16[32,7296]{1,0:T(8,128)(2,1)S(1)} %join.3.refs_0_), channel_id=1, source_target_pairs={{0,12},{1,13},{2,14},{3,15},{4,8},{5,9},{6,10},{7,11},{8,4},{9,5},... | collective-permute-start | bytes 1400840 | tf_op jit(solution)/shard_map/ppermute | solution.py:38
  31.6 13.6 %collective-permute-start.12 = (bf16[64,7296]{1,0:T(8,128)(2,1)S(1)}, bf16[64,7296]{1,0:T(8,128)(2,1)S(1)}, u32[]{:S(2)}, u32[]{:S(2)}) collective-permute-start(bf16[64,7296]{1,0:T(8,128)(2,1)S(1)} %join.4.refs_0_), channel_id=1, source_target_pairs={{0,32},{1,33},{2,34},{3,35},{4,36},{5,37},{6,38},{7,39},{8,40},{9,... | collective-permute-start | bytes 2801672 | tf_op jit(solution)/shard_map/ppermute | solution.py:38
  36.6 14.9 %collective-permute-start.13 = (bf16[64,7296]{1,0:T(8,128)(2,1)S(1)}, bf16[64,7296]{1,0:T(8,128)(2,1)S(1)}, u32[]{:S(2)}, u32[]{:S(2)}) collective-permute-start(bf16[64,7296]{1,0:T(8,128)(2,1)S(1)} %join.5.refs_1_), channel_id=1, source_target_pairs={{0,96},{1,97},{2,98},{3,99},{4,100},{5,101},{6,102},{7,103},{8,104... | collective-permute-start | bytes 2801672 | tf_op jit(solution)/shard_map/ppermute | solution.py:38
  45.2 20.4 %collective-permute-start.14 = (bf16[64,7296]{1,0:T(8,128)(2,1)S(1)}, bf16[64,7296]{1,0:T(8,128)(2,1)S(1)}, u32[]{:S(2)}, u32[]{:S(2)}) collective-permute-start(bf16[64,7296]{1,0:T(8,128)(2,1)S(1)} %collective-permute-done.12.refs_0_), channel_id=1, source_target_pairs={{0,96},{1,97},{2,98},{3,99},{4,100},{5,101},{6,102},{7,103},{8,104... | collective-permute-start | bytes 2801672 | tf_op jit(solution)/shard_map/ppermute | solution.py:38
  51.4 18.9 %collective-permute-start.20 = (bf16[64,7296]{1,0:T(8,128)(2,1)S(1)}, bf16[64,7296]{1,0:T(8,128)(2,1)S(1)}, u32[]{:S(2)}, u32[]{:S(2)}) collective-permute-start(bf16[64,7296]{1,0:T(8,128)(2,1)S(1)} %collective-permute-done.13.refs_1_), channel_id=1, source_target_pairs={{0,32},{1,33},{2,34},{3,35},{4,36},{5,37},{6,38},{7,39},{8,40},{9,... | collective-permute-start | bytes 2801672 | tf_op jit(solution)/shard_map/ppermute | solution.py:38
  51.7 23.0 %collective-permute-start.9 = (bf16[64,7296]{1,0:T(8,128)(2,1)S(1)}, bf16[64,7296]{1,0:T(8,128)(2,1)S(1)}, u32[]{:S(2)}, u32[]{:S(2)}) collective-permute-start(bf16[64,7296]{1,0:T(8,128)(2,1)S(1)} %join.4.refs_0_), channel_id=1, source_target_pairs={{0,96},{1,97},{2,98},{3,99},{4,100},{5,101},{6,102},{7,103},{8,104... | collective-permute-start | bytes 2801672 | tf_op jit(solution)/shard_map/ppermute | solution.py:38
  54.2 20.8 %collective-permute-start.10 = (bf16[64,7296]{1,0:T(8,128)(2,1)S(1)}, bf16[64,7296]{1,0:T(8,128)(2,1)S(1)}, u32[]{:S(2)}, u32[]{:S(2)}) collective-permute-start(bf16[64,7296]{1,0:T(8,128)(2,1)S(1)} %join.5.refs_1_), channel_id=1, source_target_pairs={{0,32},{1,33},{2,34},{3,35},{4,36},{5,37},{6,38},{7,39},{8,40},{9,... | collective-permute-start | bytes 2801672 | tf_op jit(solution)/shard_map/ppermute | solution.py:38
  55.6 2.0 %copy-start.1 = (bf16[2,7168,128]{2,1,0:T(8,128)(2,1)S(1)}, bf16[2,7168,128]{2,1,0:T(8,128)(2,1)}, u32[]{:S(2)}) copy-start(bf16[2,7168,128]{2,1,0:T(8,128)(2,1)} %up.1) | copy-start | bytes 11010052
  57.7 2.0 %copy-start.2 = (bf16[2,128,7168]{2,1,0:T(8,128)(2,1)S(1)}, bf16[2,128,7168]{2,1,0:T(8,128)(2,1)}, u32[]{:S(2)}) copy-start(bf16[2,128,7168]{2,1,0:T(8,128)(2,1)} %param.11) | copy-start | bytes 11010052
  69.6 15.6 %collective-permute-start.15 = (bf16[64,7168]{1,0:T(8,128)(2,1)S(1)}, bf16[64,7168]{1,0:T(8,128)(2,1)S(1)}, u32[]{:S(2)}, u32[]{:S(2)}) collective-permute-start(bf16[64,7168]{1,0:T(8,128)(2,1)S(1)} %experts.8), channel_id=1, source_target_pairs={{0,96},{1,97},{2,98},{3,99},{4,100},{5,101},{6,102},{7,103},{8,104... | collective-permute-start | bytes 2752520 | tf_op jit(solution)/shard_map/ppermute | solution.py:38
  74.4 13.7 %collective-permute-start.21 = (bf16[64,7168]{1,0:T(8,128)(2,1)S(1)}, bf16[64,7168]{1,0:T(8,128)(2,1)S(1)}, u32[]{:S(2)}, u32[]{:S(2)}) collective-permute-start(bf16[64,7168]{1,0:T(8,128)(2,1)S(1)} %experts.9), channel_id=1, source_target_pairs={{0,32},{1,33},{2,34},{3,35},{4,36},{5,37},{6,38},{7,39},{8,40},{9,... | collective-permute-start | bytes 2752520 | tf_op jit(solution)/shard_map/ppermute | solution.py:38
  78.2 16.8 %collective-permute-start.11 = (bf16[64,7168]{1,0:T(8,128)(2,1)S(1)}, bf16[64,7168]{1,0:T(8,128)(2,1)S(1)}, u32[]{:S(2)}, u32[]{:S(2)}) collective-permute-start(bf16[64,7168]{1,0:T(8,128)(2,1)S(1)} %get-tuple-element.24), channel_id=1, source_target_pairs={{0,96},{1,97},{2,98},{3,99},{4,100},{5,101},{6,102},{7,103},{8,104... | collective-permute-start | bytes 2752520 | tf_op jit(solution)/shard_map/ppermute | solution.py:38
  81.1 22.0 %collective-permute-start.19 = (bf16[64,7168]{1,0:T(8,128)(2,1)S(1)}, bf16[64,7168]{1,0:T(8,128)(2,1)S(1)}, u32[]{:S(2)}, u32[]{:S(2)}) collective-permute-start(bf16[64,7168]{1,0:T(8,128)(2,1)S(1)} %get-tuple-element.27), channel_id=1, source_target_pairs={{0,32},{1,33},{2,34},{3,35},{4,36},{5,37},{6,38},{7,39},{8,40},{9,... | collective-permute-start | bytes 2752520 | tf_op jit(solution)/shard_map/ppermute | solution.py:38
  85.3 17.5 %collective-permute-start.17 = (bf16[32,7168]{1,0:T(8,128)(2,1)S(1)}, bf16[32,7168]{1,0:T(8,128)(2,1)S(1)}, u32[]{:S(2)}, u32[]{:S(2)}) collective-permute-start(bf16[32,7168]{1,0:T(8,128)(2,1)S(1)} %add.43), channel_id=1, source_target_pairs={{0,32},{1,33},{2,34},{3,35},{4,36},{5,37},{6,38},{7,39},{8,40},{9,... | collective-permute-start | bytes 1376264 | tf_op jit(solution)/shard_map/ppermute | solution.py:38
  88.2 14.9 %collective-permute-start.22 = (bf16[32,7168]{1,0:T(8,128)(2,1)S(1)}, bf16[32,7168]{1,0:T(8,128)(2,1)S(1)}, u32[]{:S(2)}, u32[]{:S(2)}) collective-permute-start(bf16[32,7168]{1,0:T(8,128)(2,1)S(1)} %add.45), channel_id=1, source_target_pairs={{0,96},{1,97},{2,98},{3,99},{4,100},{5,101},{6,102},{7,103},{8,104... | collective-permute-start | bytes 1376264 | tf_op jit(solution)/shard_map/ppermute | solution.py:38
  90.9 14.2 %collective-permute-start.24 = (bf16[32,7168]{1,0:T(8,128)(2,1)S(1)}, bf16[32,7168]{1,0:T(8,128)(2,1)S(1)}, u32[]{:S(2)}, u32[]{:S(2)}) collective-permute-start(bf16[32,7168]{1,0:T(8,128)(2,1)S(1)} %add.47), channel_id=1, source_target_pairs={{0,96},{1,97},{2,98},{3,99},{4,100},{5,101},{6,102},{7,103},{8,104... | collective-permute-start | bytes 1376264 | tf_op jit(solution)/shard_map/ppermute | solution.py:38
  95.0 13.3 %collective-permute-start.16 = (bf16[32,7168]{1,0:T(8,128)(2,1)S(1)}, bf16[32,7168]{1,0:T(8,128)(2,1)S(1)}, u32[]{:S(2)}, u32[]{:S(2)}) collective-permute-start(bf16[32,7168]{1,0:T(8,128)(2,1)S(1)} %add.41), channel_id=1, source_target_pairs={{0,32},{1,33},{2,34},{3,35},{4,36},{5,37},{6,38},{7,39},{8,40},{9,... | collective-permute-start | bytes 1376264 | tf_op jit(solution)/shard_map/ppermute | solution.py:38
  103.0 8.6 %collective-permute-start.18 = (bf16[32,7168]{1,0:T(8,128)(2,1)S(1)}, bf16[32,7168]{1,0:T(8,128)(2,1)S(1)}, u32[]{:S(2)}, u32[]{:S(2)}) collective-permute-start(bf16[32,7168]{1,0:T(8,128)(2,1)S(1)} %add.44), channel_id=1, source_target_pairs={{0,4},{1,5},{2,6},{3,7},{4,0},{5,1},{6,2},{7,3},{8,12},{9,13},{10,... | collective-permute-start | bytes 1376264 | tf_op jit(solution)/shard_map/ppermute | solution.py:38
  103.3 13.1 %collective-permute-start.23 = (bf16[32,7168]{1,0:T(8,128)(2,1)S(1)}, bf16[32,7168]{1,0:T(8,128)(2,1)S(1)}, u32[]{:S(2)}, u32[]{:S(2)}) collective-permute-start(bf16[32,7168]{1,0:T(8,128)(2,1)S(1)} %add.46), channel_id=1, source_target_pairs={{0,8},{1,9},{2,10},{3,11},{4,12},{5,13},{6,14},{7,15},{8,0},{9,1},... | collective-permute-start | bytes 1376264 | tf_op jit(solution)/shard_map/ppermute | solution.py:38
  105.3 14.7 %collective-permute-start.25 = (bf16[32,7168]{1,0:T(8,128)(2,1)S(1)}, bf16[32,7168]{1,0:T(8,128)(2,1)S(1)}, u32[]{:S(2)}, u32[]{:S(2)}) collective-permute-start(bf16[32,7168]{1,0:T(8,128)(2,1)S(1)} %add.48), channel_id=1, source_target_pairs={{0,12},{1,13},{2,14},{3,15},{4,8},{5,9},{6,10},{7,11},{8,4},{9,5},... | collective-permute-start | bytes 1376264 | tf_op jit(solution)/shard_map/ppermute | solution.py:38
  120.0 5.8 %collective-permute-start.26 = (bf16[8,7168]{1,0:T(8,128)(2,1)S(1)}, bf16[8,7168]{1,0:T(8,128)(2,1)S(1)}, u32[]{:S(2)}, u32[]{:S(2)}) collective-permute-start(bf16[8,7168]{1,0:T(8,128)(2,1)S(1)} %add.50), channel_id=1, source_target_pairs={{0,1},{1,0},{2,3},{3,2},{4,5},{5,4},{6,7},{7,6},{8,9},{9,8},{10,11... | collective-permute-start | bytes 344072 | tf_op jit(solution)/shard_map/ppermute | solution.py:38
  121.8 6.8 %collective-permute-start.27 = (bf16[8,7168]{1,0:T(8,128)(2,1)S(1)}, bf16[8,7168]{1,0:T(8,128)(2,1)S(1)}, u32[]{:S(2)}, u32[]{:S(2)}) collective-permute-start(bf16[8,7168]{1,0:T(8,128)(2,1)S(1)} %add.51), channel_id=1, source_target_pairs={{0,3},{1,2},{2,1},{3,0},{4,7},{5,6},{6,5},{7,4},{8,11},{9,10},{10,... | collective-permute-start | bytes 344072 | tf_op jit(solution)/shard_map/ppermute | solution.py:38
  125.1 6.4 %collective-permute-start.28 = (bf16[8,7168]{1,0:T(8,128)(2,1)S(1)}, bf16[8,7168]{1,0:T(8,128)(2,1)S(1)}, u32[]{:S(2)}, u32[]{:S(2)}) collective-permute-start(bf16[8,7168]{1,0:T(8,128)(2,1)S(1)} %add.52), channel_id=1, source_target_pairs={{0,2},{1,3},{2,0},{3,1},{4,6},{5,7},{6,4},{7,5},{8,10},{9,11},{10,... | collective-permute-start | bytes 344072 | tf_op jit(solution)/shard_map/ppermute | solution.py:38
